TPU v7x, 256 devices: a 2x2x32 block of a 4x8x32 slice. The times are simulated.
256 devices in a mesh: groups: 4 (over y, x), blk: 32 (over z), sub: 2 (over core).
Axes of the slice: x: 2, y: 2, z: 32, core: 2. Of those that a mesh axis runs over, the one named last changes fastest.
The devices are a block of a 4x8x32 slice.
Arguments:
- embeddings: bfloat16 [49152, 1024], P(('groups', 'blk', 'sub')), parts along dimension 0, may hold values from -6 to 6
- member_key: int32 [49152], P(('groups', 'blk', 'sub')), parts along dimension 0, may hold values from 0 to 1073741823, as said below
- limit_index: int32 [4], P('groups'), parts along dimension 0, may hold values from 0 to 7
Outputs:
- max_cosine: float32 [49152], P(('groups', 'blk', 'sub')), parts along dimension 0
- kept_share: float32 [4], P('groups'), parts along dimension 0
There are 4 independent parts, one for each index of `groups`. A program takes and returns all parts, laid end to end along the dimension named above; each array names one. Nothing has to cross between parts.
Inputs may be any that keep to these rules, and one draw needn't show every extreme that they name: `member_key`: all keys of a cluster are distinct. A key's quotient by 268435456 is the member's sub-cluster, 0 to 3; its remainder orders the members.
All inputs are finite; a program needn't handle non-finite values.
Results may differ from a plain program's by a relative error of at most 0.0013.
Values may be sent and summed in bfloat16 or wider, within the bound.
No kernel may reach another device: no remote copies, remote signals or barrier semaphores. Data moves between devices by JAX's collectives and lax.ppermute only.
A program may use at most 64 MiB of HBM per device.

v0:
```python
import functools
import math

import jax
import jax.numpy as jnp
from jax import lax
from jax.experimental import pallas as pl
from jax.experimental.pallas import tpu as pltpu
from jax.sharding import PartitionSpec as P


LIMITS = 8
label_stride = 268435456
KEY_BASE = 32768
PIECES = 3


VMEM = pl.BlockSpec(memory_space=pltpu.VMEM)
PARAMS = pltpu.CompilerParams(vmem_limit_bytes=16 * 1024 * 1024)


def normalize_kernel(emb_ref, *out_refs):
    at = 0
    for out in out_refs:
        values = emb_ref[at : at + out.shape[0], :].astype(jnp.float32)
        mean_square = jnp.mean(values * values, axis=1, keepdims=True)
        scaled = values * lax.rsqrt(mean_square + 1e-06) * (1.0 / math.sqrt(values.shape[1]))
        out[...] = scaled.astype(jnp.bfloat16)
        at += out.shape[0]


def normalize(embeddings, sizes):
    rows, width = embeddings.shape
    return pl.pallas_call(
        normalize_kernel,
        out_shape=[jax.ShapeDtypeStruct((size, width), jnp.bfloat16) for size in sizes],
        in_specs=[VMEM],
        out_specs=[VMEM] * len(sizes),
        compiler_params=PARAMS,
        cost_estimate=pl.CostEstimate(
            flops=rows * width * 4, bytes_accessed=rows * width * 4, transcendentals=rows
        ),
        name="normalize",
    )(embeddings)


def whole_key(note):
    return note[0:1].astype(jnp.int32) * KEY_BASE + note[1:2].astype(jnp.int32)


def key_columns(note):
    keys = whole_key(note)
    return jnp.broadcast_to(keys, (128, keys.shape[1])).T


def best_of(best, row_key, low, rows, others, key_col):
    scores = lax.dot_general(
        others, rows, (((1,), (1,)), ((), ())), preferred_element_type=jnp.float32
    )
    count = rows.shape[0]
    key = jnp.concatenate([key_col] * (-(-count // 128)), axis=1)[:, :count]
    allowed = (key < row_key) & (key >= low)
    masked = jnp.where(allowed, scores, jnp.float32(-1.0))
    return jnp.maximum(best, jnp.max(masked, axis=0, keepdims=True))


def lay_kernel(count, starts, *refs):
    first = 0
    for ref in refs[:count]:
        end = first + ref.shape[0]
        for start, out in zip(starts, refs[count:]):
            low, high = max(first, start), min(end, start + out.shape[0])
            if low < high:
                out[low - start : high - start, :] = ref[low - first : high - first, :]
        first = end


def lay(pieces, cuts):
    width = pieces[0].shape[1]
    total = sum(end - start for start, end in cuts)
    return pl.pallas_call(
        functools.partial(lay_kernel, len(pieces), [start for start, _ in cuts]),
        out_shape=[jax.ShapeDtypeStruct((end - start, width), jnp.bfloat16) for start, end in cuts],
        in_specs=[VMEM] * len(pieces),
        out_specs=[VMEM] * len(cuts),
        compiler_params=PARAMS,
        cost_estimate=pl.CostEstimate(
            flops=total, bytes_accessed=4 * total * width, transcendentals=0
        ),
        name="lay",
    )(*pieces)


def visit_kernel(at_home, note_ref, whole_ref, own_note_ref, own_ref, own_columns_ref, *refs):
    best_ref, columns_ref = refs[-2:]
    note = note_ref[...]
    columns_ref[...] = key_columns(note)
    if at_home:
        key, rows_ref, others_ref, others_columns_ref = whole_key(own_note_ref[...]), own_ref, whole_ref, columns_ref
    else:
        key, rows_ref, others_ref, others_columns_ref = whole_key(note), whole_ref, own_ref, own_columns_ref
    low = key & jnp.int32(-label_stride)
    rows = rows_ref[...]
    step = rows.shape[0] // 2

    def part(n, best):
        at = pl.ds(pl.multiple_of(n * step, step), step)
        return best_of(best, key, low, rows, others_ref[at, :], others_columns_ref[at, :])

    start = refs[0][...] if len(refs) > 2 else jnp.full(best_ref.shape, -1.0, jnp.float32)
    best_ref[...] = lax.fori_loop(0, 2, part, start)


def visit(note, whole, own, acc=None):
    rows, width = whole.shape
    own_note, own_whole, own_columns = own
    operands = [note, whole, own_note, own_whole, own_columns]
    operands += [] if acc is None else [acc]
    return pl.pallas_call(
        functools.partial(visit_kernel, acc is not None),
        out_shape=[
            jax.ShapeDtypeStruct((1, rows), jnp.float32),
            jax.ShapeDtypeStruct((rows, 128), jnp.int32),
        ],
        in_specs=[VMEM] * len(operands),
        out_specs=[VMEM] * 2,
        compiler_params=PARAMS,
        cost_estimate=pl.CostEstimate(
            flops=rows, bytes_accessed=6 * rows * width, transcendentals=0
        ),
        name="visit",
    )(*operands)


def columns_kernel(note_ref, columns_ref):
    columns_ref[...] = key_columns(note_ref[...])


def columns_of(note):
    return pl.pallas_call(
        columns_kernel,
        out_shape=jax.ShapeDtypeStruct((note.shape[1], 128), jnp.int32),
        in_specs=[VMEM],
        out_specs=VMEM,
        compiler_params=PARAMS,
        name="columns",
    )(note)


def meet_kernel(first_row, pieces, blocks, extra, spread, *refs):
    note_ref = refs[0]
    rows = jnp.concatenate([r[...] for r in refs[1 : 1 + pieces]], axis=0)
    at = 1 + pieces
    count = rows.shape[0]
    row_key = whole_key(note_ref[...])[:, first_row : first_row + count]
    low = row_key & jnp.int32(-label_stride)
    best = jnp.full((1, count), -1.0, jnp.float32)
    for _ in range(blocks):
        best = best_of(best, row_key, low, rows, refs[at][...], refs[at + 1][...])
        at += 2
    if extra:
        others = jnp.concatenate([r[...] for r in refs[at + 1 : at + 1 + extra]], axis=0)
        best = best_of(best, row_key, low, rows, others, key_columns(refs[at][...]))
        at += 1 + extra
    out_ref = refs[-1]
    if spread:
        earlier = jnp.maximum(refs[at][...], refs[at + 1][...])
        best = jnp.concatenate([earlier, best], axis=1)
        for ref in refs[at + 2 : -1]:
            best = jnp.maximum(best, ref[...])
        out_ref[...] = jnp.broadcast_to(best[:, None, :], out_ref.shape)
    else:
        out_ref[...] = best


def meet(note, first_row, pieces, blocks, extra=(), spread=(), chips=0):
    count, width = sum(p.shape[0] for p in pieces), pieces[0].shape[1]
    operands = [note, *pieces]
    for whole, columns in blocks:
        operands += [whole, columns]
    operands += [*extra, *spread]
    others = sum(whole.shape[0] for whole, _ in blocks) + sum(p.shape[0] for p in extra[1:])
    out = (chips, 1, note.shape[1]) if spread else (1, count)
    return pl.pallas_call(
        functools.partial(
            meet_kernel, first_row, len(pieces), len(blocks), max(len(extra) - 1, 0), bool(spread)
        ),
        out_shape=jax.ShapeDtypeStruct(out, jnp.float32),
        in_specs=[VMEM] * len(operands),
        out_specs=VMEM,
        compiler_params=PARAMS,
        cost_estimate=pl.CostEstimate(
            flops=2 * count * others * width,
            bytes_accessed=2 * (count + others) * width,
            transcendentals=0,
        ),
        name="meet",
    )(*operands)


def finish_kernel(width, place_ref, limit_ref, mine_ref, theirs_ref, best_ref, share_ref):
    blocks, rows = mine_ref.shape
    half = rows // 2
    core, blk = place_ref[0], place_ref[1]
    k = limit_ref[0]
    limit = jnp.float32(0.0)
    for entry in range(LIMITS):
        limit = jnp.where(k == entry, jnp.float32((2.0 + 0.5 * entry) / width), limit)
    quarter = blocks // 4

    def turned(x, by):
        return jnp.concatenate([x[by:], x[:by]], axis=0)

    mine, theirs = mine_ref[...], theirs_ref[...]
    mine = jnp.concatenate([mine[:, half:], mine[:, :half]], axis=1)
    up, down = quarter, blocks - quarter
    best = jnp.where(
        core == 0,
        jnp.maximum(turned(mine, down), turned(theirs, up)),
        jnp.maximum(turned(mine, up), turned(theirs, down)),
    )
    kept = jax.nn.sigmoid(2.0 * width * (limit - best))
    total = jnp.sum(jnp.sum(kept, axis=0, keepdims=True), axis=1, keepdims=True)
    share_ref[...] = total / (blocks * rows)
    at = lax.broadcasted_iota(jnp.int32, best.shape, 0)
    own = jnp.max(jnp.where(at == blk, best, jnp.float32(-2.0)), axis=0, keepdims=True)
    best_ref[...] = own[:, :half]


def finish(place, limit_index, mine, theirs, width):
    _, rows = mine.shape
    smem = pl.BlockSpec(memory_space=pltpu.SMEM)
    return pl.pallas_call(
        functools.partial(finish_kernel, width),
        out_shape=[
            jax.ShapeDtypeStruct((1, rows // 2), jnp.float32),
            jax.ShapeDtypeStruct((1, 1), jnp.float32),
        ],
        in_specs=[smem, smem, VMEM, VMEM],
        out_specs=[VMEM, VMEM],
        compiler_params=PARAMS,
        name="finish",
    )(place, limit_index, mine, theirs)


def program(embeddings, member_key, limit_index):
    chips, cores = lax.axis_size("blk"), lax.axis_size("sub")
    rows, width = embeddings.shape
    hops = chips // 4

    def moves(by, change):
        pairs = []
        for c in range(chips):
            for core, to in ((0, (c + by) % chips), (1, (c - by) % chips)):
                pairs.append((cores * c + core, cores * to + (1 - core if change else core)))
        return pairs

    def send(x, by, change=False):
        return lax.ppermute(x, ("blk", "sub"), moves(by, change))

    def across(x):
        return lax.ppermute(x, "sub", [(0, 1), (1, 0)])

    size = cores * rows // PIECES
    cuts = [(n * size, (n + 1) * size) for n in range(PIECES)]
    everything = (0, cores * rows)
    own_key = jnp.stack(
        [(member_key // KEY_BASE).astype(jnp.float32), (member_key % KEY_BASE).astype(jnp.float32)]
    )
    mine = normalize(embeddings, (size, rows - size))
    theirs = [across(m) for m in mine]
    note = jnp.concatenate([own_key, across(own_key)], axis=1)
    *rest, whole = lay([*mine, *theirs], [*cuts[1:], everything])
    block = [mine[0], *rest]
    notes = [note]
    while len(notes) < hops:
        by = len(notes)
        far = send(jnp.concatenate(notes, axis=0), by)
        notes += [far[2 * n : 2 * n + 2] for n in range(by)]
    last_note = send(note, hops, True)
    own = (note, whole, columns_of(note))
    held = [own[1:]]
    start = jnp.full((1, cores * rows), -1.0, jnp.float32)
    acc, _ = visit(note, whole, own, start)
    for h in range(1, hops):
        block = [send(b, 1) for b in block]
        (whole,) = lay(block, [everything])
        if h < hops - 1:
            acc, columns = visit(notes[h], whole, own, acc)
        else:
            late, columns = visit(notes[h], whole, own)
        held.append((whole, columns))
    acc = send(acc, hops, True)
    late = send(late, 1, True)
    block = [send(b, 1, True) for b in block]
    (first,) = lay(block[:-1], [(0, rows)])
    facing = [across(last_note[:, :rows]), across(first)]
    split = size * (PIECES - 1)
    early = [meet(last_note, 0, block[:-1], held), meet(last_note, 0, block[:-1], [], facing)]
    everyone = meet(last_note, split, block[-1:], held, facing, (*early, acc, late), chips)

    gathered = lax.all_to_all(everyone, "blk", 0, 0, tiled=True).reshape(chips, -1)
    other_side = across(gathered)
    place = jnp.stack([lax.axis_index("sub"), lax.axis_index("blk")]).astype(jnp.int32)
    best, share = finish(place, limit_index, gathered, other_side, math.sqrt(width))
    return (best.reshape(-1), share.reshape(1))


def solution(mesh):
    in_specs = (P(("groups", "blk", "sub"), None), P(("groups", "blk", "sub")), P("groups"))
    out_specs = (P(("groups", "blk", "sub")), P("groups"))
    return jax.shard_map(
        program, mesh=mesh, in_specs=in_specs, out_specs=out_specs, check_vma=False
    )
```

profile of v0, /device:TPU:37, one launch (start us, length us, event | category | flops | bytes accessed | tf_op | source)
XLA Modules:
  0.0 175.7 jit_solution(16658494960515152362)
XLA Ops:
  0.6 1.0 copy-done
  1.6 0.2 normalize.1
  1.8 20.5 %collective-permute-start.2 = (bf16[128,1024]{1,0:T(8,128)(2,1)S(1)}, bf16[128,1024]{1,0:T(8,128)(2,1)S(1)}, u32[]{:S(2)}, u32[]{:S(2)}) collective-permute-start(bf16[128,1024]{1,0:T(8,128)(2,1)S(1)} %get-tuple-element.24.refs_0_), channel_id=1, source_target_pairs={{0,1},{1,0},{2,3},{3,2},{4,5},{5,4},{6,7},{7,6},{8,9},{9,8},{10,11... | collective-permute-start | bytes 786440 | tf_op jit(solution)/shard_map/ppermute | solution.py:262
  22.3 0.1 collective-permute-start.3
  22.5 3.8 %collective-permute-start.12 = (bf16[128,1024]{1,0:T(8,128)(2,1)S(1)}, bf16[128,1024]{1,0:T(8,128)(2,1)S(1)}, u32[]{:S(2)}, u32[]{:S(2)}) collective-permute-start(bf16[128,1024]{1,0:T(8,128)(2,1)S(1)} %get-tuple-element.24.refs_0_), channel_id=1, source_target_pairs={{0,2},{1,63},{2,4},{3,1},{4,6},{5,3},{6,8},{7,5},{8,10},{9,7},{10,... | collective-permute-start | bytes 786440 | tf_op jit(solution)/shard_map/ppermute | solution.py:259
  26.3 0.1 lay.9
  26.4 1.3 collective-permute-start.13
  27.7 1.9 %collective-permute-done.12.refs_0_ = bf16[128,1024]{1,0:T(8,128)(2,1)S(1)} collective-permute-done((bf16[128,1024]{1,0:T(8,128)(2,1)S(1)}, bf16[128,1024]{1,0:T(8,128)(2,1)S(1)}, u32[]{:S(2)}, u32[]{:S(2)}) %collective-permute-start.12) | collective-permute-done | bytes 262176 | tf_op jit(solution)/shard_map/ppermute | solution.py:259
  29.6 3.1 %collective-permute-start.15 = (bf16[128,1024]{1,0:T(8,128)(2,1)S(1)}, bf16[128,1024]{1,0:T(8,128)(2,1)S(1)}, u32[]{:S(2)}, u32[]{:S(2)}) collective-permute-start(bf16[128,1024]{1,0:T(8,128)(2,1)S(1)} %collective-permute-done.12.refs_0_), channel_id=1, source_target_pairs={{0,2},{1,63},{2,4},{3,1},{4,6},{5,3},{6,8},{7,5},{8,10},{9,7},{10,... | collective-permute-start | bytes 786440 | tf_op jit(solution)/shard_map/ppermute | solution.py:259
  32.7 2.8 %collective-permute-start.16 = (bf16[128,1024]{1,0:T(8,128)(2,1)S(1)}, bf16[128,1024]{1,0:T(8,128)(2,1)S(1)}, u32[]{:S(2)}, u32[]{:S(2)}) collective-permute-start(bf16[128,1024]{1,0:T(8,128)(2,1)S(1)} %collective-permute-done.13.refs_1_), channel_id=1, source_target_pairs={{0,2},{1,63},{2,4},{3,1},{4,6},{5,3},{6,8},{7,5},{8,10},{9,7},{10,... | collective-permute-start | bytes 786440 | tf_op jit(solution)/shard_map/ppermute | solution.py:259
  35.5 0.5 collective-permute-done.15.refs_0_
  36.0 3.1 %collective-permute-start.18 = (bf16[128,1024]{1,0:T(8,128)(2,1)S(1)}, bf16[128,1024]{1,0:T(8,128)(2,1)S(1)}, u32[]{:S(2)}, u32[]{:S(2)}) collective-permute-start(bf16[128,1024]{1,0:T(8,128)(2,1)S(1)} %collective-permute-done.15.refs_0_), channel_id=1, source_target_pairs={{0,2},{1,63},{2,4},{3,1},{4,6},{5,3},{6,8},{7,5},{8,10},{9,7},{10,... | collective-permute-start | bytes 786440 | tf_op jit(solution)/shard_map/ppermute | solution.py:259
  39.1 2.8 %collective-permute-start.19 = (bf16[128,1024]{1,0:T(8,128)(2,1)S(1)}, bf16[128,1024]{1,0:T(8,128)(2,1)S(1)}, u32[]{:S(2)}, u32[]{:S(2)}) collective-permute-start(bf16[128,1024]{1,0:T(8,128)(2,1)S(1)} %collective-permute-done.16.refs_1_), channel_id=1, source_target_pairs={{0,2},{1,63},{2,4},{3,1},{4,6},{5,3},{6,8},{7,5},{8,10},{9,7},{10,... | collective-permute-start | bytes 786440 | tf_op jit(solution)/shard_map/ppermute | solution.py:259
  41.9 2.8 %collective-permute-start.5 = (bf16[128,1024]{1,0:T(8,128)(2,1)S(1)}, bf16[128,1024]{1,0:T(8,128)(2,1)S(1)}, u32[]{:S(2)}, u32[]{:S(2)}) collective-permute-start(bf16[128,1024]{1,0:T(8,128)(2,1)S(1)} %collective-permute-done.4.refs_2_), channel_id=1, source_target_pairs={{0,2},{1,63},{2,4},{3,1},{4,6},{5,3},{6,8},{7,5},{8,10},{9,7},{10,... | collective-permute-start | bytes 786440 | tf_op jit(solution)/shard_map/ppermute | solution.py:259
  44.8 2.8 %collective-permute-start.20 = (bf16[128,1024]{1,0:T(8,128)(2,1)S(1)}, bf16[128,1024]{1,0:T(8,128)(2,1)S(1)}, u32[]{:S(2)}, u32[]{:S(2)}) collective-permute-start(bf16[128,1024]{1,0:T(8,128)(2,1)S(1)} %collective-permute-done.18.refs_0_), channel_id=1, source_target_pairs={{0,2},{1,63},{2,4},{3,1},{4,6},{5,3},{6,8},{7,5},{8,10},{9,7},{10,... | collective-permute-start | bytes 786440 | tf_op jit(solution)/shard_map/ppermute | solution.py:259
  47.6 2.8 %collective-permute-start.21 = (bf16[128,1024]{1,0:T(8,128)(2,1)S(1)}, bf16[128,1024]{1,0:T(8,128)(2,1)S(1)}, u32[]{:S(2)}, u32[]{:S(2)}) collective-permute-start(bf16[128,1024]{1,0:T(8,128)(2,1)S(1)} %collective-permute-done.19.refs_1_), channel_id=1, source_target_pairs={{0,2},{1,63},{2,4},{3,1},{4,6},{5,3},{6,8},{7,5},{8,10},{9,7},{10,... | collective-permute-start | bytes 786440 | tf_op jit(solution)/shard_map/ppermute | solution.py:259
  50.4 2.8 %collective-permute-start.6 = (bf16[128,1024]{1,0:T(8,128)(2,1)S(1)}, bf16[128,1024]{1,0:T(8,128)(2,1)S(1)}, u32[]{:S(2)}, u32[]{:S(2)}) collective-permute-start(bf16[128,1024]{1,0:T(8,128)(2,1)S(1)} %collective-permute-done.5.refs_2_), channel_id=1, source_target_pairs={{0,2},{1,63},{2,4},{3,1},{4,6},{5,3},{6,8},{7,5},{8,10},{9,7},{10,... | collective-permute-start | bytes 786440 | tf_op jit(solution)/shard_map/ppermute | solution.py:259
  53.2 2.8 %collective-permute-start.23 = (bf16[128,1024]{1,0:T(8,128)(2,1)S(1)}, bf16[128,1024]{1,0:T(8,128)(2,1)S(1)}, u32[]{:S(2)}, u32[]{:S(2)}) collective-permute-start(bf16[128,1024]{1,0:T(8,128)(2,1)S(1)} %collective-permute-done.20.refs_0_), channel_id=1, source_target_pairs={{0,2},{1,63},{2,4},{3,1},{4,6},{5,3},{6,8},{7,5},{8,10},{9,7},{10,... | collective-permute-start | bytes 786440 | tf_op jit(solution)/shard_map/ppermute | solution.py:259
  56.0 2.8 %collective-permute-start.24 = (bf16[128,1024]{1,0:T(8,128)(2,1)S(1)}, bf16[128,1024]{1,0:T(8,128)(2,1)S(1)}, u32[]{:S(2)}, u32[]{:S(2)}) collective-permute-start(bf16[128,1024]{1,0:T(8,128)(2,1)S(1)} %collective-permute-done.21.refs_1_), channel_id=1, source_target_pairs={{0,2},{1,63},{2,4},{3,1},{4,6},{5,3},{6,8},{7,5},{8,10},{9,7},{10,... | collective-permute-start | bytes 786440 | tf_op jit(solution)/shard_map/ppermute | solution.py:259
  58.8 2.8 %collective-permute-start.7 = (bf16[128,1024]{1,0:T(8,128)(2,1)S(1)}, bf16[128,1024]{1,0:T(8,128)(2,1)S(1)}, u32[]{:S(2)}, u32[]{:S(2)}) collective-permute-start(bf16[128,1024]{1,0:T(8,128)(2,1)S(1)} %collective-permute-done.6.refs_2_), channel_id=1, source_target_pairs={{0,2},{1,63},{2,4},{3,1},{4,6},{5,3},{6,8},{7,5},{8,10},{9,7},{10,... | collective-permute-start | bytes 786440 | tf_op jit(solution)/shard_map/ppermute | solution.py:259
  61.6 2.8 %collective-permute-start.25 = (bf16[128,1024]{1,0:T(8,128)(2,1)S(1)}, bf16[128,1024]{1,0:T(8,128)(2,1)S(1)}, u32[]{:S(2)}, u32[]{:S(2)}) collective-permute-start(bf16[128,1024]{1,0:T(8,128)(2,1)S(1)} %collective-permute-done.23.refs_0_), channel_id=1, source_target_pairs={{0,2},{1,63},{2,4},{3,1},{4,6},{5,3},{6,8},{7,5},{8,10},{9,7},{10,... | collective-permute-start | bytes 786440 | tf_op jit(solution)/shard_map/ppermute | solution.py:259
  64.4 2.8 %collective-permute-start.26 = (bf16[128,1024]{1,0:T(8,128)(2,1)S(1)}, bf16[128,1024]{1,0:T(8,128)(2,1)S(1)}, u32[]{:S(2)}, u32[]{:S(2)}) collective-permute-start(bf16[128,1024]{1,0:T(8,128)(2,1)S(1)} %collective-permute-done.24.refs_1_), channel_id=1, source_target_pairs={{0,2},{1,63},{2,4},{3,1},{4,6},{5,3},{6,8},{7,5},{8,10},{9,7},{10,... | collective-permute-start | bytes 786440 | tf_op jit(solution)/shard_map/ppermute | solution.py:259
  67.2 2.8 %collective-permute-start.8 = (bf16[128,1024]{1,0:T(8,128)(2,1)S(1)}, bf16[128,1024]{1,0:T(8,128)(2,1)S(1)}, u32[]{:S(2)}, u32[]{:S(2)}) collective-permute-start(bf16[128,1024]{1,0:T(8,128)(2,1)S(1)} %collective-permute-done.7.refs_2_), channel_id=1, source_target_pairs={{0,2},{1,63},{2,4},{3,1},{4,6},{5,3},{6,8},{7,5},{8,10},{9,7},{10,... | collective-permute-start | bytes 786440 | tf_op jit(solution)/shard_map/ppermute | solution.py:259
  70.0 2.8 %collective-permute-start.27 = (bf16[128,1024]{1,0:T(8,128)(2,1)S(1)}, bf16[128,1024]{1,0:T(8,128)(2,1)S(1)}, u32[]{:S(2)}, u32[]{:S(2)}) collective-permute-start(bf16[128,1024]{1,0:T(8,128)(2,1)S(1)} %collective-permute-done.25.refs_0_), channel_id=1, source_target_pairs={{0,2},{1,63},{2,4},{3,1},{4,6},{5,3},{6,8},{7,5},{8,10},{9,7},{10,... | collective-permute-start | bytes 786440 | tf_op jit(solution)/shard_map/ppermute | solution.py:259
  72.8 2.8 %collective-permute-start.28 = (bf16[128,1024]{1,0:T(8,128)(2,1)S(1)}, bf16[128,1024]{1,0:T(8,128)(2,1)S(1)}, u32[]{:S(2)}, u32[]{:S(2)}) collective-permute-start(bf16[128,1024]{1,0:T(8,128)(2,1)S(1)} %collective-permute-done.26.refs_1_), channel_id=1, source_target_pairs={{0,2},{1,63},{2,4},{3,1},{4,6},{5,3},{6,8},{7,5},{8,10},{9,7},{10,... | collective-permute-start | bytes 786440 | tf_op jit(solution)/shard_map/ppermute | solution.py:259
  75.7 2.8 %collective-permute-start.9 = (bf16[128,1024]{1,0:T(8,128)(2,1)S(1)}, bf16[128,1024]{1,0:T(8,128)(2,1)S(1)}, u32[]{:S(2)}, u32[]{:S(2)}) collective-permute-start(bf16[128,1024]{1,0:T(8,128)(2,1)S(1)} %collective-permute-done.8.refs_2_), channel_id=1, source_target_pairs={{0,2},{1,63},{2,4},{3,1},{4,6},{5,3},{6,8},{7,5},{8,10},{9,7},{10,... | collective-permute-start | bytes 786440 | tf_op jit(solution)/shard_map/ppermute | solution.py:259
  78.5 0.1 collective-permute-start
  78.6 2.8 %collective-permute-start.30 = (bf16[128,1024]{1,0:T(8,128)(2,1)S(1)}, bf16[128,1024]{1,0:T(8,128)(2,1)S(1)}, u32[]{:S(2)}, u32[]{:S(2)}) collective-permute-start(bf16[128,1024]{1,0:T(8,128)(2,1)S(1)} %collective-permute-done.27.refs_0_), channel_id=1, source_target_pairs={{0,3},{1,62},{2,5},{3,0},{4,7},{5,2},{6,9},{7,4},{8,11},{9,6},{10,... | collective-permute-start | bytes 786440 | tf_op jit(solution)/shard_map/ppermute | solution.py:259
  81.4 2.8 %collective-permute-start.31 = (bf16[128,1024]{1,0:T(8,128)(2,1)S(1)}, bf16[128,1024]{1,0:T(8,128)(2,1)S(1)}, u32[]{:S(2)}, u32[]{:S(2)}) collective-permute-start(bf16[128,1024]{1,0:T(8,128)(2,1)S(1)} %collective-permute-done.28.refs_1_), channel_id=1, source_target_pairs={{0,3},{1,62},{2,5},{3,0},{4,7},{5,2},{6,9},{7,4},{8,11},{9,6},{10,... | collective-permute-start | bytes 786440 | tf_op jit(solution)/shard_map/ppermute | solution.py:259
  84.3 0.6 collective-permute-start.14
  84.9 4.6 %collective-permute-done.14.note_ref = f32[2,384]{1,0:T(2,128)S(1)} collective-permute-done((f32[2,384]{1,0:T(2,128)S(1)}, f32[2,384]{1,0:T(2,128)S(1)}, u32[]{:S(2)}, u32[]{:S(2)}) %collective-permute-start.14) | collective-permute-done | bytes 3104 | tf_op jit(solution)/shard_map/ppermute | solution.py:259
  89.4 0.1 pad_maximum_fusion.1
  89.5 1.9 %collective-permute-start.17 = (f32[4,384]{1,0:T(4,128)S(1)}, f32[4,384]{1,0:T(4,128)S(1)}, u32[]{:S(2)}, u32[]{:S(2)}) collective-permute-start(f32[4,384]{1,0:T(4,128)S(1)} %pad_maximum_fusion.1), channel_id=1, source_target_pairs={{0,4},{1,61},{2,6},{3,63},{4,8},{5,1},{6,10},{7,3},{8,12},{9,5},{1... | collective-permute-start | bytes 18440 | tf_op jit(solution)/shard_map/ppermute | solution.py:259
  91.4 6.8 %collective-permute-start.1 = (f32[2,384]{1,0:T(2,128)S(1)}, f32[2,384]{1,0:T(2,128)S(1)}, u32[]{:S(2)}, u32[]{:S(2)}) collective-permute-start(f32[2,384]{1,0:T(2,128)S(1)} %pad_maximum_fusion.2.note_ref.own_note_ref), channel_id=1, source_target_pairs={{0,17},{1,48},{2,19},{3,50},{4,21},{5,52},{6,23},{7,54},{8,25},{9,... | collective-permute-start | bytes 9224 | tf_op jit(solution)/shard_map/ppermute | solution.py:259
  98.3 0.1 columns.1.own_columns_ref.refs_4_.refs_3_
  98.4 4.8 %collective-permute-done.1.refs_0_ = f32[2,384]{1,0:T(2,128)S(1)} collective-permute-done((f32[2,384]{1,0:T(2,128)S(1)}, f32[2,384]{1,0:T(2,128)S(1)}, u32[]{:S(2)}, u32[]{:S(2)}) %collective-permute-start.1) | collective-permute-done | bytes 3104 | tf_op jit(solution)/shard_map/ppermute | solution.py:259
  103.2 1.1 collective-permute-start.29
  104.3 1.0 collective-permute-start.10
  105.3 0.1 pad_maximum_fusion
  105.4 3.7 %collective-permute-start.22 = (f32[8,384]{1,0:T(8,128)S(1)}, f32[8,384]{1,0:T(8,128)S(1)}, u32[]{:S(2)}, u32[]{:S(2)}) collective-permute-start(f32[8,384]{1,0:T(8,128)S(1)} %pad_maximum_fusion), channel_id=1, source_target_pairs={{0,8},{1,57},{2,10},{3,59},{4,12},{5,61},{6,14},{7,63},{8,16},{9,1... | collective-permute-start | bytes 36872 | tf_op jit(solution)/shard_map/ppermute | solution.py:259
  109.2 0.1 collective-permute-start.32
  109.3 0.7 collective-permute-done.10.refs_2_
  110.0 2.9 %collective-permute-start.11 = (bf16[128,1024]{1,0:T(8,128)(2,1)S(1)}, bf16[128,1024]{1,0:T(8,128)(2,1)S(1)}, u32[]{:S(2)}, u32[]{:S(2)}) collective-permute-start(bf16[128,1024]{1,0:T(8,128)(2,1)S(1)} %collective-permute-done.10.refs_2_), channel_id=1, source_target_pairs={{0,3},{1,62},{2,5},{3,0},{4,7},{5,2},{6,9},{7,4},{8,11},{9,6},{10,... | collective-permute-start | bytes 786440 | tf_op jit(solution)/shard_map/ppermute | solution.py:259
  112.9 1.3 visit.8
  114.3 1.1 visit.9
  115.4 1.1 visit.10
  116.6 1.1 visit.11
  117.7 1.1 visit.12
  118.9 1.1 visit.13
  120.0 1.1 visit.14
  121.1 6.2 %collective-permute-start.33 = (f32[1,384]{1,0:T(1,128)S(1)}, f32[1,384]{1,0:T(1,128)S(1)}, u32[]{:S(2)}, u32[]{:S(2)}) collective-permute-start(f32[1,384]{1,0:T(1,128)S(1)} %get-tuple-element.42), channel_id=1, source_target_pairs={{0,17},{1,48},{2,19},{3,50},{4,21},{5,52},{6,23},{7,54},{8,25},{9,... | collective-permute-start | bytes 4616 | tf_op jit(solution)/shard_map/ppermute | solution.py:259
  127.4 1.1 visit.15
  128.5 0.1 collective-permute-start.34
  128.6 2.0 %meet.3.refs_20_ = f32[1,256]{1,0:T(1,128)S(1)} custom-call(f32[2,384]{1,0:T(2,128)S(1)} %collective-permute-done.1.refs_0_, bf16[128,1024]{1,0:T(8,128)(2,1)S(1)} %collective-permute-done.30.refs_0_.refs_1_, bf16[128,1024]{1,0:T(8,128)(2,1)S(1)} %collective-permute-done.31.refs_1_.refs_2_, ...), custom_call_target="tpu_custom_call" | custom-call | flops 1610612736 | bytes 6815744 | tf_op jit(solution)/shard_map/meet/pallas_call | solution.py:184
  130.6 0.3 meet.4.refs_21_
  131.0 1.9 %collective-permute-done.33.refs_22_ = f32[1,384]{1,0:T(1,128)S(1)} collective-permute-done((f32[1,384]{1,0:T(1,128)S(1)}, f32[1,384]{1,0:T(1,128)S(1)}, u32[]{:S(2)}, u32[]{:S(2)}) %collective-permute-start.33) | collective-permute-done | bytes 1568 | tf_op jit(solution)/shard_map/ppermute | solution.py:259
  132.9 0.2 collective-permute-done.34.refs_23_
  133.1 2.6 %meet.5 = f32[32,1,384]{2,1,0:T(1,128)} custom-call(f32[2,384]{1,0:T(2,128)S(1)} %collective-permute-done.1.refs_0_, bf16[128,1024]{1,0:T(8,128)(2,1)S(1)} %collective-permute-done.11.refs_1_, bf16[384,1024]{1,0:T(8,128)(2,1)S(1)} %get-tuple-element.27.whole_ref.own_ref.refs_3_.refs_2_, s32[384,128]{1,0:T(8,128)S(1)} %columns.1.own_columns_ref.refs_4_.refs_3_, ...), custom_call_target="tpu_custom_call" | custom-call | flops 855638016 | bytes 6946816 | tf_op jit(solution)/shard_map/meet/pallas_call | solution.py:184
  135.7 12.6 %all-to-all-start = ((f32[32,1,384]{2,1,0:T(1,128)}), f32[32,1,384]{2,1,0:T(1,128)S(1)}, u32[]{:S(2)}, u32[]{:S(2)}) async-start(f32[32,1,384]{2,1,0:T(1,128)} %meet.5), calls=%async_computation | async-start | bytes 98304 | tf_op jit(solution)/shard_map/all_to_all | solution.py:302
  148.3 22.0 %all-to-all-done = f32[32,1,384]{2,1,0:T(1,128)S(1)} async-done(((f32[32,1,384]{2,1,0:T(1,128)}), f32[32,1,384]{2,1,0:T(1,128)S(1)}, u32[]{:S(2)}, u32[]{:S(2)}) %all-to-all-start) | async-done | bytes 49184 | tf_op jit(solution)/shard_map/all_to_all | solution.py:302
  170.3 3.3 %collective-permute-start.35 = (f32[32,384]{1,0:T(8,128)S(1)}, f32[32,384]{1,0:T(8,128)S(1)}, u32[]{:S(2)}, u32[]{:S(2)}) collective-permute-start(f32[32,384]{1,0:T(8,128)S(1)} %bitcast.9), channel_id=1, source_target_pairs={{0,1},{1,0},{2,3},{3,2},{4,5},{5,4},{6,7},{7,6},{8,9},{9,8},{10,11... | collective-permute-start | bytes 147464 | tf_op jit(solution)/shard_map/ppermute | solution.py:262
  173.5 0.1 pad_add_fusion.place_ref
  174.3 0.2 collective-permute-done.35.theirs_ref
  174.4 1.2 finish.1
  (48 shorter events, 0.6 us)
Async XLA Ops:
  0.6 1.0 copy-start
  1.8 24.5 %collective-permute-start.2 = (bf16[128,1024]{1,0:T(8,128)(2,1)S(1)}, bf16[128,1024]{1,0:T(8,128)(2,1)S(1)}, u32[]{:S(2)}, u32[]{:S(2)}) collective-permute-start(bf16[128,1024]{1,0:T(8,128)(2,1)S(1)} %get-tuple-element.24.refs_0_), channel_id=1, source_target_pairs={{0,1},{1,0},{2,3},{3,2},{4,5},{5,4},{6,7},{7,6},{8,9},{9,8},{10,11... | collective-permute-start | bytes 786440 | tf_op jit(solution)/shard_map/ppermute | solution.py:262
  22.3 3.9 %collective-permute-start.3 = (bf16[64,1024]{1,0:T(8,128)(2,1)S(1)}, bf16[64,1024]{1,0:T(8,128)(2,1)S(1)}, u32[]{:S(2)}, u32[]{:S(2)}) collective-permute-start(bf16[64,1024]{1,0:T(8,128)(2,1)S(1)} %get-tuple-element.25.refs_1_), channel_id=1, source_target_pairs={{0,1},{1,0},{2,3},{3,2},{4,5},{5,4},{6,7},{7,6},{8,9},{9,8},{10,11... | collective-permute-start | bytes 393224 | tf_op jit(solution)/shard_map/ppermute | solution.py:262
  22.5 7.1 %collective-permute-start.12 = (bf16[128,1024]{1,0:T(8,128)(2,1)S(1)}, bf16[128,1024]{1,0:T(8,128)(2,1)S(1)}, u32[]{:S(2)}, u32[]{:S(2)}) collective-permute-start(bf16[128,1024]{1,0:T(8,128)(2,1)S(1)} %get-tuple-element.24.refs_0_), channel_id=1, source_target_pairs={{0,2},{1,63},{2,4},{3,1},{4,6},{5,3},{6,8},{7,5},{8,10},{9,7},{10,... | collective-permute-start | bytes 786440 | tf_op jit(solution)/shard_map/ppermute | solution.py:259
  26.4 49.3 %copy-start.1 = (s32[192]{0:T(256)S(1)}, s32[192]{0:T(256)}, u32[]{:S(2)}) copy-start(s32[192]{0:T(256)} %param.4) | copy-start | bytes 2308
  26.4 6.3 %collective-permute-start.13 = (bf16[128,1024]{1,0:T(8,128)(2,1)S(1)}, bf16[128,1024]{1,0:T(8,128)(2,1)S(1)}, u32[]{:S(2)}, u32[]{:S(2)}) collective-permute-start(bf16[128,1024]{1,0:T(8,128)(2,1)S(1)} %get-tuple-element.28), channel_id=1, source_target_pairs={{0,2},{1,63},{2,4},{3,1},{4,6},{5,3},{6,8},{7,5},{8,10},{9,7},{10,... | collective-permute-start | bytes 786440 | tf_op jit(solution)/shard_map/ppermute | solution.py:259
  29.6 6.4 %collective-permute-start.15 = (bf16[128,1024]{1,0:T(8,128)(2,1)S(1)}, bf16[128,1024]{1,0:T(8,128)(2,1)S(1)}, u32[]{:S(2)}, u32[]{:S(2)}) collective-permute-start(bf16[128,1024]{1,0:T(8,128)(2,1)S(1)} %collective-permute-done.12.refs_0_), channel_id=1, source_target_pairs={{0,2},{1,63},{2,4},{3,1},{4,6},{5,3},{6,8},{7,5},{8,10},{9,7},{10,... | collective-permute-start | bytes 786440 | tf_op jit(solution)/shard_map/ppermute | solution.py:259
  32.7 6.4 %collective-permute-start.16 = (bf16[128,1024]{1,0:T(8,128)(2,1)S(1)}, bf16[128,1024]{1,0:T(8,128)(2,1)S(1)}, u32[]{:S(2)}, u32[]{:S(2)}) collective-permute-start(bf16[128,1024]{1,0:T(8,128)(2,1)S(1)} %collective-permute-done.13.refs_1_), channel_id=1, source_target_pairs={{0,2},{1,63},{2,4},{3,1},{4,6},{5,3},{6,8},{7,5},{8,10},{9,7},{10,... | collective-permute-start | bytes 786440 | tf_op jit(solution)/shard_map/ppermute | solution.py:259
  35.5 6.4 %collective-permute-start.4 = (bf16[128,1024]{1,0:T(8,128)(2,1)S(1)}, bf16[128,1024]{1,0:T(8,128)(2,1)S(1)}, u32[]{:S(2)}, u32[]{:S(2)}) collective-permute-start(bf16[128,1024]{1,0:T(8,128)(2,1)S(1)} %get-tuple-element.26), channel_id=1, source_target_pairs={{0,2},{1,63},{2,4},{3,1},{4,6},{5,3},{6,8},{7,5},{8,10},{9,7},{10,... | collective-permute-start | bytes 786440 | tf_op jit(solution)/shard_map/ppermute | solution.py:259
  36.0 8.7 %collective-permute-start.18 = (bf16[128,1024]{1,0:T(8,128)(2,1)S(1)}, bf16[128,1024]{1,0:T(8,128)(2,1)S(1)}, u32[]{:S(2)}, u32[]{:S(2)}) collective-permute-start(bf16[128,1024]{1,0:T(8,128)(2,1)S(1)} %collective-permute-done.15.refs_0_), channel_id=1, source_target_pairs={{0,2},{1,63},{2,4},{3,1},{4,6},{5,3},{6,8},{7,5},{8,10},{9,7},{10,... | collective-permute-start | bytes 786440 | tf_op jit(solution)/shard_map/ppermute | solution.py:259
  39.1 8.4 %collective-permute-start.19 = (bf16[128,1024]{1,0:T(8,128)(2,1)S(1)}, bf16[128,1024]{1,0:T(8,128)(2,1)S(1)}, u32[]{:S(2)}, u32[]{:S(2)}) collective-permute-start(bf16[128,1024]{1,0:T(8,128)(2,1)S(1)} %collective-permute-done.16.refs_1_), channel_id=1, source_target_pairs={{0,2},{1,63},{2,4},{3,1},{4,6},{5,3},{6,8},{7,5},{8,10},{9,7},{10,... | collective-permute-start | bytes 786440 | tf_op jit(solution)/shard_map/ppermute | solution.py:259
  41.9 8.4 %collective-permute-start.5 = (bf16[128,1024]{1,0:T(8,128)(2,1)S(1)}, bf16[128,1024]{1,0:T(8,128)(2,1)S(1)}, u32[]{:S(2)}, u32[]{:S(2)}) collective-permute-start(bf16[128,1024]{1,0:T(8,128)(2,1)S(1)} %collective-permute-done.4.refs_2_), channel_id=1, source_target_pairs={{0,2},{1,63},{2,4},{3,1},{4,6},{5,3},{6,8},{7,5},{8,10},{9,7},{10,... | collective-permute-start | bytes 786440 | tf_op jit(solution)/shard_map/ppermute | solution.py:259
  44.8 8.4 %collective-permute-start.20 = (bf16[128,1024]{1,0:T(8,128)(2,1)S(1)}, bf16[128,1024]{1,0:T(8,128)(2,1)S(1)}, u32[]{:S(2)}, u32[]{:S(2)}) collective-permute-start(bf16[128,1024]{1,0:T(8,128)(2,1)S(1)} %collective-permute-done.18.refs_0_), channel_id=1, source_target_pairs={{0,2},{1,63},{2,4},{3,1},{4,6},{5,3},{6,8},{7,5},{8,10},{9,7},{10,... | collective-permute-start | bytes 786440 | tf_op jit(solution)/shard_map/ppermute | solution.py:259
  47.6 8.4 %collective-permute-start.21 = (bf16[128,1024]{1,0:T(8,128)(2,1)S(1)}, bf16[128,1024]{1,0:T(8,128)(2,1)S(1)}, u32[]{:S(2)}, u32[]{:S(2)}) collective-permute-start(bf16[128,1024]{1,0:T(8,128)(2,1)S(1)} %collective-permute-done.19.refs_1_), channel_id=1, source_target_pairs={{0,2},{1,63},{2,4},{3,1},{4,6},{5,3},{6,8},{7,5},{8,10},{9,7},{10,... | collective-permute-start | bytes 786440 | tf_op jit(solution)/shard_map/ppermute | solution.py:259
  50.4 8.4 %collective-permute-start.6 = (bf16[128,1024]{1,0:T(8,128)(2,1)S(1)}, bf16[128,1024]{1,0:T(8,128)(2,1)S(1)}, u32[]{:S(2)}, u32[]{:S(2)}) collective-permute-start(bf16[128,1024]{1,0:T(8,128)(2,1)S(1)} %collective-permute-done.5.refs_2_), channel_id=1, source_target_pairs={{0,2},{1,63},{2,4},{3,1},{4,6},{5,3},{6,8},{7,5},{8,10},{9,7},{10,... | collective-permute-start | bytes 786440 | tf_op jit(solution)/shard_map/ppermute | solution.py:259
  53.2 8.4 %collective-permute-start.23 = (bf16[128,1024]{1,0:T(8,128)(2,1)S(1)}, bf16[128,1024]{1,0:T(8,128)(2,1)S(1)}, u32[]{:S(2)}, u32[]{:S(2)}) collective-permute-start(bf16[128,1024]{1,0:T(8,128)(2,1)S(1)} %collective-permute-done.20.refs_0_), channel_id=1, source_target_pairs={{0,2},{1,63},{2,4},{3,1},{4,6},{5,3},{6,8},{7,5},{8,10},{9,7},{10,... | collective-permute-start | bytes 786440 | tf_op jit(solution)/shard_map/ppermute | solution.py:259
  56.0 8.4 %collective-permute-start.24 = (bf16[128,1024]{1,0:T(8,128)(2,1)S(1)}, bf16[128,1024]{1,0:T(8,128)(2,1)S(1)}, u32[]{:S(2)}, u32[]{:S(2)}) collective-permute-start(bf16[128,1024]{1,0:T(8,128)(2,1)S(1)} %collective-permute-done.21.refs_1_), channel_id=1, source_target_pairs={{0,2},{1,63},{2,4},{3,1},{4,6},{5,3},{6,8},{7,5},{8,10},{9,7},{10,... | collective-permute-start | bytes 786440 | tf_op jit(solution)/shard_map/ppermute | solution.py:259
  58.8 8.4 %collective-permute-start.7 = (bf16[128,1024]{1,0:T(8,128)(2,1)S(1)}, bf16[128,1024]{1,0:T(8,128)(2,1)S(1)}, u32[]{:S(2)}, u32[]{:S(2)}) collective-permute-start(bf16[128,1024]{1,0:T(8,128)(2,1)S(1)} %collective-permute-done.6.refs_2_), channel_id=1, source_target_pairs={{0,2},{1,63},{2,4},{3,1},{4,6},{5,3},{6,8},{7,5},{8,10},{9,7},{10,... | collective-permute-start | bytes 786440 | tf_op jit(solution)/shard_map/ppermute | solution.py:259
  61.6 8.4 %collective-permute-start.25 = (bf16[128,1024]{1,0:T(8,128)(2,1)S(1)}, bf16[128,1024]{1,0:T(8,128)(2,1)S(1)}, u32[]{:S(2)}, u32[]{:S(2)}) collective-permute-start(bf16[128,1024]{1,0:T(8,128)(2,1)S(1)} %collective-permute-done.23.refs_0_), channel_id=1, source_target_pairs={{0,2},{1,63},{2,4},{3,1},{4,6},{5,3},{6,8},{7,5},{8,10},{9,7},{10,... | collective-permute-start | bytes 786440 | tf_op jit(solution)/shard_map/ppermute | solution.py:259
  64.4 8.4 %collective-permute-start.26 = (bf16[128,1024]{1,0:T(8,128)(2,1)S(1)}, bf16[128,1024]{1,0:T(8,128)(2,1)S(1)}, u32[]{:S(2)}, u32[]{:S(2)}) collective-permute-start(bf16[128,1024]{1,0:T(8,128)(2,1)S(1)} %collective-permute-done.24.refs_1_), channel_id=1, source_target_pairs={{0,2},{1,63},{2,4},{3,1},{4,6},{5,3},{6,8},{7,5},{8,10},{9,7},{10,... | collective-permute-start | bytes 786440 | tf_op jit(solution)/shard_map/ppermute | solution.py:259
  67.2 8.4 %collective-permute-start.8 = (bf16[128,1024]{1,0:T(8,128)(2,1)S(1)}, bf16[128,1024]{1,0:T(8,128)(2,1)S(1)}, u32[]{:S(2)}, u32[]{:S(2)}) collective-permute-start(bf16[128,1024]{1,0:T(8,128)(2,1)S(1)} %collective-permute-done.7.refs_2_), channel_id=1, source_target_pairs={{0,2},{1,63},{2,4},{3,1},{4,6},{5,3},{6,8},{7,5},{8,10},{9,7},{10,... | collective-permute-start | bytes 786440 | tf_op jit(solution)/shard_map/ppermute | solution.py:259
  70.0 8.6 %collective-permute-start.27 = (bf16[128,1024]{1,0:T(8,128)(2,1)S(1)}, bf16[128,1024]{1,0:T(8,128)(2,1)S(1)}, u32[]{:S(2)}, u32[]{:S(2)}) collective-permute-start(bf16[128,1024]{1,0:T(8,128)(2,1)S(1)} %collective-permute-done.25.refs_0_), channel_id=1, source_target_pairs={{0,2},{1,63},{2,4},{3,1},{4,6},{5,3},{6,8},{7,5},{8,10},{9,7},{10,... | collective-permute-start | bytes 786440 | tf_op jit(solution)/shard_map/ppermute | solution.py:259
  72.8 8.6 %collective-permute-start.28 = (bf16[128,1024]{1,0:T(8,128)(2,1)S(1)}, bf16[128,1024]{1,0:T(8,128)(2,1)S(1)}, u32[]{:S(2)}, u32[]{:S(2)}) collective-permute-start(bf16[128,1024]{1,0:T(8,128)(2,1)S(1)} %collective-permute-done.26.refs_1_), channel_id=1, source_target_pairs={{0,2},{1,63},{2,4},{3,1},{4,6},{5,3},{6,8},{7,5},{8,10},{9,7},{10,... | collective-permute-start | bytes 786440 | tf_op jit(solution)/shard_map/ppermute | solution.py:259
  75.7 28.6 %collective-permute-start.9 = (bf16[128,1024]{1,0:T(8,128)(2,1)S(1)}, bf16[128,1024]{1,0:T(8,128)(2,1)S(1)}, u32[]{:S(2)}, u32[]{:S(2)}) collective-permute-start(bf16[128,1024]{1,0:T(8,128)(2,1)S(1)} %collective-permute-done.8.refs_2_), channel_id=1, source_target_pairs={{0,2},{1,63},{2,4},{3,1},{4,6},{5,3},{6,8},{7,5},{8,10},{9,7},{10,... | collective-permute-start | bytes 786440 | tf_op jit(solution)/shard_map/ppermute | solution.py:259
  78.5 5.7 %collective-permute-start = (f32[2,192]{1,0:T(2,128)S(1)}, f32[2,192]{1,0:T(2,128)S(1)}, u32[]{:S(2)}, u32[]{:S(2)}) collective-permute-start(f32[2,192]{1,0:T(2,128)S(1)} %pad_maximum_fusion.3), channel_id=1, source_target_pairs={{0,1},{1,0},{2,3},{3,2},{4,5},{5,4},{6,7},{7,6},{8,9},{9,8},{10,11... | collective-permute-start | bytes 4616 | tf_op jit(solution)/shard_map/ppermute | solution.py:262
  78.6 30.5 %collective-permute-start.30 = (bf16[128,1024]{1,0:T(8,128)(2,1)S(1)}, bf16[128,1024]{1,0:T(8,128)(2,1)S(1)}, u32[]{:S(2)}, u32[]{:S(2)}) collective-permute-start(bf16[128,1024]{1,0:T(8,128)(2,1)S(1)} %collective-permute-done.27.refs_0_), channel_id=1, source_target_pairs={{0,3},{1,62},{2,5},{3,0},{4,7},{5,2},{6,9},{7,4},{8,11},{9,6},{10,... | collective-permute-start | bytes 786440 | tf_op jit(solution)/shard_map/ppermute | solution.py:259
  81.4 27.7 %collective-permute-start.31 = (bf16[128,1024]{1,0:T(8,128)(2,1)S(1)}, bf16[128,1024]{1,0:T(8,128)(2,1)S(1)}, u32[]{:S(2)}, u32[]{:S(2)}) collective-permute-start(bf16[128,1024]{1,0:T(8,128)(2,1)S(1)} %collective-permute-done.28.refs_1_), channel_id=1, source_target_pairs={{0,3},{1,62},{2,5},{3,0},{4,7},{5,2},{6,9},{7,4},{8,11},{9,6},{10,... | collective-permute-start | bytes 786440 | tf_op jit(solution)/shard_map/ppermute | solution.py:259
  84.3 5.1 %collective-permute-start.14 = (f32[2,384]{1,0:T(2,128)S(1)}, f32[2,384]{1,0:T(2,128)S(1)}, u32[]{:S(2)}, u32[]{:S(2)}) collective-permute-start(f32[2,384]{1,0:T(2,128)S(1)} %pad_maximum_fusion.2.note_ref.own_note_ref), channel_id=1, source_target_pairs={{0,2},{1,63},{2,4},{3,1},{4,6},{5,3},{6,8},{7,5},{8,10},{9,7},{10,... | collective-permute-start | bytes 9224 | tf_op jit(solution)/shard_map/ppermute | solution.py:259
  89.5 15.8 %collective-permute-start.17 = (f32[4,384]{1,0:T(4,128)S(1)}, f32[4,384]{1,0:T(4,128)S(1)}, u32[]{:S(2)}, u32[]{:S(2)}) collective-permute-start(f32[4,384]{1,0:T(4,128)S(1)} %pad_maximum_fusion.1), channel_id=1, source_target_pairs={{0,4},{1,61},{2,6},{3,63},{4,8},{5,1},{6,10},{7,3},{8,12},{9,5},{1... | collective-permute-start | bytes 18440 | tf_op jit(solution)/shard_map/ppermute | solution.py:259
  91.4 11.7 %collective-permute-start.1 = (f32[2,384]{1,0:T(2,128)S(1)}, f32[2,384]{1,0:T(2,128)S(1)}, u32[]{:S(2)}, u32[]{:S(2)}) collective-permute-start(f32[2,384]{1,0:T(2,128)S(1)} %pad_maximum_fusion.2.note_ref.own_note_ref), channel_id=1, source_target_pairs={{0,17},{1,48},{2,19},{3,50},{4,21},{5,52},{6,23},{7,54},{8,25},{9,... | collective-permute-start | bytes 9224 | tf_op jit(solution)/shard_map/ppermute | solution.py:259
  103.2 27.5 %collective-permute-start.29 = (f32[2,192]{1,0:T(2,128)S(1)}, f32[2,192]{1,0:T(2,128)S(1)}, u32[]{:S(2)}, u32[]{:S(2)}) collective-permute-start(f32[2,192]{1,0:T(2,128)S(1)} %slice.35), channel_id=1, source_target_pairs={{0,1},{1,0},{2,3},{3,2},{4,5},{5,4},{6,7},{7,6},{8,9},{9,8},{10,11... | collective-permute-start | bytes 4616 | tf_op jit(solution)/shard_map/ppermute | solution.py:262
  104.3 5.8 %collective-permute-start.10 = (bf16[128,1024]{1,0:T(8,128)(2,1)S(1)}, bf16[128,1024]{1,0:T(8,128)(2,1)S(1)}, u32[]{:S(2)}, u32[]{:S(2)}) collective-permute-start(bf16[128,1024]{1,0:T(8,128)(2,1)S(1)} %collective-permute-done.9.refs_2_), channel_id=1, source_target_pairs={{0,2},{1,63},{2,4},{3,1},{4,6},{5,3},{6,8},{7,5},{8,10},{9,7},{10,... | collective-permute-start | bytes 786440 | tf_op jit(solution)/shard_map/ppermute | solution.py:259
  105.4 7.5 %collective-permute-start.22 = (f32[8,384]{1,0:T(8,128)S(1)}, f32[8,384]{1,0:T(8,128)S(1)}, u32[]{:S(2)}, u32[]{:S(2)}) collective-permute-start(f32[8,384]{1,0:T(8,128)S(1)} %pad_maximum_fusion), channel_id=1, source_target_pairs={{0,8},{1,57},{2,10},{3,59},{4,12},{5,61},{6,14},{7,63},{8,16},{9,1... | collective-permute-start | bytes 36872 | tf_op jit(solution)/shard_map/ppermute | solution.py:259
  109.2 21.5 %collective-permute-start.32 = (bf16[192,1024]{1,0:T(8,128)(2,1)S(1)}, bf16[192,1024]{1,0:T(8,128)(2,1)S(1)}, u32[]{:S(2)}, u32[]{:S(2)}) collective-permute-start(bf16[192,1024]{1,0:T(8,128)(2,1)S(1)} %lay.17), channel_id=1, source_target_pairs={{0,1},{1,0},{2,3},{3,2},{4,5},{5,4},{6,7},{7,6},{8,9},{9,8},{10,11... | collective-permute-start | bytes 1179656 | tf_op jit(solution)/shard_map/ppermute | solution.py:262
  110.0 23.1 %collective-permute-start.11 = (bf16[128,1024]{1,0:T(8,128)(2,1)S(1)}, bf16[128,1024]{1,0:T(8,128)(2,1)S(1)}, u32[]{:S(2)}, u32[]{:S(2)}) collective-permute-start(bf16[128,1024]{1,0:T(8,128)(2,1)S(1)} %collective-permute-done.10.refs_2_), channel_id=1, source_target_pairs={{0,3},{1,62},{2,5},{3,0},{4,7},{5,2},{6,9},{7,4},{8,11},{9,6},{10,... | collective-permute-start | bytes 786440 | tf_op jit(solution)/shard_map/ppermute | solution.py:259
  121.1 11.8 %collective-permute-start.33 = (f32[1,384]{1,0:T(1,128)S(1)}, f32[1,384]{1,0:T(1,128)S(1)}, u32[]{:S(2)}, u32[]{:S(2)}) collective-permute-start(f32[1,384]{1,0:T(1,128)S(1)} %get-tuple-element.42), channel_id=1, source_target_pairs={{0,17},{1,48},{2,19},{3,50},{4,21},{5,52},{6,23},{7,54},{8,25},{9,... | collective-permute-start | bytes 4616 | tf_op jit(solution)/shard_map/ppermute | solution.py:259
  128.5 4.6 %collective-permute-start.34 = (f32[1,384]{1,0:T(1,128)S(1)}, f32[1,384]{1,0:T(1,128)S(1)}, u32[]{:S(2)}, u32[]{:S(2)}) collective-permute-start(f32[1,384]{1,0:T(1,128)S(1)} %get-tuple-element.43), channel_id=1, source_target_pairs={{0,3},{1,62},{2,5},{3,0},{4,7},{5,2},{6,9},{7,4},{8,11},{9,6},{10,... | collective-permute-start | bytes 4616 | tf_op jit(solution)/shard_map/ppermute | solution.py:259
  135.7 34.6 %all-to-all-start = ((f32[32,1,384]{2,1,0:T(1,128)}), f32[32,1,384]{2,1,0:T(1,128)S(1)}, u32[]{:S(2)}, u32[]{:S(2)}) async-start(f32[32,1,384]{2,1,0:T(1,128)} %meet.5), calls=%async_computation | async-start | bytes 98304 | tf_op jit(solution)/shard_map/all_to_all | solution.py:302
  170.3 4.1 %collective-permute-start.35 = (f32[32,384]{1,0:T(8,128)S(1)}, f32[32,384]{1,0:T(8,128)S(1)}, u32[]{:S(2)}, u32[]{:S(2)}) collective-permute-start(f32[32,384]{1,0:T(8,128)S(1)} %bitcast.9), channel_id=1, source_target_pairs={{0,1},{1,0},{2,3},{3,2},{4,5},{5,4},{6,7},{7,6},{8,9},{9,8},{10,11... | collective-permute-start | bytes 147464 | tf_op jit(solution)/shard_map/ppermute | solution.py:262
where the time goes:
time: 176 us
  starting transfers between devices  120 us (68%)
  waiting for transfers between devices  36.8 us (21%)
  Pallas kernels  15.8 us (9%)
    ppermute x30, starting transfers between devices, send(): return lax.ppermute(x, ('blk', 'sub'), moves(by, change))  82.3 us
    ppermute x6, starting transfers between devices, across(): return lax.ppermute(x, 'sub', [(0, 1), (1, 0)])  25.3 us
    all_to_all x1, waiting for transfers between devices, program(): lax.all_to_all(everyone, 'blk', 0, 0, tiled=True).reshape(chips, -1)  22 us
    ppermute x30, waiting for transfers between devices, send(): return lax.ppermute(x, ('blk', 'sub'), moves(by, change))  14.6 us
    all_to_all x1, starting transfers between devices, program(): lax.all_to_all(everyone, 'blk', 0, 0, tiled=True).reshape(chips, -1)  12.6 us
    pallas_call x8, Pallas kernels, visit(): pl.pallas_call(functools.partial(visit_kernel, acc is not None), out_shap...  8.89 us
    pallas_call x3, Pallas kernels, meet(): pl.pallas_call(functools.partial(meet_kernel, first_row, len(pieces), len...  4.91 us
  transfers between devices with their start and end apart: 37, of which 9 were waited for; matrix products, arithmetic and copies ran while one was open for 0% of the time, Pallas kernels for 7%

commit v1 on v0

--- a/solution.py
+++ b/solution.py
@@ -11,7 +11,7 @@
 
 LIMITS = 8
 label_stride = 268435456
-KEY_BASE = 32768
+TAIL = 8
 PIECES = 3
 
 
@@ -44,13 +44,28 @@
     )(embeddings)
 
 
-def whole_key(note):
-    return note[0:1].astype(jnp.int32) * KEY_BASE + note[1:2].astype(jnp.int32)
-
-
-def key_columns(note):
-    keys = whole_key(note)
+def key_columns(keys):
     return jnp.broadcast_to(keys, (128, keys.shape[1])).T
+
+
+def read_tail(ref, count):
+    tail = ref[ref.shape[0] - TAIL :, :count].astype(jnp.float32)
+    keys = jnp.zeros((1, count), jnp.int32)
+    for n in range(4):
+        keys = keys * 256 + tail[n : n + 1].astype(jnp.int32)
+    return keys, tail[4:5] + tail[5:6] + tail[6:7]
+
+
+def write_tail(ref, keys, acc):
+    rows = [((keys >> (24 - 8 * n)) & 255).astype(jnp.float32) for n in range(4)]
+    for _ in range(3):
+        part = acc.astype(jnp.bfloat16).astype(jnp.float32)
+        rows.append(part)
+        acc = acc - part
+    rows.append(jnp.zeros_like(acc))
+    count, start = keys.shape[1], ref.shape[0] - TAIL
+    ref[start:, :count] = jnp.concatenate(rows, axis=0).astype(jnp.bfloat16)
+    ref[start:, count:] = jnp.zeros((TAIL, ref.shape[1] - count), jnp.bfloat16)
 
 
 def best_of(best, row_key, low, rows, others, key_col):
@@ -91,68 +106,101 @@
     )(*pieces)
 
 
-def visit_kernel(at_home, note_ref, whole_ref, own_note_ref, own_ref, own_columns_ref, *refs):
+def front_visit_kernel(pieces, keys_ref, own_ref, own_columns_ref, *refs):
     best_ref, columns_ref = refs[-2:]
-    note = note_ref[...]
-    columns_ref[...] = key_columns(note)
-    if at_home:
-        key, rows_ref, others_ref, others_columns_ref = whole_key(own_note_ref[...]), own_ref, whole_ref, columns_ref
-    else:
-        key, rows_ref, others_ref, others_columns_ref = whole_key(note), whole_ref, own_ref, own_columns_ref
-    low = key & jnp.int32(-label_stride)
-    rows = rows_ref[...]
-    step = rows.shape[0] // 2
-
-    def part(n, best):
-        at = pl.ds(pl.multiple_of(n * step, step), step)
-        return best_of(best, key, low, rows, others_ref[at, :], others_columns_ref[at, :])
-
-    start = refs[0][...] if len(refs) > 2 else jnp.full(best_ref.shape, -1.0, jnp.float32)
-    best_ref[...] = lax.fori_loop(0, 2, part, start)
-
-
-def visit(note, whole, own, acc=None):
-    rows, width = whole.shape
-    own_note, own_whole, own_columns = own
-    operands = [note, whole, own_note, own_whole, own_columns]
-    operands += [] if acc is None else [acc]
-    return pl.pallas_call(
-        functools.partial(visit_kernel, acc is not None),
+    keys = keys_ref[...]
+    columns_ref[...] = key_columns(keys)
+    rows = jnp.concatenate([r[...] for r in refs[:pieces]], axis=0)
+    count = rows.shape[0]
+    row_key = keys[:, :count]
+    low = row_key & jnp.int32(-label_stride)
+    start = jnp.full(best_ref.shape, -1.0, jnp.float32)
+    best_ref[...] = best_of(start, row_key, low, rows, own_ref[...], own_columns_ref[...])
+
+
+def front_visit(keys, own, pieces):
+    total, width = own[0].shape
+    count = sum(p.shape[0] for p in pieces)
+    operands = [keys, *own, *pieces]
+    return pl.pallas_call(
+        functools.partial(front_visit_kernel, len(pieces)),
         out_shape=[
-            jax.ShapeDtypeStruct((1, rows), jnp.float32),
-            jax.ShapeDtypeStruct((rows, 128), jnp.int32),
+            jax.ShapeDtypeStruct((1, count), jnp.float32),
+            jax.ShapeDtypeStruct((total, 128), jnp.int32),
         ],
         in_specs=[VMEM] * len(operands),
         out_specs=[VMEM] * 2,
         compiler_params=PARAMS,
         cost_estimate=pl.CostEstimate(
-            flops=rows, bytes_accessed=6 * rows * width, transcendentals=0
-        ),
-        name="visit",
+            flops=total, bytes_accessed=4 * total * width, transcendentals=0
+        ),
+        name="front_visit",
     )(*operands)
 
 
-def columns_kernel(note_ref, columns_ref):
-    columns_ref[...] = key_columns(note_ref[...])
-
-
-def columns_of(note):
+def last_visit_kernel(begins, keys_ref, own_ref, own_columns_ref, front_ref, piece_ref, *refs):
+    if begins:
+        next_ref, out_ref = refs
+        earlier, next_keys = None, next_ref[...]
+    else:
+        next_out_ref, out_ref = refs
+        next_keys, earlier = read_tail(piece_ref, keys_ref.shape[1])
+        next_out_ref[...] = next_keys
+    keys = keys_ref[...]
+    count = out_ref.shape[0] - TAIL
+    rows = piece_ref[:count, :]
+    row_key = keys[:, keys.shape[1] - count :]
+    low = row_key & jnp.int32(-label_stride)
+    start = jnp.full((1, count), -1.0, jnp.float32)
+    best = best_of(start, row_key, low, rows, own_ref[...], own_columns_ref[...])
+    acc = jnp.concatenate([front_ref[...], best], axis=1)
+    if earlier is not None:
+        acc = jnp.maximum(acc, earlier)
+    out_ref[:count, :] = rows
+    write_tail(out_ref, next_keys, acc)
+
+
+def last_visit(keys, own, front, piece, next_keys=None):
+    begins = next_keys is not None
+    total, width = own[0].shape
+    rows = piece.shape[0] + (TAIL if begins else 0)
+    operands = [keys, *own, front, piece] + ([next_keys] if begins else [])
+    out_shape = [] if begins else [jax.ShapeDtypeStruct(keys.shape, jnp.int32)]
+    out_shape.append(jax.ShapeDtypeStruct((rows, width), jnp.bfloat16))
+    return pl.pallas_call(
+        functools.partial(last_visit_kernel, begins),
+        out_shape=out_shape,
+        in_specs=[VMEM] * len(operands),
+        out_specs=[VMEM] * len(out_shape),
+        compiler_params=PARAMS,
+        cost_estimate=pl.CostEstimate(
+            flops=total, bytes_accessed=4 * total * width, transcendentals=0
+        ),
+        name="last_visit",
+    )(*operands)
+
+
+def columns_kernel(keys_ref, columns_ref):
+    columns_ref[...] = key_columns(keys_ref[...])
+
+
+def columns_of(keys):
     return pl.pallas_call(
         columns_kernel,
-        out_shape=jax.ShapeDtypeStruct((note.shape[1], 128), jnp.int32),
+        out_shape=jax.ShapeDtypeStruct((keys.shape[1], 128), jnp.int32),
         in_specs=[VMEM],
         out_specs=VMEM,
         compiler_params=PARAMS,
         name="columns",
-    )(note)
+    )(keys)
 
 
 def meet_kernel(first_row, pieces, blocks, extra, spread, *refs):
     note_ref = refs[0]
-    rows = jnp.concatenate([r[...] for r in refs[1 : 1 + pieces]], axis=0)
+    count = min(sum(r.shape[0] for r in refs[1 : 1 + pieces]), note_ref.shape[1] - first_row)
+    rows = jnp.concatenate([r[...] for r in refs[1 : 1 + pieces]], axis=0)[:count]
     at = 1 + pieces
-    count = rows.shape[0]
-    row_key = whole_key(note_ref[...])[:, first_row : first_row + count]
+    row_key = note_ref[:, first_row : first_row + count]
     low = row_key & jnp.int32(-label_stride)
     best = jnp.full((1, count), -1.0, jnp.float32)
     for _ in range(blocks):
@@ -160,14 +208,14 @@
         at += 2
     if extra:
         others = jnp.concatenate([r[...] for r in refs[at + 1 : at + 1 + extra]], axis=0)
-        best = best_of(best, row_key, low, rows, others, key_columns(refs[at][...]))
+        columns = key_columns(refs[at][...])[: others.shape[0]]
+        best = best_of(best, row_key, low, rows, others, columns)
         at += 1 + extra
     out_ref = refs[-1]
     if spread:
         earlier = jnp.maximum(refs[at][...], refs[at + 1][...])
         best = jnp.concatenate([earlier, best], axis=1)
-        for ref in refs[at + 2 : -1]:
-            best = jnp.maximum(best, ref[...])
+        best = jnp.maximum(best, read_tail(refs[1], best.shape[1])[1])
         out_ref[...] = jnp.broadcast_to(best[:, None, :], out_ref.shape)
     else:
         out_ref[...] = best
@@ -261,43 +309,35 @@
     def across(x):
         return lax.ppermute(x, "sub", [(0, 1), (1, 0)])
 
-    size = cores * rows // PIECES
+    total = cores * rows
+    size = total // PIECES
     cuts = [(n * size, (n + 1) * size) for n in range(PIECES)]
-    everything = (0, cores * rows)
-    own_key = jnp.stack(
-        [(member_key // KEY_BASE).astype(jnp.float32), (member_key % KEY_BASE).astype(jnp.float32)]
-    )
+    keys = member_key.reshape(1, rows)
+    keys = jnp.concatenate([keys, across(keys)], axis=1)
+    next_keys = send(keys, 1)
     mine = normalize(embeddings, (size, rows - size))
     theirs = [across(m) for m in mine]
-    note = jnp.concatenate([own_key, across(own_key)], axis=1)
-    *rest, whole = lay([*mine, *theirs], [*cuts[1:], everything])
+    *rest, whole = lay([*mine, *theirs], [*cuts[1:], (0, total)])
     block = [mine[0], *rest]
-    notes = [note]
-    while len(notes) < hops:
-        by = len(notes)
-        far = send(jnp.concatenate(notes, axis=0), by)
-        notes += [far[2 * n : 2 * n + 2] for n in range(by)]
-    last_note = send(note, hops, True)
-    own = (note, whole, columns_of(note))
-    held = [own[1:]]
-    start = jnp.full((1, cores * rows), -1.0, jnp.float32)
-    acc, _ = visit(note, whole, own, start)
-    for h in range(1, hops):
+    own = (whole, columns_of(keys))
+    held = [own]
+    best, _ = front_visit(keys, own, block[:-1])
+    (block[-1],) = last_visit(keys, own, best, block[-1], next_keys)
+    for _ in range(1, hops):
+        keys = next_keys
         block = [send(b, 1) for b in block]
-        (whole,) = lay(block, [everything])
-        if h < hops - 1:
-            acc, columns = visit(notes[h], whole, own, acc)
-        else:
-            late, columns = visit(notes[h], whole, own)
+        best, columns = front_visit(keys, own, block[:-1])
+        next_keys, last = last_visit(keys, own, best, block[-1])
+        (whole,) = lay(block, [(0, total)])
         held.append((whole, columns))
-    acc = send(acc, hops, True)
-    late = send(late, 1, True)
+        block[-1] = last
+    last_keys = across(next_keys)
     block = [send(b, 1, True) for b in block]
     (first,) = lay(block[:-1], [(0, rows)])
-    facing = [across(last_note[:, :rows]), across(first)]
+    facing = [next_keys, across(first)]
     split = size * (PIECES - 1)
-    early = [meet(last_note, 0, block[:-1], held), meet(last_note, 0, block[:-1], [], facing)]
-    everyone = meet(last_note, split, block[-1:], held, facing, (*early, acc, late), chips)
+    early = [meet(last_keys, 0, block[:-1], held), meet(last_keys, 0, block[:-1], [], facing)]
+    everyone = meet(last_keys, split, block[-1:], held, facing, early, chips)
 
     gathered = lax.all_to_all(everyone, "blk", 0, 0, tiled=True).reshape(chips, -1)
     other_side = across(gathered)

time: 176 us -> 149 us (0.85)
  starting transfers between devices: 120 us -> 96.8 us
  Pallas kernels: 15.8 us -> 14 us
    ppermute x30 -> x25, starting transfers between devices: 82.3 us -> 59.3 us  [send(): return lax.ppermute(x, ('blk', 'sub'), moves(by, change))]
    ppermute x30 -> x25, waiting for transfers between devices: 14.6 us -> 12.5 us  [send(): return lax.ppermute(x, ('blk', 'sub'), moves(by, change))]
    pallas_call x9 -> x17, Pallas kernels: 9.02 us -> 7.2 us  [the longest x8 3.97 us: front_visit(): pl.pallas_call(functools.partial(front_visit_kernel, len(pieces)), out_sh...]
  transfers between devices with their start and end apart: 37 -> 32, of which waited for: 9 -> 9; matrix products, arithmetic and copies ran while one was open for 0% -> 0% of each run, Pallas kernels for 7% -> 7%
where the time goes in v1:
time: 149 us
  starting transfers between devices  96.8 us (65%)
  waiting for transfers between devices  35.1 us (24%)
  Pallas kernels  14 us (9%)
  between operations  1.54 us (1%)
    ppermute x25, starting transfers between devices, send(): return lax.ppermute(x, ('blk', 'sub'), moves(by, change))  59.3 us
    ppermute x6, starting transfers between devices, across(): return lax.ppermute(x, 'sub', [(0, 1), (1, 0)])  24.7 us
    all_to_all x1, waiting for transfers between devices, program(): lax.all_to_all(everyone, 'blk', 0, 0, tiled=True).reshape(chips, -1)  22 us
    all_to_all x1, starting transfers between devices, program(): lax.all_to_all(everyone, 'blk', 0, 0, tiled=True).reshape(chips, -1)  12.9 us
    ppermute x25, waiting for transfers between devices, send(): return lax.ppermute(x, ('blk', 'sub'), moves(by, change))  12.5 us
    pallas_call x3, Pallas kernels, meet(): pl.pallas_call(functools.partial(meet_kernel, first_row, len(pieces), len...  4.92 us
    pallas_call x8, Pallas kernels, front_visit(): pl.pallas_call(functools.partial(front_visit_kernel, len(pieces)), out_sh...  3.97 us
    pallas_call x8, Pallas kernels, last_visit(): pl.pallas_call(functools.partial(last_visit_kernel, begins), out_shape=ou...  3.1 us
  transfers between devices with their start and end apart: 32, of which 9 were waited for; matrix products, arithmetic and copies ran while one was open for 0% of the time, Pallas kernels for 7%

profile of v1, /device:TPU:37, one launch (start us, length us, event | category | flops | bytes accessed | tf_op | source)
XLA Modules:
  0.0 148.7 jit_solution(4488049233035414283)
XLA Ops:
  0.6 1.0 copy-done
  1.6 0.2 normalize.1
  1.8 20.5 %collective-permute-start.2 = (bf16[128,1024]{1,0:T(8,128)(2,1)S(1)}, bf16[128,1024]{1,0:T(8,128)(2,1)S(1)}, u32[]{:S(2)}, u32[]{:S(2)}) collective-permute-start(bf16[128,1024]{1,0:T(8,128)(2,1)S(1)} %get-tuple-element.38.refs_0_), channel_id=1, source_target_pairs={{0,1},{1,0},{2,3},{3,2},{4,5},{5,4},{6,7},{7,6},{8,9},{9,8},{10,11... | collective-permute-start | bytes 786440 | tf_op jit(solution)/shard_map/ppermute | solution.py:310
  22.3 0.1 collective-permute-start.3
  22.5 3.8 %collective-permute-start.4 = (bf16[128,1024]{1,0:T(8,128)(2,1)S(1)}, bf16[128,1024]{1,0:T(8,128)(2,1)S(1)}, u32[]{:S(2)}, u32[]{:S(2)}) collective-permute-start(bf16[128,1024]{1,0:T(8,128)(2,1)S(1)} %get-tuple-element.38.refs_0_), channel_id=1, source_target_pairs={{0,2},{1,63},{2,4},{3,1},{4,6},{5,3},{6,8},{7,5},{8,10},{9,7},{10,... | collective-permute-start | bytes 786440 | tf_op jit(solution)/shard_map/ppermute | solution.py:307
  26.3 0.1 lay.9
  26.4 1.3 collective-permute-start.5
  27.7 1.9 %collective-permute-done.4.refs_0_ = bf16[128,1024]{1,0:T(8,128)(2,1)S(1)} collective-permute-done((bf16[128,1024]{1,0:T(8,128)(2,1)S(1)}, bf16[128,1024]{1,0:T(8,128)(2,1)S(1)}, u32[]{:S(2)}, u32[]{:S(2)}) %collective-permute-start.4) | collective-permute-done | bytes 262176 | tf_op jit(solution)/shard_map/ppermute | solution.py:307
  29.6 3.1 %collective-permute-start.7 = (bf16[128,1024]{1,0:T(8,128)(2,1)S(1)}, bf16[128,1024]{1,0:T(8,128)(2,1)S(1)}, u32[]{:S(2)}, u32[]{:S(2)}) collective-permute-start(bf16[128,1024]{1,0:T(8,128)(2,1)S(1)} %collective-permute-done.4.refs_0_), channel_id=1, source_target_pairs={{0,2},{1,63},{2,4},{3,1},{4,6},{5,3},{6,8},{7,5},{8,10},{9,7},{10,... | collective-permute-start | bytes 786440 | tf_op jit(solution)/shard_map/ppermute | solution.py:307
  32.7 2.8 %collective-permute-start.8 = (bf16[128,1024]{1,0:T(8,128)(2,1)S(1)}, bf16[128,1024]{1,0:T(8,128)(2,1)S(1)}, u32[]{:S(2)}, u32[]{:S(2)}) collective-permute-start(bf16[128,1024]{1,0:T(8,128)(2,1)S(1)} %collective-permute-done.5.refs_1_), channel_id=1, source_target_pairs={{0,2},{1,63},{2,4},{3,1},{4,6},{5,3},{6,8},{7,5},{8,10},{9,7},{10,... | collective-permute-start | bytes 786440 | tf_op jit(solution)/shard_map/ppermute | solution.py:307
  35.7 0.1 columns.1.own_columns_ref.refs_4_.refs_3_
  35.8 1.1 front_visit.9
  36.8 2.0 %collective-permute-done.1.keys_ref.refs_0_ = s32[1,384]{1,0:T(1,128)S(1)} collective-permute-done((s32[1,384]{1,0:T(1,128)S(1)}, s32[1,384]{1,0:T(1,128)S(1)}, u32[]{:S(2)}, u32[]{:S(2)}) %collective-permute-start.1) | collective-permute-done | bytes 1568 | tf_op jit(solution)/shard_map/ppermute | solution.py:307
  38.8 0.4 last_visit.8
  39.2 3.3 %collective-permute-start.6 = (bf16[136,1024]{1,0:T(8,128)(2,1)S(1)}, bf16[136,1024]{1,0:T(8,128)(2,1)S(1)}, u32[]{:S(2)}, u32[]{:S(2)}) collective-permute-start(bf16[136,1024]{1,0:T(8,128)(2,1)S(1)} %last_visit.8), channel_id=1, source_target_pairs={{0,2},{1,63},{2,4},{3,1},{4,6},{5,3},{6,8},{7,5},{8,10},{9,7},{10,... | collective-permute-start | bytes 835592 | tf_op jit(solution)/shard_map/ppermute | solution.py:307
  42.5 0.1 collective-permute-start.10
  42.6 0.1 collective-permute-start.11
  42.8 0.4 front_visit.8
  43.2 2.8 %collective-permute-done.6.piece_ref.refs_2_ = bf16[136,1024]{1,0:T(8,128)(2,1)S(1)} collective-permute-done((bf16[136,1024]{1,0:T(8,128)(2,1)S(1)}, bf16[136,1024]{1,0:T(8,128)(2,1)S(1)}, u32[]{:S(2)}, u32[]{:S(2)}) %collective-permute-start.6) | collective-permute-done | bytes 278560 | tf_op jit(solution)/shard_map/ppermute | solution.py:307
  46.0 0.4 last_visit.9
  46.4 3.2 %collective-permute-start.9 = (bf16[136,1024]{1,0:T(8,128)(2,1)S(1)}, bf16[136,1024]{1,0:T(8,128)(2,1)S(1)}, u32[]{:S(2)}, u32[]{:S(2)}) collective-permute-start(bf16[136,1024]{1,0:T(8,128)(2,1)S(1)} %get-tuple-element.47), channel_id=1, source_target_pairs={{0,2},{1,63},{2,4},{3,1},{4,6},{5,3},{6,8},{7,5},{8,10},{9,7},{10,... | collective-permute-start | bytes 835592 | tf_op jit(solution)/shard_map/ppermute | solution.py:307
  49.6 2.3 %collective-permute-start.13 = (bf16[128,1024]{1,0:T(8,128)(2,1)S(1)}, bf16[128,1024]{1,0:T(8,128)(2,1)S(1)}, u32[]{:S(2)}, u32[]{:S(2)}) collective-permute-start(bf16[128,1024]{1,0:T(8,128)(2,1)S(1)} %collective-permute-done.10.refs_0_), channel_id=1, source_target_pairs={{0,2},{1,63},{2,4},{3,1},{4,6},{5,3},{6,8},{7,5},{8,10},{9,7},{10,... | collective-permute-start | bytes 786440 | tf_op jit(solution)/shard_map/ppermute | solution.py:307
  51.9 2.8 %collective-permute-start.14 = (bf16[128,1024]{1,0:T(8,128)(2,1)S(1)}, bf16[128,1024]{1,0:T(8,128)(2,1)S(1)}, u32[]{:S(2)}, u32[]{:S(2)}) collective-permute-start(bf16[128,1024]{1,0:T(8,128)(2,1)S(1)} %collective-permute-done.11.refs_1_), channel_id=1, source_target_pairs={{0,2},{1,63},{2,4},{3,1},{4,6},{5,3},{6,8},{7,5},{8,10},{9,7},{10,... | collective-permute-start | bytes 786440 | tf_op jit(solution)/shard_map/ppermute | solution.py:307
  54.7 0.4 front_visit.10
  55.1 0.4 last_visit.10
  55.5 2.7 %collective-permute-start.12 = (bf16[136,1024]{1,0:T(8,128)(2,1)S(1)}, bf16[136,1024]{1,0:T(8,128)(2,1)S(1)}, u32[]{:S(2)}, u32[]{:S(2)}) collective-permute-start(bf16[136,1024]{1,0:T(8,128)(2,1)S(1)} %get-tuple-element.50), channel_id=1, source_target_pairs={{0,2},{1,63},{2,4},{3,1},{4,6},{5,3},{6,8},{7,5},{8,10},{9,7},{10,... | collective-permute-start | bytes 835592 | tf_op jit(solution)/shard_map/ppermute | solution.py:307
  58.2 2.3 %collective-permute-start.16 = (bf16[128,1024]{1,0:T(8,128)(2,1)S(1)}, bf16[128,1024]{1,0:T(8,128)(2,1)S(1)}, u32[]{:S(2)}, u32[]{:S(2)}) collective-permute-start(bf16[128,1024]{1,0:T(8,128)(2,1)S(1)} %collective-permute-done.13.refs_0_), channel_id=1, source_target_pairs={{0,2},{1,63},{2,4},{3,1},{4,6},{5,3},{6,8},{7,5},{8,10},{9,7},{10,... | collective-permute-start | bytes 786440 | tf_op jit(solution)/shard_map/ppermute | solution.py:307
  60.5 2.8 %collective-permute-start.17 = (bf16[128,1024]{1,0:T(8,128)(2,1)S(1)}, bf16[128,1024]{1,0:T(8,128)(2,1)S(1)}, u32[]{:S(2)}, u32[]{:S(2)}) collective-permute-start(bf16[128,1024]{1,0:T(8,128)(2,1)S(1)} %collective-permute-done.14.refs_1_), channel_id=1, source_target_pairs={{0,2},{1,63},{2,4},{3,1},{4,6},{5,3},{6,8},{7,5},{8,10},{9,7},{10,... | collective-permute-start | bytes 786440 | tf_op jit(solution)/shard_map/ppermute | solution.py:307
  63.3 0.4 front_visit.11
  63.8 0.4 last_visit.11
  64.1 2.6 %collective-permute-start.15 = (bf16[136,1024]{1,0:T(8,128)(2,1)S(1)}, bf16[136,1024]{1,0:T(8,128)(2,1)S(1)}, u32[]{:S(2)}, u32[]{:S(2)}) collective-permute-start(bf16[136,1024]{1,0:T(8,128)(2,1)S(1)} %get-tuple-element.53), channel_id=1, source_target_pairs={{0,2},{1,63},{2,4},{3,1},{4,6},{5,3},{6,8},{7,5},{8,10},{9,7},{10,... | collective-permute-start | bytes 835592 | tf_op jit(solution)/shard_map/ppermute | solution.py:307
  66.8 2.3 %collective-permute-start.19 = (bf16[128,1024]{1,0:T(8,128)(2,1)S(1)}, bf16[128,1024]{1,0:T(8,128)(2,1)S(1)}, u32[]{:S(2)}, u32[]{:S(2)}) collective-permute-start(bf16[128,1024]{1,0:T(8,128)(2,1)S(1)} %collective-permute-done.16.refs_0_), channel_id=1, source_target_pairs={{0,2},{1,63},{2,4},{3,1},{4,6},{5,3},{6,8},{7,5},{8,10},{9,7},{10,... | collective-permute-start | bytes 786440 | tf_op jit(solution)/shard_map/ppermute | solution.py:307
  69.1 2.8 %collective-permute-start.20 = (bf16[128,1024]{1,0:T(8,128)(2,1)S(1)}, bf16[128,1024]{1,0:T(8,128)(2,1)S(1)}, u32[]{:S(2)}, u32[]{:S(2)}) collective-permute-start(bf16[128,1024]{1,0:T(8,128)(2,1)S(1)} %collective-permute-done.17.refs_1_), channel_id=1, source_target_pairs={{0,2},{1,63},{2,4},{3,1},{4,6},{5,3},{6,8},{7,5},{8,10},{9,7},{10,... | collective-permute-start | bytes 786440 | tf_op jit(solution)/shard_map/ppermute | solution.py:307
  71.9 0.4 front_visit.12
  72.3 0.4 last_visit.12
  72.7 2.7 %collective-permute-start.18 = (bf16[136,1024]{1,0:T(8,128)(2,1)S(1)}, bf16[136,1024]{1,0:T(8,128)(2,1)S(1)}, u32[]{:S(2)}, u32[]{:S(2)}) collective-permute-start(bf16[136,1024]{1,0:T(8,128)(2,1)S(1)} %get-tuple-element.56), channel_id=1, source_target_pairs={{0,2},{1,63},{2,4},{3,1},{4,6},{5,3},{6,8},{7,5},{8,10},{9,7},{10,... | collective-permute-start | bytes 835592 | tf_op jit(solution)/shard_map/ppermute | solution.py:307
  75.4 2.3 %collective-permute-start.22 = (bf16[128,1024]{1,0:T(8,128)(2,1)S(1)}, bf16[128,1024]{1,0:T(8,128)(2,1)S(1)}, u32[]{:S(2)}, u32[]{:S(2)}) collective-permute-start(bf16[128,1024]{1,0:T(8,128)(2,1)S(1)} %collective-permute-done.19.refs_0_), channel_id=1, source_target_pairs={{0,2},{1,63},{2,4},{3,1},{4,6},{5,3},{6,8},{7,5},{8,10},{9,7},{10,... | collective-permute-start | bytes 786440 | tf_op jit(solution)/shard_map/ppermute | solution.py:307
  77.7 2.8 %collective-permute-start.23 = (bf16[128,1024]{1,0:T(8,128)(2,1)S(1)}, bf16[128,1024]{1,0:T(8,128)(2,1)S(1)}, u32[]{:S(2)}, u32[]{:S(2)}) collective-permute-start(bf16[128,1024]{1,0:T(8,128)(2,1)S(1)} %collective-permute-done.20.refs_1_), channel_id=1, source_target_pairs={{0,2},{1,63},{2,4},{3,1},{4,6},{5,3},{6,8},{7,5},{8,10},{9,7},{10,... | collective-permute-start | bytes 786440 | tf_op jit(solution)/shard_map/ppermute | solution.py:307
  80.5 0.4 front_visit.13
  81.0 0.4 last_visit.13
  81.3 2.7 %collective-permute-start.21 = (bf16[136,1024]{1,0:T(8,128)(2,1)S(1)}, bf16[136,1024]{1,0:T(8,128)(2,1)S(1)}, u32[]{:S(2)}, u32[]{:S(2)}) collective-permute-start(bf16[136,1024]{1,0:T(8,128)(2,1)S(1)} %get-tuple-element.59), channel_id=1, source_target_pairs={{0,2},{1,63},{2,4},{3,1},{4,6},{5,3},{6,8},{7,5},{8,10},{9,7},{10,... | collective-permute-start | bytes 835592 | tf_op jit(solution)/shard_map/ppermute | solution.py:307
  84.0 3.7 %collective-permute-start.27 = (bf16[128,1024]{1,0:T(8,128)(2,1)S(1)}, bf16[128,1024]{1,0:T(8,128)(2,1)S(1)}, u32[]{:S(2)}, u32[]{:S(2)}) collective-permute-start(bf16[128,1024]{1,0:T(8,128)(2,1)S(1)} %collective-permute-done.22.refs_0_), channel_id=1, source_target_pairs={{0,3},{1,62},{2,5},{3,0},{4,7},{5,2},{6,9},{7,4},{8,11},{9,6},{10,... | collective-permute-start | bytes 786440 | tf_op jit(solution)/shard_map/ppermute | solution.py:307
  87.7 1.5 collective-permute-start.28
  89.2 0.4 front_visit.14
  89.6 0.4 last_visit.14
  90.0 2.8 %collective-permute-start.24 = (bf16[136,1024]{1,0:T(8,128)(2,1)S(1)}, bf16[136,1024]{1,0:T(8,128)(2,1)S(1)}, u32[]{:S(2)}, u32[]{:S(2)}) collective-permute-start(bf16[136,1024]{1,0:T(8,128)(2,1)S(1)} %get-tuple-element.62), channel_id=1, source_target_pairs={{0,2},{1,63},{2,4},{3,1},{4,6},{5,3},{6,8},{7,5},{8,10},{9,7},{10,... | collective-permute-start | bytes 835592 | tf_op jit(solution)/shard_map/ppermute | solution.py:307
  92.8 2.3 %collective-permute-done.27.refs_0_.refs_1_ = bf16[128,1024]{1,0:T(8,128)(2,1)S(1)} collective-permute-done((bf16[128,1024]{1,0:T(8,128)(2,1)S(1)}, bf16[128,1024]{1,0:T(8,128)(2,1)S(1)}, u32[]{:S(2)}, u32[]{:S(2)}) %collective-permute-start.27) | collective-permute-done | bytes 262176 | tf_op jit(solution)/shard_map/ppermute | solution.py:307
  95.1 2.8 %collective-permute-done.28.refs_1_.refs_2_ = bf16[128,1024]{1,0:T(8,128)(2,1)S(1)} collective-permute-done((bf16[128,1024]{1,0:T(8,128)(2,1)S(1)}, bf16[128,1024]{1,0:T(8,128)(2,1)S(1)}, u32[]{:S(2)}, u32[]{:S(2)}) %collective-permute-start.28) | collective-permute-done | bytes 262176 | tf_op jit(solution)/shard_map/ppermute | solution.py:307
  97.9 0.1 collective-permute-start.29
  98.1 0.4 front_visit.15
  98.5 0.4 last_visit.15
  98.9 2.4 %collective-permute-start.26 = (bf16[136,1024]{1,0:T(8,128)(2,1)S(1)}, bf16[136,1024]{1,0:T(8,128)(2,1)S(1)}, u32[]{:S(2)}, u32[]{:S(2)}) collective-permute-start(bf16[136,1024]{1,0:T(8,128)(2,1)S(1)} %get-tuple-element.64), channel_id=1, source_target_pairs={{0,3},{1,62},{2,5},{3,0},{4,7},{5,2},{6,9},{7,4},{8,11},{9,6},{10,... | collective-permute-start | bytes 835592 | tf_op jit(solution)/shard_map/ppermute | solution.py:307
  101.3 0.9 collective-permute-start.25
  102.6 0.4 collective-permute-done.25.refs_0_
  103.0 2.0 %meet.3.refs_20_ = f32[1,256]{1,0:T(1,128)S(1)} custom-call(s32[1,384]{1,0:T(1,128)S(1)} %collective-permute-done.25.refs_0_, bf16[128,1024]{1,0:T(8,128)(2,1)S(1)} %collective-permute-done.27.refs_0_.refs_1_, bf16[128,1024]{1,0:T(8,128)(2,1)S(1)} %collective-permute-done.28.refs_1_.refs_2_, bf16[384,1024]{1,0:T(8,128)(2,1)S(1)} %get-tuple-element.40.own_ref.refs_3_.refs_2_, ...), custom_call_target="tpu_custom_call" | custom-call | flops 1610612736 | bytes 6815744 | tf_op jit(solution)/shard_map/meet/pallas_call | solution.py:232
  105.1 0.3 meet.4.refs_21_
  105.4 0.8 collective-permute-done.26.refs_1_
  106.2 2.6 %meet.5 = f32[32,1,384]{2,1,0:T(1,128)} custom-call(s32[1,384]{1,0:T(1,128)S(1)} %collective-permute-done.25.refs_0_, bf16[136,1024]{1,0:T(8,128)(2,1)S(1)} %collective-permute-done.26.refs_1_, bf16[384,1024]{1,0:T(8,128)(2,1)S(1)} %get-tuple-element.40.own_ref.refs_3_.refs_2_, s32[384,128]{1,0:T(8,128)S(1)} %columns.1.own_columns_ref.refs_4_.refs_3_, ...), custom_call_target="tpu_custom_call" | custom-call | flops 909115392 | bytes 6963200 | tf_op jit(solution)/shard_map/meet/pallas_call | solution.py:232
  108.7 12.9 %all-to-all-start = ((f32[32,1,384]{2,1,0:T(1,128)}), f32[32,1,384]{2,1,0:T(1,128)S(1)}, u32[]{:S(2)}, u32[]{:S(2)}) async-start(f32[32,1,384]{2,1,0:T(1,128)} %meet.5), calls=%async_computation | async-start | bytes 98304 | tf_op jit(solution)/shard_map/all_to_all | solution.py:342
  121.6 22.0 %all-to-all-done = f32[32,1,384]{2,1,0:T(1,128)S(1)} async-done(((f32[32,1,384]{2,1,0:T(1,128)}), f32[32,1,384]{2,1,0:T(1,128)S(1)}, u32[]{:S(2)}, u32[]{:S(2)}) %all-to-all-start) | async-done | bytes 49184 | tf_op jit(solution)/shard_map/all_to_all | solution.py:342
  143.7 2.9 %collective-permute-start.30 = (f32[32,384]{1,0:T(8,128)S(1)}, f32[32,384]{1,0:T(8,128)S(1)}, u32[]{:S(2)}, u32[]{:S(2)}) collective-permute-start(f32[32,384]{1,0:T(8,128)S(1)} %bitcast.8), channel_id=1, source_target_pairs={{0,1},{1,0},{2,3},{3,2},{4,5},{5,4},{6,7},{7,6},{8,9},{9,8},{10,11... | collective-permute-start | bytes 147464 | tf_op jit(solution)/shard_map/ppermute | solution.py:310
  146.6 0.1 pad_add_fusion.1.place_ref
  147.3 0.2 collective-permute-done.30.theirs_ref
  147.4 1.2 finish.1
  (38 shorter events, 0.6 us)
Async XLA Ops:
  0.6 1.0 copy-start
  1.8 24.5 %collective-permute-start.2 = (bf16[128,1024]{1,0:T(8,128)(2,1)S(1)}, bf16[128,1024]{1,0:T(8,128)(2,1)S(1)}, u32[]{:S(2)}, u32[]{:S(2)}) collective-permute-start(bf16[128,1024]{1,0:T(8,128)(2,1)S(1)} %get-tuple-element.38.refs_0_), channel_id=1, source_target_pairs={{0,1},{1,0},{2,3},{3,2},{4,5},{5,4},{6,7},{7,6},{8,9},{9,8},{10,11... | collective-permute-start | bytes 786440 | tf_op jit(solution)/shard_map/ppermute | solution.py:310
  22.3 3.9 %collective-permute-start.3 = (bf16[64,1024]{1,0:T(8,128)(2,1)S(1)}, bf16[64,1024]{1,0:T(8,128)(2,1)S(1)}, u32[]{:S(2)}, u32[]{:S(2)}) collective-permute-start(bf16[64,1024]{1,0:T(8,128)(2,1)S(1)} %get-tuple-element.39.refs_1_), channel_id=1, source_target_pairs={{0,1},{1,0},{2,3},{3,2},{4,5},{5,4},{6,7},{7,6},{8,9},{9,8},{10,11... | collective-permute-start | bytes 393224 | tf_op jit(solution)/shard_map/ppermute | solution.py:310
  22.5 7.1 %collective-permute-start.4 = (bf16[128,1024]{1,0:T(8,128)(2,1)S(1)}, bf16[128,1024]{1,0:T(8,128)(2,1)S(1)}, u32[]{:S(2)}, u32[]{:S(2)}) collective-permute-start(bf16[128,1024]{1,0:T(8,128)(2,1)S(1)} %get-tuple-element.38.refs_0_), channel_id=1, source_target_pairs={{0,2},{1,63},{2,4},{3,1},{4,6},{5,3},{6,8},{7,5},{8,10},{9,7},{10,... | collective-permute-start | bytes 786440 | tf_op jit(solution)/shard_map/ppermute | solution.py:307
  26.4 1.3 copy-start.1
  26.4 6.3 %collective-permute-start.5 = (bf16[128,1024]{1,0:T(8,128)(2,1)S(1)}, bf16[128,1024]{1,0:T(8,128)(2,1)S(1)}, u32[]{:S(2)}, u32[]{:S(2)}) collective-permute-start(bf16[128,1024]{1,0:T(8,128)(2,1)S(1)} %get-tuple-element.41.refs_1_), channel_id=1, source_target_pairs={{0,2},{1,63},{2,4},{3,1},{4,6},{5,3},{6,8},{7,5},{8,10},{9,7},{10,... | collective-permute-start | bytes 786440 | tf_op jit(solution)/shard_map/ppermute | solution.py:307
  27.7 7.8 %collective-permute-start = (s32[1,192]{1,0:T(1,128)S(1)}, s32[1,192]{1,0:T(1,128)S(1)}, u32[]{:S(2)}, u32[]{:S(2)}) collective-permute-start(s32[1,192]{1,0:T(1,128)S(1)} %bitcast.10), channel_id=1, source_target_pairs={{0,1},{1,0},{2,3},{3,2},{4,5},{5,4},{6,7},{7,6},{8,9},{9,8},{10,11... | collective-permute-start | bytes 2312 | tf_op jit(solution)/shard_map/ppermute | solution.py:310
  29.6 12.9 %collective-permute-start.7 = (bf16[128,1024]{1,0:T(8,128)(2,1)S(1)}, bf16[128,1024]{1,0:T(8,128)(2,1)S(1)}, u32[]{:S(2)}, u32[]{:S(2)}) collective-permute-start(bf16[128,1024]{1,0:T(8,128)(2,1)S(1)} %collective-permute-done.4.refs_0_), channel_id=1, source_target_pairs={{0,2},{1,63},{2,4},{3,1},{4,6},{5,3},{6,8},{7,5},{8,10},{9,7},{10,... | collective-permute-start | bytes 786440 | tf_op jit(solution)/shard_map/ppermute | solution.py:307
  32.7 9.9 %collective-permute-start.8 = (bf16[128,1024]{1,0:T(8,128)(2,1)S(1)}, bf16[128,1024]{1,0:T(8,128)(2,1)S(1)}, u32[]{:S(2)}, u32[]{:S(2)}) collective-permute-start(bf16[128,1024]{1,0:T(8,128)(2,1)S(1)} %collective-permute-done.5.refs_1_), channel_id=1, source_target_pairs={{0,2},{1,63},{2,4},{3,1},{4,6},{5,3},{6,8},{7,5},{8,10},{9,7},{10,... | collective-permute-start | bytes 786440 | tf_op jit(solution)/shard_map/ppermute | solution.py:307
  35.6 3.3 %collective-permute-start.1 = (s32[1,384]{1,0:T(1,128)S(1)}, s32[1,384]{1,0:T(1,128)S(1)}, u32[]{:S(2)}, u32[]{:S(2)}) collective-permute-start(s32[1,384]{1,0:T(1,128)S(1)} %pad_add_fusion.keys_ref), channel_id=1, source_target_pairs={{0,2},{1,63},{2,4},{3,1},{4,6},{5,3},{6,8},{7,5},{8,10},{9,7},{10,... | collective-permute-start | bytes 4616 | tf_op jit(solution)/shard_map/ppermute | solution.py:307
  39.2 6.8 %collective-permute-start.6 = (bf16[136,1024]{1,0:T(8,128)(2,1)S(1)}, bf16[136,1024]{1,0:T(8,128)(2,1)S(1)}, u32[]{:S(2)}, u32[]{:S(2)}) collective-permute-start(bf16[136,1024]{1,0:T(8,128)(2,1)S(1)} %last_visit.8), channel_id=1, source_target_pairs={{0,2},{1,63},{2,4},{3,1},{4,6},{5,3},{6,8},{7,5},{8,10},{9,7},{10,... | collective-permute-start | bytes 835592 | tf_op jit(solution)/shard_map/ppermute | solution.py:307
  42.5 7.1 %collective-permute-start.10 = (bf16[128,1024]{1,0:T(8,128)(2,1)S(1)}, bf16[128,1024]{1,0:T(8,128)(2,1)S(1)}, u32[]{:S(2)}, u32[]{:S(2)}) collective-permute-start(bf16[128,1024]{1,0:T(8,128)(2,1)S(1)} %collective-permute-done.7.refs_0_), channel_id=1, source_target_pairs={{0,2},{1,63},{2,4},{3,1},{4,6},{5,3},{6,8},{7,5},{8,10},{9,7},{10,... | collective-permute-start | bytes 786440 | tf_op jit(solution)/shard_map/ppermute | solution.py:307
  42.6 9.3 %collective-permute-start.11 = (bf16[128,1024]{1,0:T(8,128)(2,1)S(1)}, bf16[128,1024]{1,0:T(8,128)(2,1)S(1)}, u32[]{:S(2)}, u32[]{:S(2)}) collective-permute-start(bf16[128,1024]{1,0:T(8,128)(2,1)S(1)} %collective-permute-done.8.refs_1_), channel_id=1, source_target_pairs={{0,2},{1,63},{2,4},{3,1},{4,6},{5,3},{6,8},{7,5},{8,10},{9,7},{10,... | collective-permute-start | bytes 786440 | tf_op jit(solution)/shard_map/ppermute | solution.py:307
  46.4 8.8 %collective-permute-start.9 = (bf16[136,1024]{1,0:T(8,128)(2,1)S(1)}, bf16[136,1024]{1,0:T(8,128)(2,1)S(1)}, u32[]{:S(2)}, u32[]{:S(2)}) collective-permute-start(bf16[136,1024]{1,0:T(8,128)(2,1)S(1)} %get-tuple-element.47), channel_id=1, source_target_pairs={{0,2},{1,63},{2,4},{3,1},{4,6},{5,3},{6,8},{7,5},{8,10},{9,7},{10,... | collective-permute-start | bytes 835592 | tf_op jit(solution)/shard_map/ppermute | solution.py:307
  49.6 8.6 %collective-permute-start.13 = (bf16[128,1024]{1,0:T(8,128)(2,1)S(1)}, bf16[128,1024]{1,0:T(8,128)(2,1)S(1)}, u32[]{:S(2)}, u32[]{:S(2)}) collective-permute-start(bf16[128,1024]{1,0:T(8,128)(2,1)S(1)} %collective-permute-done.10.refs_0_), channel_id=1, source_target_pairs={{0,2},{1,63},{2,4},{3,1},{4,6},{5,3},{6,8},{7,5},{8,10},{9,7},{10,... | collective-permute-start | bytes 786440 | tf_op jit(solution)/shard_map/ppermute | solution.py:307
  51.9 8.6 %collective-permute-start.14 = (bf16[128,1024]{1,0:T(8,128)(2,1)S(1)}, bf16[128,1024]{1,0:T(8,128)(2,1)S(1)}, u32[]{:S(2)}, u32[]{:S(2)}) collective-permute-start(bf16[128,1024]{1,0:T(8,128)(2,1)S(1)} %collective-permute-done.11.refs_1_), channel_id=1, source_target_pairs={{0,2},{1,63},{2,4},{3,1},{4,6},{5,3},{6,8},{7,5},{8,10},{9,7},{10,... | collective-permute-start | bytes 786440 | tf_op jit(solution)/shard_map/ppermute | solution.py:307
  55.5 8.2 %collective-permute-start.12 = (bf16[136,1024]{1,0:T(8,128)(2,1)S(1)}, bf16[136,1024]{1,0:T(8,128)(2,1)S(1)}, u32[]{:S(2)}, u32[]{:S(2)}) collective-permute-start(bf16[136,1024]{1,0:T(8,128)(2,1)S(1)} %get-tuple-element.50), channel_id=1, source_target_pairs={{0,2},{1,63},{2,4},{3,1},{4,6},{5,3},{6,8},{7,5},{8,10},{9,7},{10,... | collective-permute-start | bytes 835592 | tf_op jit(solution)/shard_map/ppermute | solution.py:307
  58.2 8.6 %collective-permute-start.16 = (bf16[128,1024]{1,0:T(8,128)(2,1)S(1)}, bf16[128,1024]{1,0:T(8,128)(2,1)S(1)}, u32[]{:S(2)}, u32[]{:S(2)}) collective-permute-start(bf16[128,1024]{1,0:T(8,128)(2,1)S(1)} %collective-permute-done.13.refs_0_), channel_id=1, source_target_pairs={{0,2},{1,63},{2,4},{3,1},{4,6},{5,3},{6,8},{7,5},{8,10},{9,7},{10,... | collective-permute-start | bytes 786440 | tf_op jit(solution)/shard_map/ppermute | solution.py:307
  60.5 8.6 %collective-permute-start.17 = (bf16[128,1024]{1,0:T(8,128)(2,1)S(1)}, bf16[128,1024]{1,0:T(8,128)(2,1)S(1)}, u32[]{:S(2)}, u32[]{:S(2)}) collective-permute-start(bf16[128,1024]{1,0:T(8,128)(2,1)S(1)} %collective-permute-done.14.refs_1_), channel_id=1, source_target_pairs={{0,2},{1,63},{2,4},{3,1},{4,6},{5,3},{6,8},{7,5},{8,10},{9,7},{10,... | collective-permute-start | bytes 786440 | tf_op jit(solution)/shard_map/ppermute | solution.py:307
  64.1 8.2 %collective-permute-start.15 = (bf16[136,1024]{1,0:T(8,128)(2,1)S(1)}, bf16[136,1024]{1,0:T(8,128)(2,1)S(1)}, u32[]{:S(2)}, u32[]{:S(2)}) collective-permute-start(bf16[136,1024]{1,0:T(8,128)(2,1)S(1)} %get-tuple-element.53), channel_id=1, source_target_pairs={{0,2},{1,63},{2,4},{3,1},{4,6},{5,3},{6,8},{7,5},{8,10},{9,7},{10,... | collective-permute-start | bytes 835592 | tf_op jit(solution)/shard_map/ppermute | solution.py:307
  66.8 8.6 %collective-permute-start.19 = (bf16[128,1024]{1,0:T(8,128)(2,1)S(1)}, bf16[128,1024]{1,0:T(8,128)(2,1)S(1)}, u32[]{:S(2)}, u32[]{:S(2)}) collective-permute-start(bf16[128,1024]{1,0:T(8,128)(2,1)S(1)} %collective-permute-done.16.refs_0_), channel_id=1, source_target_pairs={{0,2},{1,63},{2,4},{3,1},{4,6},{5,3},{6,8},{7,5},{8,10},{9,7},{10,... | collective-permute-start | bytes 786440 | tf_op jit(solution)/shard_map/ppermute | solution.py:307
  69.1 8.6 %collective-permute-start.20 = (bf16[128,1024]{1,0:T(8,128)(2,1)S(1)}, bf16[128,1024]{1,0:T(8,128)(2,1)S(1)}, u32[]{:S(2)}, u32[]{:S(2)}) collective-permute-start(bf16[128,1024]{1,0:T(8,128)(2,1)S(1)} %collective-permute-done.17.refs_1_), channel_id=1, source_target_pairs={{0,2},{1,63},{2,4},{3,1},{4,6},{5,3},{6,8},{7,5},{8,10},{9,7},{10,... | collective-permute-start | bytes 786440 | tf_op jit(solution)/shard_map/ppermute | solution.py:307
  72.7 8.2 %collective-permute-start.18 = (bf16[136,1024]{1,0:T(8,128)(2,1)S(1)}, bf16[136,1024]{1,0:T(8,128)(2,1)S(1)}, u32[]{:S(2)}, u32[]{:S(2)}) collective-permute-start(bf16[136,1024]{1,0:T(8,128)(2,1)S(1)} %get-tuple-element.56), channel_id=1, source_target_pairs={{0,2},{1,63},{2,4},{3,1},{4,6},{5,3},{6,8},{7,5},{8,10},{9,7},{10,... | collective-permute-start | bytes 835592 | tf_op jit(solution)/shard_map/ppermute | solution.py:307
  75.4 8.6 %collective-permute-start.22 = (bf16[128,1024]{1,0:T(8,128)(2,1)S(1)}, bf16[128,1024]{1,0:T(8,128)(2,1)S(1)}, u32[]{:S(2)}, u32[]{:S(2)}) collective-permute-start(bf16[128,1024]{1,0:T(8,128)(2,1)S(1)} %collective-permute-done.19.refs_0_), channel_id=1, source_target_pairs={{0,2},{1,63},{2,4},{3,1},{4,6},{5,3},{6,8},{7,5},{8,10},{9,7},{10,... | collective-permute-start | bytes 786440 | tf_op jit(solution)/shard_map/ppermute | solution.py:307
  77.7 10.0 %collective-permute-start.23 = (bf16[128,1024]{1,0:T(8,128)(2,1)S(1)}, bf16[128,1024]{1,0:T(8,128)(2,1)S(1)}, u32[]{:S(2)}, u32[]{:S(2)}) collective-permute-start(bf16[128,1024]{1,0:T(8,128)(2,1)S(1)} %collective-permute-done.20.refs_1_), channel_id=1, source_target_pairs={{0,2},{1,63},{2,4},{3,1},{4,6},{5,3},{6,8},{7,5},{8,10},{9,7},{10,... | collective-permute-start | bytes 786440 | tf_op jit(solution)/shard_map/ppermute | solution.py:307
  81.3 8.3 %collective-permute-start.21 = (bf16[136,1024]{1,0:T(8,128)(2,1)S(1)}, bf16[136,1024]{1,0:T(8,128)(2,1)S(1)}, u32[]{:S(2)}, u32[]{:S(2)}) collective-permute-start(bf16[136,1024]{1,0:T(8,128)(2,1)S(1)} %get-tuple-element.59), channel_id=1, source_target_pairs={{0,2},{1,63},{2,4},{3,1},{4,6},{5,3},{6,8},{7,5},{8,10},{9,7},{10,... | collective-permute-start | bytes 835592 | tf_op jit(solution)/shard_map/ppermute | solution.py:307
  84.0 11.1 %collective-permute-start.27 = (bf16[128,1024]{1,0:T(8,128)(2,1)S(1)}, bf16[128,1024]{1,0:T(8,128)(2,1)S(1)}, u32[]{:S(2)}, u32[]{:S(2)}) collective-permute-start(bf16[128,1024]{1,0:T(8,128)(2,1)S(1)} %collective-permute-done.22.refs_0_), channel_id=1, source_target_pairs={{0,3},{1,62},{2,5},{3,0},{4,7},{5,2},{6,9},{7,4},{8,11},{9,6},{10,... | collective-permute-start | bytes 786440 | tf_op jit(solution)/shard_map/ppermute | solution.py:307
  87.7 10.2 %collective-permute-start.28 = (bf16[128,1024]{1,0:T(8,128)(2,1)S(1)}, bf16[128,1024]{1,0:T(8,128)(2,1)S(1)}, u32[]{:S(2)}, u32[]{:S(2)}) collective-permute-start(bf16[128,1024]{1,0:T(8,128)(2,1)S(1)} %collective-permute-done.23.refs_1_), channel_id=1, source_target_pairs={{0,3},{1,62},{2,5},{3,0},{4,7},{5,2},{6,9},{7,4},{8,11},{9,6},{10,... | collective-permute-start | bytes 786440 | tf_op jit(solution)/shard_map/ppermute | solution.py:307
  90.0 8.5 %collective-permute-start.24 = (bf16[136,1024]{1,0:T(8,128)(2,1)S(1)}, bf16[136,1024]{1,0:T(8,128)(2,1)S(1)}, u32[]{:S(2)}, u32[]{:S(2)}) collective-permute-start(bf16[136,1024]{1,0:T(8,128)(2,1)S(1)} %get-tuple-element.62), channel_id=1, source_target_pairs={{0,2},{1,63},{2,4},{3,1},{4,6},{5,3},{6,8},{7,5},{8,10},{9,7},{10,... | collective-permute-start | bytes 835592 | tf_op jit(solution)/shard_map/ppermute | solution.py:307
  97.9 7.2 %collective-permute-start.29 = (bf16[192,1024]{1,0:T(8,128)(2,1)S(1)}, bf16[192,1024]{1,0:T(8,128)(2,1)S(1)}, u32[]{:S(2)}, u32[]{:S(2)}) collective-permute-start(bf16[192,1024]{1,0:T(8,128)(2,1)S(1)} %lay.17), channel_id=1, source_target_pairs={{0,1},{1,0},{2,3},{3,2},{4,5},{5,4},{6,7},{7,6},{8,9},{9,8},{10,11... | collective-permute-start | bytes 1179656 | tf_op jit(solution)/shard_map/ppermute | solution.py:310
  98.9 7.3 %collective-permute-start.26 = (bf16[136,1024]{1,0:T(8,128)(2,1)S(1)}, bf16[136,1024]{1,0:T(8,128)(2,1)S(1)}, u32[]{:S(2)}, u32[]{:S(2)}) collective-permute-start(bf16[136,1024]{1,0:T(8,128)(2,1)S(1)} %get-tuple-element.64), channel_id=1, source_target_pairs={{0,3},{1,62},{2,5},{3,0},{4,7},{5,2},{6,9},{7,4},{8,11},{9,6},{10,... | collective-permute-start | bytes 835592 | tf_op jit(solution)/shard_map/ppermute | solution.py:307
  101.3 1.8 %collective-permute-start.25 = (s32[1,384]{1,0:T(1,128)S(1)}, s32[1,384]{1,0:T(1,128)S(1)}, u32[]{:S(2)}, u32[]{:S(2)}) collective-permute-start(s32[1,384]{1,0:T(1,128)S(1)} %get-tuple-element.63.refs_3_.refs_18_), channel_id=1, source_target_pairs={{0,1},{1,0},{2,3},{3,2},{4,5},{5,4},{6,7},{7,6},{8,9},{9,8},{10,11... | collective-permute-start | bytes 4616 | tf_op jit(solution)/shard_map/ppermute | solution.py:310
  108.7 34.9 %all-to-all-start = ((f32[32,1,384]{2,1,0:T(1,128)}), f32[32,1,384]{2,1,0:T(1,128)S(1)}, u32[]{:S(2)}, u32[]{:S(2)}) async-start(f32[32,1,384]{2,1,0:T(1,128)} %meet.5), calls=%async_computation | async-start | bytes 98304 | tf_op jit(solution)/shard_map/all_to_all | solution.py:342
  143.7 3.8 %collective-permute-start.30 = (f32[32,384]{1,0:T(8,128)S(1)}, f32[32,384]{1,0:T(8,128)S(1)}, u32[]{:S(2)}, u32[]{:S(2)}) collective-permute-start(f32[32,384]{1,0:T(8,128)S(1)} %bitcast.8), channel_id=1, source_target_pairs={{0,1},{1,0},{2,3},{3,2},{4,5},{5,4},{6,7},{7,6},{8,9},{9,8},{10,11... | collective-permute-start | bytes 147464 | tf_op jit(solution)/shard_map/ppermute | solution.py:310

commit v2 on v1

--- a/solution.py
+++ b/solution.py
@@ -79,8 +79,11 @@
     return jnp.maximum(best, jnp.max(masked, axis=0, keepdims=True))
 
 
-def lay_kernel(count, starts, *refs):
+def lay_kernel(count, starts, keyed, *refs):
     first = 0
+    if keyed:
+        refs[-1][...] = key_columns(refs[count][...])
+        refs = refs[:count] + refs[count + 1 : -1]
     for ref in refs[:count]:
         end = first + ref.shape[0]
         for start, out in zip(starts, refs[count:]):
@@ -90,85 +93,49 @@
         first = end
 
 
-def lay(pieces, cuts):
+def lay(pieces, cuts, keys=()):
     width = pieces[0].shape[1]
     total = sum(end - start for start, end in cuts)
     return pl.pallas_call(
-        functools.partial(lay_kernel, len(pieces), [start for start, _ in cuts]),
-        out_shape=[jax.ShapeDtypeStruct((end - start, width), jnp.bfloat16) for start, end in cuts],
-        in_specs=[VMEM] * len(pieces),
-        out_specs=[VMEM] * len(cuts),
+        functools.partial(lay_kernel, len(pieces), [start for start, _ in cuts], bool(keys)),
+        out_shape=[jax.ShapeDtypeStruct((end - start, width), jnp.bfloat16) for start, end in cuts]
+        + [jax.ShapeDtypeStruct((k.shape[1], 128), jnp.int32) for k in keys],
+        in_specs=[VMEM] * (len(pieces) + len(keys)),
+        out_specs=[VMEM] * (len(cuts) + len(keys)),
         compiler_params=PARAMS,
         cost_estimate=pl.CostEstimate(
             flops=total, bytes_accessed=4 * total * width, transcendentals=0
         ),
         name="lay",
-    )(*pieces)
-
-
-def front_visit_kernel(pieces, keys_ref, own_ref, own_columns_ref, *refs):
-    best_ref, columns_ref = refs[-2:]
-    keys = keys_ref[...]
-    columns_ref[...] = key_columns(keys)
-    rows = jnp.concatenate([r[...] for r in refs[:pieces]], axis=0)
-    count = rows.shape[0]
-    row_key = keys[:, :count]
-    low = row_key & jnp.int32(-label_stride)
-    start = jnp.full(best_ref.shape, -1.0, jnp.float32)
-    best_ref[...] = best_of(start, row_key, low, rows, own_ref[...], own_columns_ref[...])
-
-
-def front_visit(keys, own, pieces):
+    )(*pieces, *keys)
+
+
+def visit_kernel(begins, pieces, own_ref, own_columns_ref, *refs):
+    piece_refs, out_ref = refs[:pieces], refs[-1]
+    count = out_ref.shape[0] - TAIL
+    last = piece_refs[-1][:count, :]
+    rows = jnp.concatenate([*[r[...] for r in piece_refs[:-1]], last], axis=0)
+    acc = jnp.full((1, rows.shape[0]), -1.0, jnp.float32)
+    if begins:
+        keys = refs[pieces][...]
+    else:
+        keys, acc = read_tail(piece_refs[-1], rows.shape[0])
+        refs[pieces][...] = keys
+    low = keys & jnp.int32(-label_stride)
+    acc = best_of(acc, keys, low, rows, own_ref[...], own_columns_ref[...])
+    out_ref[:count, :] = last
+    write_tail(out_ref, keys, acc)
+
+
+def visit(own, pieces, keys=None):
+    begins = keys is not None
     total, width = own[0].shape
-    count = sum(p.shape[0] for p in pieces)
-    operands = [keys, *own, *pieces]
-    return pl.pallas_call(
-        functools.partial(front_visit_kernel, len(pieces)),
-        out_shape=[
-            jax.ShapeDtypeStruct((1, count), jnp.float32),
-            jax.ShapeDtypeStruct((total, 128), jnp.int32),
-        ],
-        in_specs=[VMEM] * len(operands),
-        out_specs=[VMEM] * 2,
-        compiler_params=PARAMS,
-        cost_estimate=pl.CostEstimate(
-            flops=total, bytes_accessed=4 * total * width, transcendentals=0
-        ),
-        name="front_visit",
-    )(*operands)
-
-
-def last_visit_kernel(begins, keys_ref, own_ref, own_columns_ref, front_ref, piece_ref, *refs):
-    if begins:
-        next_ref, out_ref = refs
-        earlier, next_keys = None, next_ref[...]
-    else:
-        next_out_ref, out_ref = refs
-        next_keys, earlier = read_tail(piece_ref, keys_ref.shape[1])
-        next_out_ref[...] = next_keys
-    keys = keys_ref[...]
-    count = out_ref.shape[0] - TAIL
-    rows = piece_ref[:count, :]
-    row_key = keys[:, keys.shape[1] - count :]
-    low = row_key & jnp.int32(-label_stride)
-    start = jnp.full((1, count), -1.0, jnp.float32)
-    best = best_of(start, row_key, low, rows, own_ref[...], own_columns_ref[...])
-    acc = jnp.concatenate([front_ref[...], best], axis=1)
-    if earlier is not None:
-        acc = jnp.maximum(acc, earlier)
-    out_ref[:count, :] = rows
-    write_tail(out_ref, next_keys, acc)
-
-
-def last_visit(keys, own, front, piece, next_keys=None):
-    begins = next_keys is not None
-    total, width = own[0].shape
-    rows = piece.shape[0] + (TAIL if begins else 0)
-    operands = [keys, *own, front, piece] + ([next_keys] if begins else [])
-    out_shape = [] if begins else [jax.ShapeDtypeStruct(keys.shape, jnp.int32)]
+    rows = pieces[-1].shape[0] + (TAIL if begins else 0)
+    operands = [*own, *pieces] + ([keys] if begins else [])
+    out_shape = [] if begins else [jax.ShapeDtypeStruct((1, total), jnp.int32)]
     out_shape.append(jax.ShapeDtypeStruct((rows, width), jnp.bfloat16))
     return pl.pallas_call(
-        functools.partial(last_visit_kernel, begins),
+        functools.partial(visit_kernel, begins, len(pieces)),
         out_shape=out_shape,
         in_specs=[VMEM] * len(operands),
         out_specs=[VMEM] * len(out_shape),
@@ -176,7 +143,7 @@
         cost_estimate=pl.CostEstimate(
             flops=total, bytes_accessed=4 * total * width, transcendentals=0
         ),
-        name="last_visit",
+        name="visit",
     )(*operands)
 
 
@@ -314,24 +281,21 @@
     cuts = [(n * size, (n + 1) * size) for n in range(PIECES)]
     keys = member_key.reshape(1, rows)
     keys = jnp.concatenate([keys, across(keys)], axis=1)
-    next_keys = send(keys, 1)
     mine = normalize(embeddings, (size, rows - size))
     theirs = [across(m) for m in mine]
-    *rest, whole = lay([*mine, *theirs], [*cuts[1:], (0, total)])
-    block = [mine[0], *rest]
+    (second,) = lay([mine[1], theirs[0]], [(0, size)])
+    *rest, whole = lay([*mine, *theirs], [*cuts[2:], (0, total)])
+    block = [mine[0], second, *rest]
     own = (whole, columns_of(keys))
     held = [own]
-    best, _ = front_visit(keys, own, block[:-1])
-    (block[-1],) = last_visit(keys, own, best, block[-1], next_keys)
+    (block[-1],) = visit(own, block, keys)
     for _ in range(1, hops):
-        keys = next_keys
         block = [send(b, 1) for b in block]
-        best, columns = front_visit(keys, own, block[:-1])
-        next_keys, last = last_visit(keys, own, best, block[-1])
-        (whole,) = lay(block, [(0, total)])
-        held.append((whole, columns))
+        keys, last = visit(own, block)
+        held.append(lay(block, [(0, total)], [keys]))
         block[-1] = last
-    last_keys = across(next_keys)
+    last_keys = send(keys, 1, True)
+    next_keys = send(keys, 1)
     block = [send(b, 1, True) for b in block]
     (first,) = lay(block[:-1], [(0, rows)])
     facing = [next_keys, across(first)]

time: 149 us -> 146 us (0.980)
  waiting for transfers between devices: 35.1 us -> 32.7 us
  Pallas kernels: 14 us -> 12.4 us
    ppermute x25 -> x26, starting transfers between devices: 59.3 us -> 62 us  [send(): return lax.ppermute(x, ('blk', 'sub'), moves(by, change))]
    pallas_call x16 -> x8, Pallas kernels: 7.07 us -> 4.89 us  [visit(): pl.pallas_call(functools.partial(visit_kernel, begins, len(pieces)), out_...]
    ppermute x25 -> x26, waiting for transfers between devices: 12.5 us -> 10.6 us  [send(): return lax.ppermute(x, ('blk', 'sub'), moves(by, change))]
    ppermute x6 -> x5, starting transfers between devices: 24.7 us -> 24.1 us  [across(): return lax.ppermute(x, 'sub', [(0, 1), (1, 0)])]
  transfers between devices with their start and end apart: 32 -> 32, of which waited for: 9 -> 17; matrix products, arithmetic and copies ran while one was open for 0% -> 0% of each run, Pallas kernels for 7% -> 6%
where the time goes in v2:
time: 146 us
  starting transfers between devices  98.2 us (67%)
  waiting for transfers between devices  32.7 us (22%)
  Pallas kernels  12.4 us (8%)
  between operations  1.5 us (1%)
    ppermute x26, starting transfers between devices, send(): return lax.ppermute(x, ('blk', 'sub'), moves(by, change))  62 us
    ppermute x5, starting transfers between devices, across(): return lax.ppermute(x, 'sub', [(0, 1), (1, 0)])  24.1 us
    all_to_all x1, waiting for transfers between devices, program(): lax.all_to_all(everyone, 'blk', 0, 0, tiled=True).reshape(chips, -1)  22 us
    all_to_all x1, starting transfers between devices, program(): lax.all_to_all(everyone, 'blk', 0, 0, tiled=True).reshape(chips, -1)  12.1 us
    ppermute x26, waiting for transfers between devices, send(): return lax.ppermute(x, ('blk', 'sub'), moves(by, change))  10.6 us
    pallas_call x8, Pallas kernels, visit(): pl.pallas_call(functools.partial(visit_kernel, begins, len(pieces)), out_...  4.89 us
    pallas_call x3, Pallas kernels, meet(): pl.pallas_call(functools.partial(meet_kernel, first_row, len(pieces), len...  4.89 us
  transfers between devices with their start and end apart: 32, of which 17 were waited for; matrix products, arithmetic and copies ran while one was open for 0% of the time, Pallas kernels for 6%

profile of v2, /device:TPU:37, one launch (start us, length us, event | category | flops | bytes accessed | tf_op | source)
XLA Modules:
  0.0 145.9 jit_solution(16175009281371375516)
XLA Ops:
  0.6 1.0 copy-done
  1.6 0.2 normalize.1
  1.8 20.5 %collective-permute-start = (bf16[128,1024]{1,0:T(8,128)(2,1)S(1)}, bf16[128,1024]{1,0:T(8,128)(2,1)S(1)}, u32[]{:S(2)}, u32[]{:S(2)}) collective-permute-start(bf16[128,1024]{1,0:T(8,128)(2,1)S(1)} %get-tuple-element.36.refs_0_), channel_id=1, source_target_pairs={{0,1},{1,0},{2,3},{3,2},{4,5},{5,4},{6,7},{7,6},{8,9},{9,8},{10,11... | collective-permute-start | bytes 786440 | tf_op jit(solution)/shard_map/ppermute | solution.py:277
  22.3 3.8 %collective-permute-start.3 = (bf16[128,1024]{1,0:T(8,128)(2,1)S(1)}, bf16[128,1024]{1,0:T(8,128)(2,1)S(1)}, u32[]{:S(2)}, u32[]{:S(2)}) collective-permute-start(bf16[128,1024]{1,0:T(8,128)(2,1)S(1)} %get-tuple-element.36.refs_0_), channel_id=1, source_target_pairs={{0,2},{1,63},{2,4},{3,1},{4,6},{5,3},{6,8},{7,5},{8,10},{9,7},{10,... | collective-permute-start | bytes 786440 | tf_op jit(solution)/shard_map/ppermute | solution.py:274
  26.2 1.3 collective-permute-start.10
  27.4 0.5 collective-permute-start.2
  27.9 1.5 %collective-permute-done.3.refs_0_ = bf16[128,1024]{1,0:T(8,128)(2,1)S(1)} collective-permute-done((bf16[128,1024]{1,0:T(8,128)(2,1)S(1)}, bf16[128,1024]{1,0:T(8,128)(2,1)S(1)}, u32[]{:S(2)}, u32[]{:S(2)}) %collective-permute-start.3) | collective-permute-done | bytes 262176 | tf_op jit(solution)/shard_map/ppermute | solution.py:274
  29.4 3.1 %collective-permute-start.4 = (bf16[128,1024]{1,0:T(8,128)(2,1)S(1)}, bf16[128,1024]{1,0:T(8,128)(2,1)S(1)}, u32[]{:S(2)}, u32[]{:S(2)}) collective-permute-start(bf16[128,1024]{1,0:T(8,128)(2,1)S(1)} %collective-permute-done.3.refs_0_), channel_id=1, source_target_pairs={{0,2},{1,63},{2,4},{3,1},{4,6},{5,3},{6,8},{7,5},{8,10},{9,7},{10,... | collective-permute-start | bytes 786440 | tf_op jit(solution)/shard_map/ppermute | solution.py:274
  32.6 2.8 %collective-permute-start.11 = (bf16[128,1024]{1,0:T(8,128)(2,1)S(1)}, bf16[128,1024]{1,0:T(8,128)(2,1)S(1)}, u32[]{:S(2)}, u32[]{:S(2)}) collective-permute-start(bf16[128,1024]{1,0:T(8,128)(2,1)S(1)} %collective-permute-done.10.refs_1_), channel_id=1, source_target_pairs={{0,2},{1,63},{2,4},{3,1},{4,6},{5,3},{6,8},{7,5},{8,10},{9,7},{10,... | collective-permute-start | bytes 786440 | tf_op jit(solution)/shard_map/ppermute | solution.py:274
  35.7 0.6 visit.8
  36.3 0.1 collective-permute-start.17
  36.4 2.6 %collective-permute-start.5 = (bf16[128,1024]{1,0:T(8,128)(2,1)S(1)}, bf16[128,1024]{1,0:T(8,128)(2,1)S(1)}, u32[]{:S(2)}, u32[]{:S(2)}) collective-permute-start(bf16[128,1024]{1,0:T(8,128)(2,1)S(1)} %collective-permute-done.4.refs_0_), channel_id=1, source_target_pairs={{0,2},{1,63},{2,4},{3,1},{4,6},{5,3},{6,8},{7,5},{8,10},{9,7},{10,... | collective-permute-start | bytes 786440 | tf_op jit(solution)/shard_map/ppermute | solution.py:274
  39.0 2.8 %collective-permute-start.12 = (bf16[128,1024]{1,0:T(8,128)(2,1)S(1)}, bf16[128,1024]{1,0:T(8,128)(2,1)S(1)}, u32[]{:S(2)}, u32[]{:S(2)}) collective-permute-start(bf16[128,1024]{1,0:T(8,128)(2,1)S(1)} %collective-permute-done.11.refs_1_), channel_id=1, source_target_pairs={{0,2},{1,63},{2,4},{3,1},{4,6},{5,3},{6,8},{7,5},{8,10},{9,7},{10,... | collective-permute-start | bytes 786440 | tf_op jit(solution)/shard_map/ppermute | solution.py:274
  41.8 0.3 collective-permute-done.17.refs_2_
  42.1 0.6 visit.9
  42.7 2.8 %collective-permute-start.18 = (bf16[136,1024]{1,0:T(8,128)(2,1)S(1)}, bf16[136,1024]{1,0:T(8,128)(2,1)S(1)}, u32[]{:S(2)}, u32[]{:S(2)}) collective-permute-start(bf16[136,1024]{1,0:T(8,128)(2,1)S(1)} %get-tuple-element.40), channel_id=1, source_target_pairs={{0,2},{1,63},{2,4},{3,1},{4,6},{5,3},{6,8},{7,5},{8,10},{9,7},{10,... | collective-permute-start | bytes 835592 | tf_op jit(solution)/shard_map/ppermute | solution.py:274
  45.5 2.1 %collective-permute-start.6 = (bf16[128,1024]{1,0:T(8,128)(2,1)S(1)}, bf16[128,1024]{1,0:T(8,128)(2,1)S(1)}, u32[]{:S(2)}, u32[]{:S(2)}) collective-permute-start(bf16[128,1024]{1,0:T(8,128)(2,1)S(1)} %collective-permute-done.5.refs_0_), channel_id=1, source_target_pairs={{0,2},{1,63},{2,4},{3,1},{4,6},{5,3},{6,8},{7,5},{8,10},{9,7},{10,... | collective-permute-start | bytes 786440 | tf_op jit(solution)/shard_map/ppermute | solution.py:274
  47.7 2.7 %collective-permute-start.13 = (bf16[128,1024]{1,0:T(8,128)(2,1)S(1)}, bf16[128,1024]{1,0:T(8,128)(2,1)S(1)}, u32[]{:S(2)}, u32[]{:S(2)}) collective-permute-start(bf16[128,1024]{1,0:T(8,128)(2,1)S(1)} %collective-permute-done.12.refs_1_), channel_id=1, source_target_pairs={{0,2},{1,63},{2,4},{3,1},{4,6},{5,3},{6,8},{7,5},{8,10},{9,7},{10,... | collective-permute-start | bytes 786440 | tf_op jit(solution)/shard_map/ppermute | solution.py:274
  50.4 0.3 collective-permute-done.18.refs_2_
  50.7 0.6 visit.10
  51.3 3.0 %collective-permute-start.19 = (bf16[136,1024]{1,0:T(8,128)(2,1)S(1)}, bf16[136,1024]{1,0:T(8,128)(2,1)S(1)}, u32[]{:S(2)}, u32[]{:S(2)}) collective-permute-start(bf16[136,1024]{1,0:T(8,128)(2,1)S(1)} %get-tuple-element.41), channel_id=1, source_target_pairs={{0,2},{1,63},{2,4},{3,1},{4,6},{5,3},{6,8},{7,5},{8,10},{9,7},{10,... | collective-permute-start | bytes 835592 | tf_op jit(solution)/shard_map/ppermute | solution.py:274
  54.3 1.9 %collective-permute-start.7 = (bf16[128,1024]{1,0:T(8,128)(2,1)S(1)}, bf16[128,1024]{1,0:T(8,128)(2,1)S(1)}, u32[]{:S(2)}, u32[]{:S(2)}) collective-permute-start(bf16[128,1024]{1,0:T(8,128)(2,1)S(1)} %collective-permute-done.6.refs_0_), channel_id=1, source_target_pairs={{0,2},{1,63},{2,4},{3,1},{4,6},{5,3},{6,8},{7,5},{8,10},{9,7},{10,... | collective-permute-start | bytes 786440 | tf_op jit(solution)/shard_map/ppermute | solution.py:274
  56.3 2.7 %collective-permute-start.14 = (bf16[128,1024]{1,0:T(8,128)(2,1)S(1)}, bf16[128,1024]{1,0:T(8,128)(2,1)S(1)}, u32[]{:S(2)}, u32[]{:S(2)}) collective-permute-start(bf16[128,1024]{1,0:T(8,128)(2,1)S(1)} %collective-permute-done.13.refs_1_), channel_id=1, source_target_pairs={{0,2},{1,63},{2,4},{3,1},{4,6},{5,3},{6,8},{7,5},{8,10},{9,7},{10,... | collective-permute-start | bytes 786440 | tf_op jit(solution)/shard_map/ppermute | solution.py:274
  59.0 0.3 collective-permute-done.19.refs_2_
  59.3 0.6 visit.11
  59.9 2.8 %collective-permute-start.20 = (bf16[136,1024]{1,0:T(8,128)(2,1)S(1)}, bf16[136,1024]{1,0:T(8,128)(2,1)S(1)}, u32[]{:S(2)}, u32[]{:S(2)}) collective-permute-start(bf16[136,1024]{1,0:T(8,128)(2,1)S(1)} %get-tuple-element.42), channel_id=1, source_target_pairs={{0,2},{1,63},{2,4},{3,1},{4,6},{5,3},{6,8},{7,5},{8,10},{9,7},{10,... | collective-permute-start | bytes 835592 | tf_op jit(solution)/shard_map/ppermute | solution.py:274
  62.7 2.1 %collective-permute-start.8 = (bf16[128,1024]{1,0:T(8,128)(2,1)S(1)}, bf16[128,1024]{1,0:T(8,128)(2,1)S(1)}, u32[]{:S(2)}, u32[]{:S(2)}) collective-permute-start(bf16[128,1024]{1,0:T(8,128)(2,1)S(1)} %collective-permute-done.7.refs_0_), channel_id=1, source_target_pairs={{0,2},{1,63},{2,4},{3,1},{4,6},{5,3},{6,8},{7,5},{8,10},{9,7},{10,... | collective-permute-start | bytes 786440 | tf_op jit(solution)/shard_map/ppermute | solution.py:274
  64.9 2.7 %collective-permute-start.15 = (bf16[128,1024]{1,0:T(8,128)(2,1)S(1)}, bf16[128,1024]{1,0:T(8,128)(2,1)S(1)}, u32[]{:S(2)}, u32[]{:S(2)}) collective-permute-start(bf16[128,1024]{1,0:T(8,128)(2,1)S(1)} %collective-permute-done.14.refs_1_), channel_id=1, source_target_pairs={{0,2},{1,63},{2,4},{3,1},{4,6},{5,3},{6,8},{7,5},{8,10},{9,7},{10,... | collective-permute-start | bytes 786440 | tf_op jit(solution)/shard_map/ppermute | solution.py:274
  67.6 0.3 collective-permute-done.20.refs_2_
  67.9 0.6 visit.12
  68.5 2.8 %collective-permute-start.21 = (bf16[136,1024]{1,0:T(8,128)(2,1)S(1)}, bf16[136,1024]{1,0:T(8,128)(2,1)S(1)}, u32[]{:S(2)}, u32[]{:S(2)}) collective-permute-start(bf16[136,1024]{1,0:T(8,128)(2,1)S(1)} %get-tuple-element.43), channel_id=1, source_target_pairs={{0,2},{1,63},{2,4},{3,1},{4,6},{5,3},{6,8},{7,5},{8,10},{9,7},{10,... | collective-permute-start | bytes 835592 | tf_op jit(solution)/shard_map/ppermute | solution.py:274
  71.3 2.1 %collective-permute-start.9 = (bf16[128,1024]{1,0:T(8,128)(2,1)S(1)}, bf16[128,1024]{1,0:T(8,128)(2,1)S(1)}, u32[]{:S(2)}, u32[]{:S(2)}) collective-permute-start(bf16[128,1024]{1,0:T(8,128)(2,1)S(1)} %collective-permute-done.8.refs_0_), channel_id=1, source_target_pairs={{0,2},{1,63},{2,4},{3,1},{4,6},{5,3},{6,8},{7,5},{8,10},{9,7},{10,... | collective-permute-start | bytes 786440 | tf_op jit(solution)/shard_map/ppermute | solution.py:274
  73.5 2.7 %collective-permute-start.16 = (bf16[128,1024]{1,0:T(8,128)(2,1)S(1)}, bf16[128,1024]{1,0:T(8,128)(2,1)S(1)}, u32[]{:S(2)}, u32[]{:S(2)}) collective-permute-start(bf16[128,1024]{1,0:T(8,128)(2,1)S(1)} %collective-permute-done.15.refs_1_), channel_id=1, source_target_pairs={{0,2},{1,63},{2,4},{3,1},{4,6},{5,3},{6,8},{7,5},{8,10},{9,7},{10,... | collective-permute-start | bytes 786440 | tf_op jit(solution)/shard_map/ppermute | solution.py:274
  76.2 0.3 collective-permute-done.21.refs_2_
  76.5 0.6 visit.13
  77.1 2.8 %collective-permute-start.22 = (bf16[136,1024]{1,0:T(8,128)(2,1)S(1)}, bf16[136,1024]{1,0:T(8,128)(2,1)S(1)}, u32[]{:S(2)}, u32[]{:S(2)}) collective-permute-start(bf16[136,1024]{1,0:T(8,128)(2,1)S(1)} %get-tuple-element.44), channel_id=1, source_target_pairs={{0,2},{1,63},{2,4},{3,1},{4,6},{5,3},{6,8},{7,5},{8,10},{9,7},{10,... | collective-permute-start | bytes 835592 | tf_op jit(solution)/shard_map/ppermute | solution.py:274
  79.9 2.4 %collective-permute-start.27 = (bf16[128,1024]{1,0:T(8,128)(2,1)S(1)}, bf16[128,1024]{1,0:T(8,128)(2,1)S(1)}, u32[]{:S(2)}, u32[]{:S(2)}) collective-permute-start(bf16[128,1024]{1,0:T(8,128)(2,1)S(1)} %collective-permute-done.9.refs_0_), channel_id=1, source_target_pairs={{0,3},{1,62},{2,5},{3,0},{4,7},{5,2},{6,9},{7,4},{8,11},{9,6},{10,... | collective-permute-start | bytes 786440 | tf_op jit(solution)/shard_map/ppermute | solution.py:274
  82.3 2.4 %collective-permute-start.28 = (bf16[128,1024]{1,0:T(8,128)(2,1)S(1)}, bf16[128,1024]{1,0:T(8,128)(2,1)S(1)}, u32[]{:S(2)}, u32[]{:S(2)}) collective-permute-start(bf16[128,1024]{1,0:T(8,128)(2,1)S(1)} %collective-permute-done.16.refs_1_), channel_id=1, source_target_pairs={{0,3},{1,62},{2,5},{3,0},{4,7},{5,2},{6,9},{7,4},{8,11},{9,6},{10,... | collective-permute-start | bytes 786440 | tf_op jit(solution)/shard_map/ppermute | solution.py:274
  84.7 0.4 collective-permute-done.22.refs_2_
  85.1 0.6 visit.14
  85.7 2.8 %collective-permute-start.23 = (bf16[136,1024]{1,0:T(8,128)(2,1)S(1)}, bf16[136,1024]{1,0:T(8,128)(2,1)S(1)}, u32[]{:S(2)}, u32[]{:S(2)}) collective-permute-start(bf16[136,1024]{1,0:T(8,128)(2,1)S(1)} %get-tuple-element.45), channel_id=1, source_target_pairs={{0,2},{1,63},{2,4},{3,1},{4,6},{5,3},{6,8},{7,5},{8,10},{9,7},{10,... | collective-permute-start | bytes 835592 | tf_op jit(solution)/shard_map/ppermute | solution.py:274
  88.5 1.0 collective-permute-done.27.refs_0_.refs_1_
  89.5 2.8 %collective-permute-done.28.refs_1_.refs_2_ = bf16[128,1024]{1,0:T(8,128)(2,1)S(1)} collective-permute-done((bf16[128,1024]{1,0:T(8,128)(2,1)S(1)}, bf16[128,1024]{1,0:T(8,128)(2,1)S(1)}, u32[]{:S(2)}, u32[]{:S(2)}) %collective-permute-start.28) | collective-permute-done | bytes 262176 | tf_op jit(solution)/shard_map/ppermute | solution.py:274
  92.3 0.1 collective-permute-start.29
  92.5 1.2 collective-permute-done.23.refs_2_
  93.7 0.6 visit.15
  94.3 2.9 %collective-permute-start.25 = (bf16[136,1024]{1,0:T(8,128)(2,1)S(1)}, bf16[136,1024]{1,0:T(8,128)(2,1)S(1)}, u32[]{:S(2)}, u32[]{:S(2)}) collective-permute-start(bf16[136,1024]{1,0:T(8,128)(2,1)S(1)} %get-tuple-element.47), channel_id=1, source_target_pairs={{0,3},{1,62},{2,5},{3,0},{4,7},{5,2},{6,9},{7,4},{8,11},{9,6},{10,... | collective-permute-start | bytes 835592 | tf_op jit(solution)/shard_map/ppermute | solution.py:274
  97.2 0.4 collective-permute-start.24
  97.6 0.1 lay.12
  97.7 0.1 lay.13
  97.9 0.1 lay.14
  98.0 0.1 lay.15
  98.2 0.1 lay.16
  98.3 0.1 lay.17
  98.4 1.6 %collective-permute-start.26 = (s32[1,384]{1,0:T(1,128)S(1)}, s32[1,384]{1,0:T(1,128)S(1)}, u32[]{:S(2)}, u32[]{:S(2)}) collective-permute-start(s32[1,384]{1,0:T(1,128)S(1)} %get-tuple-element.46.refs_3_), channel_id=1, source_target_pairs={{0,2},{1,63},{2,4},{3,1},{4,6},{5,3},{6,8},{7,5},{8,10},{9,7},{10,... | collective-permute-start | bytes 4616 | tf_op jit(solution)/shard_map/ppermute | solution.py:274
  100.1 1.7 %collective-permute-done.24.refs_0_ = s32[1,384]{1,0:T(1,128)S(1)} collective-permute-done((s32[1,384]{1,0:T(1,128)S(1)}, s32[1,384]{1,0:T(1,128)S(1)}, u32[]{:S(2)}, u32[]{:S(2)}) %collective-permute-start.24) | collective-permute-done | bytes 1568 | tf_op jit(solution)/shard_map/ppermute | solution.py:274
  101.9 2.0 %meet.3.refs_20_ = f32[1,256]{1,0:T(1,128)S(1)} custom-call(s32[1,384]{1,0:T(1,128)S(1)} %collective-permute-done.24.refs_0_, bf16[128,1024]{1,0:T(8,128)(2,1)S(1)} %collective-permute-done.27.refs_0_.refs_1_, bf16[128,1024]{1,0:T(8,128)(2,1)S(1)} %collective-permute-done.28.refs_1_.refs_2_, bf16[384,1024]{1,0:T(8,128)(2,1)S(1)} %get-tuple-element.38.own_ref.refs_3_.refs_2_, ...), custom_call_target="tpu_custom_call" | custom-call | flops 1610612736 | bytes 6815744 | tf_op jit(solution)/shard_map/meet/pallas_call | solution.py:199
  103.9 0.3 meet.4.refs_21_
  104.3 2.6 %meet.5 = f32[32,1,384]{2,1,0:T(1,128)} custom-call(s32[1,384]{1,0:T(1,128)S(1)} %collective-permute-done.24.refs_0_, bf16[136,1024]{1,0:T(8,128)(2,1)S(1)} %collective-permute-done.25.refs_1_, bf16[384,1024]{1,0:T(8,128)(2,1)S(1)} %get-tuple-element.38.own_ref.refs_3_.refs_2_, s32[384,128]{1,0:T(8,128)S(1)} %columns.1.own_columns_ref.refs_4_.refs_3_, ...), custom_call_target="tpu_custom_call" | custom-call | flops 909115392 | bytes 6963200 | tf_op jit(solution)/shard_map/meet/pallas_call | solution.py:199
  106.8 12.1 %all-to-all-start = ((f32[32,1,384]{2,1,0:T(1,128)}), f32[32,1,384]{2,1,0:T(1,128)S(1)}, u32[]{:S(2)}, u32[]{:S(2)}) async-start(f32[32,1,384]{2,1,0:T(1,128)} %meet.5), calls=%async_computation | async-start | bytes 98304 | tf_op jit(solution)/shard_map/all_to_all | solution.py:306
  118.9 22.0 %all-to-all-done = f32[32,1,384]{2,1,0:T(1,128)S(1)} async-done(((f32[32,1,384]{2,1,0:T(1,128)}), f32[32,1,384]{2,1,0:T(1,128)S(1)}, u32[]{:S(2)}, u32[]{:S(2)}) %all-to-all-start) | async-done | bytes 49184 | tf_op jit(solution)/shard_map/all_to_all | solution.py:306
  140.9 2.9 %collective-permute-start.30 = (f32[32,384]{1,0:T(8,128)S(1)}, f32[32,384]{1,0:T(8,128)S(1)}, u32[]{:S(2)}, u32[]{:S(2)}) collective-permute-start(f32[32,384]{1,0:T(8,128)S(1)} %bitcast.8), channel_id=1, source_target_pairs={{0,1},{1,0},{2,3},{3,2},{4,5},{5,4},{6,7},{7,6},{8,9},{9,8},{10,11... | collective-permute-start | bytes 147464 | tf_op jit(solution)/shard_map/ppermute | solution.py:277
  144.5 0.2 collective-permute-done.30.theirs_ref
  144.7 1.2 finish.1
  (31 shorter events, 1.0 us)
Async XLA Ops:
  0.6 1.0 copy-start
  1.8 24.3 %collective-permute-start = (bf16[128,1024]{1,0:T(8,128)(2,1)S(1)}, bf16[128,1024]{1,0:T(8,128)(2,1)S(1)}, u32[]{:S(2)}, u32[]{:S(2)}) collective-permute-start(bf16[128,1024]{1,0:T(8,128)(2,1)S(1)} %get-tuple-element.36.refs_0_), channel_id=1, source_target_pairs={{0,1},{1,0},{2,3},{3,2},{4,5},{5,4},{6,7},{7,6},{8,9},{9,8},{10,11... | collective-permute-start | bytes 786440 | tf_op jit(solution)/shard_map/ppermute | solution.py:277
  22.3 7.1 %collective-permute-start.3 = (bf16[128,1024]{1,0:T(8,128)(2,1)S(1)}, bf16[128,1024]{1,0:T(8,128)(2,1)S(1)}, u32[]{:S(2)}, u32[]{:S(2)}) collective-permute-start(bf16[128,1024]{1,0:T(8,128)(2,1)S(1)} %get-tuple-element.36.refs_0_), channel_id=1, source_target_pairs={{0,2},{1,63},{2,4},{3,1},{4,6},{5,3},{6,8},{7,5},{8,10},{9,7},{10,... | collective-permute-start | bytes 786440 | tf_op jit(solution)/shard_map/ppermute | solution.py:274
  26.1 1.3 copy-start.1
  26.2 6.4 %collective-permute-start.10 = (bf16[128,1024]{1,0:T(8,128)(2,1)S(1)}, bf16[128,1024]{1,0:T(8,128)(2,1)S(1)}, u32[]{:S(2)}, u32[]{:S(2)}) collective-permute-start(bf16[128,1024]{1,0:T(8,128)(2,1)S(1)} %lay.11.refs_1_), channel_id=1, source_target_pairs={{0,2},{1,63},{2,4},{3,1},{4,6},{5,3},{6,8},{7,5},{8,10},{9,7},{10,... | collective-permute-start | bytes 786440 | tf_op jit(solution)/shard_map/ppermute | solution.py:274
  27.4 8.1 %collective-permute-start.1 = (bf16[64,1024]{1,0:T(8,128)(2,1)S(1)}, bf16[64,1024]{1,0:T(8,128)(2,1)S(1)}, u32[]{:S(2)}, u32[]{:S(2)}) collective-permute-start(bf16[64,1024]{1,0:T(8,128)(2,1)S(1)} %get-tuple-element.37.refs_1_.refs_0_), channel_id=1, source_target_pairs={{0,1},{1,0},{2,3},{3,2},{4,5},{5,4},{6,7},{7,6},{8,9},{9,8},{10,11... | collective-permute-start | bytes 393224 | tf_op jit(solution)/shard_map/ppermute | solution.py:277
  27.4 7.9 %collective-permute-start.2 = (s32[1,192]{1,0:T(1,128)S(1)}, s32[1,192]{1,0:T(1,128)S(1)}, u32[]{:S(2)}, u32[]{:S(2)}) collective-permute-start(s32[1,192]{1,0:T(1,128)S(1)} %bitcast.10), channel_id=1, source_target_pairs={{0,1},{1,0},{2,3},{3,2},{4,5},{5,4},{6,7},{7,6},{8,9},{9,8},{10,11... | collective-permute-start | bytes 2312 | tf_op jit(solution)/shard_map/ppermute | solution.py:277
  29.4 7.0 %collective-permute-start.4 = (bf16[128,1024]{1,0:T(8,128)(2,1)S(1)}, bf16[128,1024]{1,0:T(8,128)(2,1)S(1)}, u32[]{:S(2)}, u32[]{:S(2)}) collective-permute-start(bf16[128,1024]{1,0:T(8,128)(2,1)S(1)} %collective-permute-done.3.refs_0_), channel_id=1, source_target_pairs={{0,2},{1,63},{2,4},{3,1},{4,6},{5,3},{6,8},{7,5},{8,10},{9,7},{10,... | collective-permute-start | bytes 786440 | tf_op jit(solution)/shard_map/ppermute | solution.py:274
  32.6 6.4 %collective-permute-start.11 = (bf16[128,1024]{1,0:T(8,128)(2,1)S(1)}, bf16[128,1024]{1,0:T(8,128)(2,1)S(1)}, u32[]{:S(2)}, u32[]{:S(2)}) collective-permute-start(bf16[128,1024]{1,0:T(8,128)(2,1)S(1)} %collective-permute-done.10.refs_1_), channel_id=1, source_target_pairs={{0,2},{1,63},{2,4},{3,1},{4,6},{5,3},{6,8},{7,5},{8,10},{9,7},{10,... | collective-permute-start | bytes 786440 | tf_op jit(solution)/shard_map/ppermute | solution.py:274
  36.3 5.8 %collective-permute-start.17 = (bf16[136,1024]{1,0:T(8,128)(2,1)S(1)}, bf16[136,1024]{1,0:T(8,128)(2,1)S(1)}, u32[]{:S(2)}, u32[]{:S(2)}) collective-permute-start(bf16[136,1024]{1,0:T(8,128)(2,1)S(1)} %visit.8), channel_id=1, source_target_pairs={{0,2},{1,63},{2,4},{3,1},{4,6},{5,3},{6,8},{7,5},{8,10},{9,7},{10,... | collective-permute-start | bytes 835592 | tf_op jit(solution)/shard_map/ppermute | solution.py:274
  36.4 9.1 %collective-permute-start.5 = (bf16[128,1024]{1,0:T(8,128)(2,1)S(1)}, bf16[128,1024]{1,0:T(8,128)(2,1)S(1)}, u32[]{:S(2)}, u32[]{:S(2)}) collective-permute-start(bf16[128,1024]{1,0:T(8,128)(2,1)S(1)} %collective-permute-done.4.refs_0_), channel_id=1, source_target_pairs={{0,2},{1,63},{2,4},{3,1},{4,6},{5,3},{6,8},{7,5},{8,10},{9,7},{10,... | collective-permute-start | bytes 786440 | tf_op jit(solution)/shard_map/ppermute | solution.py:274
  39.0 8.7 %collective-permute-start.12 = (bf16[128,1024]{1,0:T(8,128)(2,1)S(1)}, bf16[128,1024]{1,0:T(8,128)(2,1)S(1)}, u32[]{:S(2)}, u32[]{:S(2)}) collective-permute-start(bf16[128,1024]{1,0:T(8,128)(2,1)S(1)} %collective-permute-done.11.refs_1_), channel_id=1, source_target_pairs={{0,2},{1,63},{2,4},{3,1},{4,6},{5,3},{6,8},{7,5},{8,10},{9,7},{10,... | collective-permute-start | bytes 786440 | tf_op jit(solution)/shard_map/ppermute | solution.py:274
  42.7 8.0 %collective-permute-start.18 = (bf16[136,1024]{1,0:T(8,128)(2,1)S(1)}, bf16[136,1024]{1,0:T(8,128)(2,1)S(1)}, u32[]{:S(2)}, u32[]{:S(2)}) collective-permute-start(bf16[136,1024]{1,0:T(8,128)(2,1)S(1)} %get-tuple-element.40), channel_id=1, source_target_pairs={{0,2},{1,63},{2,4},{3,1},{4,6},{5,3},{6,8},{7,5},{8,10},{9,7},{10,... | collective-permute-start | bytes 835592 | tf_op jit(solution)/shard_map/ppermute | solution.py:274
  45.5 8.8 %collective-permute-start.6 = (bf16[128,1024]{1,0:T(8,128)(2,1)S(1)}, bf16[128,1024]{1,0:T(8,128)(2,1)S(1)}, u32[]{:S(2)}, u32[]{:S(2)}) collective-permute-start(bf16[128,1024]{1,0:T(8,128)(2,1)S(1)} %collective-permute-done.5.refs_0_), channel_id=1, source_target_pairs={{0,2},{1,63},{2,4},{3,1},{4,6},{5,3},{6,8},{7,5},{8,10},{9,7},{10,... | collective-permute-start | bytes 786440 | tf_op jit(solution)/shard_map/ppermute | solution.py:274
  47.7 8.6 %collective-permute-start.13 = (bf16[128,1024]{1,0:T(8,128)(2,1)S(1)}, bf16[128,1024]{1,0:T(8,128)(2,1)S(1)}, u32[]{:S(2)}, u32[]{:S(2)}) collective-permute-start(bf16[128,1024]{1,0:T(8,128)(2,1)S(1)} %collective-permute-done.12.refs_1_), channel_id=1, source_target_pairs={{0,2},{1,63},{2,4},{3,1},{4,6},{5,3},{6,8},{7,5},{8,10},{9,7},{10,... | collective-permute-start | bytes 786440 | tf_op jit(solution)/shard_map/ppermute | solution.py:274
  51.3 8.0 %collective-permute-start.19 = (bf16[136,1024]{1,0:T(8,128)(2,1)S(1)}, bf16[136,1024]{1,0:T(8,128)(2,1)S(1)}, u32[]{:S(2)}, u32[]{:S(2)}) collective-permute-start(bf16[136,1024]{1,0:T(8,128)(2,1)S(1)} %get-tuple-element.41), channel_id=1, source_target_pairs={{0,2},{1,63},{2,4},{3,1},{4,6},{5,3},{6,8},{7,5},{8,10},{9,7},{10,... | collective-permute-start | bytes 835592 | tf_op jit(solution)/shard_map/ppermute | solution.py:274
  54.3 8.4 %collective-permute-start.7 = (bf16[128,1024]{1,0:T(8,128)(2,1)S(1)}, bf16[128,1024]{1,0:T(8,128)(2,1)S(1)}, u32[]{:S(2)}, u32[]{:S(2)}) collective-permute-start(bf16[128,1024]{1,0:T(8,128)(2,1)S(1)} %collective-permute-done.6.refs_0_), channel_id=1, source_target_pairs={{0,2},{1,63},{2,4},{3,1},{4,6},{5,3},{6,8},{7,5},{8,10},{9,7},{10,... | collective-permute-start | bytes 786440 | tf_op jit(solution)/shard_map/ppermute | solution.py:274
  56.3 8.6 %collective-permute-start.14 = (bf16[128,1024]{1,0:T(8,128)(2,1)S(1)}, bf16[128,1024]{1,0:T(8,128)(2,1)S(1)}, u32[]{:S(2)}, u32[]{:S(2)}) collective-permute-start(bf16[128,1024]{1,0:T(8,128)(2,1)S(1)} %collective-permute-done.13.refs_1_), channel_id=1, source_target_pairs={{0,2},{1,63},{2,4},{3,1},{4,6},{5,3},{6,8},{7,5},{8,10},{9,7},{10,... | collective-permute-start | bytes 786440 | tf_op jit(solution)/shard_map/ppermute | solution.py:274
  59.9 8.0 %collective-permute-start.20 = (bf16[136,1024]{1,0:T(8,128)(2,1)S(1)}, bf16[136,1024]{1,0:T(8,128)(2,1)S(1)}, u32[]{:S(2)}, u32[]{:S(2)}) collective-permute-start(bf16[136,1024]{1,0:T(8,128)(2,1)S(1)} %get-tuple-element.42), channel_id=1, source_target_pairs={{0,2},{1,63},{2,4},{3,1},{4,6},{5,3},{6,8},{7,5},{8,10},{9,7},{10,... | collective-permute-start | bytes 835592 | tf_op jit(solution)/shard_map/ppermute | solution.py:274
  62.7 8.6 %collective-permute-start.8 = (bf16[128,1024]{1,0:T(8,128)(2,1)S(1)}, bf16[128,1024]{1,0:T(8,128)(2,1)S(1)}, u32[]{:S(2)}, u32[]{:S(2)}) collective-permute-start(bf16[128,1024]{1,0:T(8,128)(2,1)S(1)} %collective-permute-done.7.refs_0_), channel_id=1, source_target_pairs={{0,2},{1,63},{2,4},{3,1},{4,6},{5,3},{6,8},{7,5},{8,10},{9,7},{10,... | collective-permute-start | bytes 786440 | tf_op jit(solution)/shard_map/ppermute | solution.py:274
  64.9 8.6 %collective-permute-start.15 = (bf16[128,1024]{1,0:T(8,128)(2,1)S(1)}, bf16[128,1024]{1,0:T(8,128)(2,1)S(1)}, u32[]{:S(2)}, u32[]{:S(2)}) collective-permute-start(bf16[128,1024]{1,0:T(8,128)(2,1)S(1)} %collective-permute-done.14.refs_1_), channel_id=1, source_target_pairs={{0,2},{1,63},{2,4},{3,1},{4,6},{5,3},{6,8},{7,5},{8,10},{9,7},{10,... | collective-permute-start | bytes 786440 | tf_op jit(solution)/shard_map/ppermute | solution.py:274
  68.5 8.0 %collective-permute-start.21 = (bf16[136,1024]{1,0:T(8,128)(2,1)S(1)}, bf16[136,1024]{1,0:T(8,128)(2,1)S(1)}, u32[]{:S(2)}, u32[]{:S(2)}) collective-permute-start(bf16[136,1024]{1,0:T(8,128)(2,1)S(1)} %get-tuple-element.43), channel_id=1, source_target_pairs={{0,2},{1,63},{2,4},{3,1},{4,6},{5,3},{6,8},{7,5},{8,10},{9,7},{10,... | collective-permute-start | bytes 835592 | tf_op jit(solution)/shard_map/ppermute | solution.py:274
  71.3 8.6 %collective-permute-start.9 = (bf16[128,1024]{1,0:T(8,128)(2,1)S(1)}, bf16[128,1024]{1,0:T(8,128)(2,1)S(1)}, u32[]{:S(2)}, u32[]{:S(2)}) collective-permute-start(bf16[128,1024]{1,0:T(8,128)(2,1)S(1)} %collective-permute-done.8.refs_0_), channel_id=1, source_target_pairs={{0,2},{1,63},{2,4},{3,1},{4,6},{5,3},{6,8},{7,5},{8,10},{9,7},{10,... | collective-permute-start | bytes 786440 | tf_op jit(solution)/shard_map/ppermute | solution.py:274
  73.5 8.8 %collective-permute-start.16 = (bf16[128,1024]{1,0:T(8,128)(2,1)S(1)}, bf16[128,1024]{1,0:T(8,128)(2,1)S(1)}, u32[]{:S(2)}, u32[]{:S(2)}) collective-permute-start(bf16[128,1024]{1,0:T(8,128)(2,1)S(1)} %collective-permute-done.15.refs_1_), channel_id=1, source_target_pairs={{0,2},{1,63},{2,4},{3,1},{4,6},{5,3},{6,8},{7,5},{8,10},{9,7},{10,... | collective-permute-start | bytes 786440 | tf_op jit(solution)/shard_map/ppermute | solution.py:274
  77.1 8.0 %collective-permute-start.22 = (bf16[136,1024]{1,0:T(8,128)(2,1)S(1)}, bf16[136,1024]{1,0:T(8,128)(2,1)S(1)}, u32[]{:S(2)}, u32[]{:S(2)}) collective-permute-start(bf16[136,1024]{1,0:T(8,128)(2,1)S(1)} %get-tuple-element.44), channel_id=1, source_target_pairs={{0,2},{1,63},{2,4},{3,1},{4,6},{5,3},{6,8},{7,5},{8,10},{9,7},{10,... | collective-permute-start | bytes 835592 | tf_op jit(solution)/shard_map/ppermute | solution.py:274
  79.9 9.6 %collective-permute-start.27 = (bf16[128,1024]{1,0:T(8,128)(2,1)S(1)}, bf16[128,1024]{1,0:T(8,128)(2,1)S(1)}, u32[]{:S(2)}, u32[]{:S(2)}) collective-permute-start(bf16[128,1024]{1,0:T(8,128)(2,1)S(1)} %collective-permute-done.9.refs_0_), channel_id=1, source_target_pairs={{0,3},{1,62},{2,5},{3,0},{4,7},{5,2},{6,9},{7,4},{8,11},{9,6},{10,... | collective-permute-start | bytes 786440 | tf_op jit(solution)/shard_map/ppermute | solution.py:274
  82.3 10.0 %collective-permute-start.28 = (bf16[128,1024]{1,0:T(8,128)(2,1)S(1)}, bf16[128,1024]{1,0:T(8,128)(2,1)S(1)}, u32[]{:S(2)}, u32[]{:S(2)}) collective-permute-start(bf16[128,1024]{1,0:T(8,128)(2,1)S(1)} %collective-permute-done.16.refs_1_), channel_id=1, source_target_pairs={{0,3},{1,62},{2,5},{3,0},{4,7},{5,2},{6,9},{7,4},{8,11},{9,6},{10,... | collective-permute-start | bytes 786440 | tf_op jit(solution)/shard_map/ppermute | solution.py:274
  85.7 8.0 %collective-permute-start.23 = (bf16[136,1024]{1,0:T(8,128)(2,1)S(1)}, bf16[136,1024]{1,0:T(8,128)(2,1)S(1)}, u32[]{:S(2)}, u32[]{:S(2)}) collective-permute-start(bf16[136,1024]{1,0:T(8,128)(2,1)S(1)} %get-tuple-element.45), channel_id=1, source_target_pairs={{0,2},{1,63},{2,4},{3,1},{4,6},{5,3},{6,8},{7,5},{8,10},{9,7},{10,... | collective-permute-start | bytes 835592 | tf_op jit(solution)/shard_map/ppermute | solution.py:274
  92.3 11.6 %collective-permute-start.29 = (bf16[192,1024]{1,0:T(8,128)(2,1)S(1)}, bf16[192,1024]{1,0:T(8,128)(2,1)S(1)}, u32[]{:S(2)}, u32[]{:S(2)}) collective-permute-start(bf16[192,1024]{1,0:T(8,128)(2,1)S(1)} %lay.19), channel_id=1, source_target_pairs={{0,1},{1,0},{2,3},{3,2},{4,5},{5,4},{6,7},{7,6},{8,9},{9,8},{10,11... | collective-permute-start | bytes 1179656 | tf_op jit(solution)/shard_map/ppermute | solution.py:277
  94.3 9.9 %collective-permute-start.25 = (bf16[136,1024]{1,0:T(8,128)(2,1)S(1)}, bf16[136,1024]{1,0:T(8,128)(2,1)S(1)}, u32[]{:S(2)}, u32[]{:S(2)}) collective-permute-start(bf16[136,1024]{1,0:T(8,128)(2,1)S(1)} %get-tuple-element.47), channel_id=1, source_target_pairs={{0,3},{1,62},{2,5},{3,0},{4,7},{5,2},{6,9},{7,4},{8,11},{9,6},{10,... | collective-permute-start | bytes 835592 | tf_op jit(solution)/shard_map/ppermute | solution.py:274
  97.2 4.6 %collective-permute-start.24 = (s32[1,384]{1,0:T(1,128)S(1)}, s32[1,384]{1,0:T(1,128)S(1)}, u32[]{:S(2)}, u32[]{:S(2)}) collective-permute-start(s32[1,384]{1,0:T(1,128)S(1)} %get-tuple-element.46.refs_3_), channel_id=1, source_target_pairs={{0,3},{1,62},{2,5},{3,0},{4,7},{5,2},{6,9},{7,4},{8,11},{9,6},{10,... | collective-permute-start | bytes 4616 | tf_op jit(solution)/shard_map/ppermute | solution.py:274
  98.4 5.5 %collective-permute-start.26 = (s32[1,384]{1,0:T(1,128)S(1)}, s32[1,384]{1,0:T(1,128)S(1)}, u32[]{:S(2)}, u32[]{:S(2)}) collective-permute-start(s32[1,384]{1,0:T(1,128)S(1)} %get-tuple-element.46.refs_3_), channel_id=1, source_target_pairs={{0,2},{1,63},{2,4},{3,1},{4,6},{5,3},{6,8},{7,5},{8,10},{9,7},{10,... | collective-permute-start | bytes 4616 | tf_op jit(solution)/shard_map/ppermute | solution.py:274
  106.8 34.1 %all-to-all-start = ((f32[32,1,384]{2,1,0:T(1,128)}), f32[32,1,384]{2,1,0:T(1,128)S(1)}, u32[]{:S(2)}, u32[]{:S(2)}) async-start(f32[32,1,384]{2,1,0:T(1,128)} %meet.5), calls=%async_computation | async-start | bytes 98304 | tf_op jit(solution)/shard_map/all_to_all | solution.py:306
  140.9 3.8 %collective-permute-start.30 = (f32[32,384]{1,0:T(8,128)S(1)}, f32[32,384]{1,0:T(8,128)S(1)}, u32[]{:S(2)}, u32[]{:S(2)}) collective-permute-start(f32[32,384]{1,0:T(8,128)S(1)} %bitcast.8), channel_id=1, source_target_pairs={{0,1},{1,0},{2,3},{3,2},{4,5},{5,4},{6,7},{7,6},{8,9},{9,8},{10,11... | collective-permute-start | bytes 147464 | tf_op jit(solution)/shard_map/ppermute | solution.py:277

commit v3 on v2

--- a/solution.py
+++ b/solution.py
@@ -145,6 +145,46 @@
         ),
         name="visit",
     )(*operands)
+
+
+def late_visit_kernel(pieces, own_ref, own_columns_ref, *refs):
+    piece_refs, out_ref = refs[:pieces], refs[-1]
+    total = out_ref.shape[1]
+    rows = jnp.concatenate([r[...] for r in piece_refs], axis=0)[:total]
+    keys, acc = read_tail(piece_refs[-1], total)
+    low = keys & jnp.int32(-label_stride)
+    out_ref[...] = best_of(acc, keys, low, rows, own_ref[...], own_columns_ref[...])
+
+
+def late_visit(own, pieces):
+    total, width = own[0].shape
+    operands = [*own, *pieces]
+    return pl.pallas_call(
+        functools.partial(late_visit_kernel, len(pieces)),
+        out_shape=jax.ShapeDtypeStruct((1, total), jnp.float32),
+        in_specs=[VMEM] * len(operands),
+        out_specs=VMEM,
+        compiler_params=PARAMS,
+        cost_estimate=pl.CostEstimate(
+            flops=total, bytes_accessed=4 * total * width, transcendentals=0
+        ),
+        name="late_visit",
+    )(*operands)
+
+
+def decode_kernel(piece_ref, keys_ref):
+    keys_ref[...] = read_tail(piece_ref, keys_ref.shape[1])[0]
+
+
+def decode(piece, count):
+    return pl.pallas_call(
+        decode_kernel,
+        out_shape=jax.ShapeDtypeStruct((1, count), jnp.int32),
+        in_specs=[VMEM],
+        out_specs=VMEM,
+        compiler_params=PARAMS,
+        name="decode",
+    )(piece)
 
 
 def columns_kernel(keys_ref, columns_ref):
@@ -183,6 +223,7 @@
         earlier = jnp.maximum(refs[at][...], refs[at + 1][...])
         best = jnp.concatenate([earlier, best], axis=1)
         best = jnp.maximum(best, read_tail(refs[1], best.shape[1])[1])
+        best = jnp.maximum(best, refs[at + 2][...])
         out_ref[...] = jnp.broadcast_to(best[:, None, :], out_ref.shape)
     else:
         out_ref[...] = best
@@ -289,19 +330,24 @@
     own = (whole, columns_of(keys))
     held = [own]
     (block[-1],) = visit(own, block, keys)
-    for _ in range(1, hops):
+    for h in range(1, hops):
         block = [send(b, 1) for b in block]
-        keys, last = visit(own, block)
+        if h < hops - 1:
+            keys, last = visit(own, block)
+        else:
+            keys, last = decode(block[-1], total), block[-1]
+            late = late_visit(own, block)
         held.append(lay(block, [(0, total)], [keys]))
         block[-1] = last
     last_keys = send(keys, 1, True)
     next_keys = send(keys, 1)
+    late = send(late, 1, True)
     block = [send(b, 1, True) for b in block]
     (first,) = lay(block[:-1], [(0, rows)])
     facing = [next_keys, across(first)]
     split = size * (PIECES - 1)
     early = [meet(last_keys, 0, block[:-1], held), meet(last_keys, 0, block[:-1], [], facing)]
-    everyone = meet(last_keys, split, block[-1:], held, facing, early, chips)
+    everyone = meet(last_keys, split, block[-1:], held, facing, (*early, late), chips)
 
     gathered = lax.all_to_all(everyone, "blk", 0, 0, tiled=True).reshape(chips, -1)
     other_side = across(gathered)

time: 146 us -> 147 us (level)
    ppermute x5, starting transfers between devices: 24.1 us -> 21.6 us  [across(): return lax.ppermute(x, 'sub', [(0, 1), (1, 0)])]
    ppermute x26 -> x27, starting transfers between devices: 62 us -> 64.5 us  [send(): return lax.ppermute(x, ('blk', 'sub'), moves(by, change))]
    all_to_all x1, waiting for transfers between devices: 22 us -> 24.2 us  [program(): lax.all_to_all(everyone, 'blk', 0, 0, tiled=True).reshape(chips, -1)]
    ppermute x26 -> x27, waiting for transfers between devices: 10.6 us -> 8.84 us  [send(): return lax.ppermute(x, ('blk', 'sub'), moves(by, change))]
    pallas_call x8 -> x7, Pallas kernels: 4.89 us -> 4.3 us  [visit(): pl.pallas_call(functools.partial(visit_kernel, begins, len(pieces)), out_...]
  transfers between devices with their start and end apart: 32 -> 33, of which waited for: 17 -> 16; matrix products, arithmetic and copies ran while one was open for 0% -> 0% of each run, Pallas kernels for 6% -> 6%
where the time goes in v3:
time: 147 us
  starting transfers between devices  98.7 us (67%)
  waiting for transfers between devices  33.2 us (23%)
  Pallas kernels  12.4 us (8%)
  between operations  1.51 us (1%)
    ppermute x27, starting transfers between devices, send(): return lax.ppermute(x, ('blk', 'sub'), moves(by, change))  64.5 us
    all_to_all x1, waiting for transfers between devices, program(): lax.all_to_all(everyone, 'blk', 0, 0, tiled=True).reshape(chips, -1)  24.2 us
    ppermute x5, starting transfers between devices, across(): return lax.ppermute(x, 'sub', [(0, 1), (1, 0)])  21.6 us
    all_to_all x1, starting transfers between devices, program(): lax.all_to_all(everyone, 'blk', 0, 0, tiled=True).reshape(chips, -1)  12.6 us
    ppermute x27, waiting for transfers between devices, send(): return lax.ppermute(x, ('blk', 'sub'), moves(by, change))  8.84 us
    pallas_call x3, Pallas kernels, meet(): pl.pallas_call(functools.partial(meet_kernel, first_row, len(pieces), len...  4.93 us
    pallas_call x7, Pallas kernels, visit(): pl.pallas_call(functools.partial(visit_kernel, begins, len(pieces)), out_...  4.3 us
  transfers between devices with their start and end apart: 33, of which 16 were waited for; matrix products, arithmetic and copies ran while one was open for 0% of the time, Pallas kernels for 6%

profile of v3, /device:TPU:37, one launch (start us, length us, event | category | flops | bytes accessed | tf_op | source)
XLA Modules:
  0.0 147.0 jit_solution(2463897355704874743)
XLA Ops:
  0.6 1.0 copy-done
  1.6 0.2 normalize.1
  1.8 20.5 %collective-permute-start = (bf16[128,1024]{1,0:T(8,128)(2,1)S(1)}, bf16[128,1024]{1,0:T(8,128)(2,1)S(1)}, u32[]{:S(2)}, u32[]{:S(2)}) collective-permute-start(bf16[128,1024]{1,0:T(8,128)(2,1)S(1)} %get-tuple-element.34.refs_0_), channel_id=1, source_target_pairs={{0,1},{1,0},{2,3},{3,2},{4,5},{5,4},{6,7},{7,6},{8,9},{9,8},{10,11... | collective-permute-start | bytes 786440 | tf_op jit(solution)/shard_map/ppermute | solution.py:318
  22.3 3.8 %collective-permute-start.3 = (bf16[128,1024]{1,0:T(8,128)(2,1)S(1)}, bf16[128,1024]{1,0:T(8,128)(2,1)S(1)}, u32[]{:S(2)}, u32[]{:S(2)}) collective-permute-start(bf16[128,1024]{1,0:T(8,128)(2,1)S(1)} %get-tuple-element.34.refs_0_), channel_id=1, source_target_pairs={{0,2},{1,63},{2,4},{3,1},{4,6},{5,3},{6,8},{7,5},{8,10},{9,7},{10,... | collective-permute-start | bytes 786440 | tf_op jit(solution)/shard_map/ppermute | solution.py:315
  26.2 1.3 collective-permute-start.9
  27.4 0.5 collective-permute-start.2
  27.9 1.5 %collective-permute-done.3.refs_0_ = bf16[128,1024]{1,0:T(8,128)(2,1)S(1)} collective-permute-done((bf16[128,1024]{1,0:T(8,128)(2,1)S(1)}, bf16[128,1024]{1,0:T(8,128)(2,1)S(1)}, u32[]{:S(2)}, u32[]{:S(2)}) %collective-permute-start.3) | collective-permute-done | bytes 262176 | tf_op jit(solution)/shard_map/ppermute | solution.py:315
  29.4 3.1 %collective-permute-start.4 = (bf16[128,1024]{1,0:T(8,128)(2,1)S(1)}, bf16[128,1024]{1,0:T(8,128)(2,1)S(1)}, u32[]{:S(2)}, u32[]{:S(2)}) collective-permute-start(bf16[128,1024]{1,0:T(8,128)(2,1)S(1)} %collective-permute-done.3.refs_0_), channel_id=1, source_target_pairs={{0,2},{1,63},{2,4},{3,1},{4,6},{5,3},{6,8},{7,5},{8,10},{9,7},{10,... | collective-permute-start | bytes 786440 | tf_op jit(solution)/shard_map/ppermute | solution.py:315
  32.6 2.8 %collective-permute-start.10 = (bf16[128,1024]{1,0:T(8,128)(2,1)S(1)}, bf16[128,1024]{1,0:T(8,128)(2,1)S(1)}, u32[]{:S(2)}, u32[]{:S(2)}) collective-permute-start(bf16[128,1024]{1,0:T(8,128)(2,1)S(1)} %collective-permute-done.9.refs_1_), channel_id=1, source_target_pairs={{0,2},{1,63},{2,4},{3,1},{4,6},{5,3},{6,8},{7,5},{8,10},{9,7},{10,... | collective-permute-start | bytes 786440 | tf_op jit(solution)/shard_map/ppermute | solution.py:315
  35.7 0.6 visit.7
  36.3 0.1 collective-permute-start.15
  36.4 2.6 %collective-permute-start.5 = (bf16[128,1024]{1,0:T(8,128)(2,1)S(1)}, bf16[128,1024]{1,0:T(8,128)(2,1)S(1)}, u32[]{:S(2)}, u32[]{:S(2)}) collective-permute-start(bf16[128,1024]{1,0:T(8,128)(2,1)S(1)} %collective-permute-done.4.refs_0_), channel_id=1, source_target_pairs={{0,2},{1,63},{2,4},{3,1},{4,6},{5,3},{6,8},{7,5},{8,10},{9,7},{10,... | collective-permute-start | bytes 786440 | tf_op jit(solution)/shard_map/ppermute | solution.py:315
  39.0 2.8 %collective-permute-start.11 = (bf16[128,1024]{1,0:T(8,128)(2,1)S(1)}, bf16[128,1024]{1,0:T(8,128)(2,1)S(1)}, u32[]{:S(2)}, u32[]{:S(2)}) collective-permute-start(bf16[128,1024]{1,0:T(8,128)(2,1)S(1)} %collective-permute-done.10.refs_1_), channel_id=1, source_target_pairs={{0,2},{1,63},{2,4},{3,1},{4,6},{5,3},{6,8},{7,5},{8,10},{9,7},{10,... | collective-permute-start | bytes 786440 | tf_op jit(solution)/shard_map/ppermute | solution.py:315
  41.8 0.3 collective-permute-done.15.refs_2_
  42.1 0.6 visit.8
  42.7 2.8 %collective-permute-start.16 = (bf16[136,1024]{1,0:T(8,128)(2,1)S(1)}, bf16[136,1024]{1,0:T(8,128)(2,1)S(1)}, u32[]{:S(2)}, u32[]{:S(2)}) collective-permute-start(bf16[136,1024]{1,0:T(8,128)(2,1)S(1)} %get-tuple-element.38), channel_id=1, source_target_pairs={{0,2},{1,63},{2,4},{3,1},{4,6},{5,3},{6,8},{7,5},{8,10},{9,7},{10,... | collective-permute-start | bytes 835592 | tf_op jit(solution)/shard_map/ppermute | solution.py:315
  45.5 2.1 %collective-permute-start.6 = (bf16[128,1024]{1,0:T(8,128)(2,1)S(1)}, bf16[128,1024]{1,0:T(8,128)(2,1)S(1)}, u32[]{:S(2)}, u32[]{:S(2)}) collective-permute-start(bf16[128,1024]{1,0:T(8,128)(2,1)S(1)} %collective-permute-done.5.refs_0_), channel_id=1, source_target_pairs={{0,2},{1,63},{2,4},{3,1},{4,6},{5,3},{6,8},{7,5},{8,10},{9,7},{10,... | collective-permute-start | bytes 786440 | tf_op jit(solution)/shard_map/ppermute | solution.py:315
  47.7 2.7 %collective-permute-start.12 = (bf16[128,1024]{1,0:T(8,128)(2,1)S(1)}, bf16[128,1024]{1,0:T(8,128)(2,1)S(1)}, u32[]{:S(2)}, u32[]{:S(2)}) collective-permute-start(bf16[128,1024]{1,0:T(8,128)(2,1)S(1)} %collective-permute-done.11.refs_1_), channel_id=1, source_target_pairs={{0,2},{1,63},{2,4},{3,1},{4,6},{5,3},{6,8},{7,5},{8,10},{9,7},{10,... | collective-permute-start | bytes 786440 | tf_op jit(solution)/shard_map/ppermute | solution.py:315
  50.4 0.3 collective-permute-done.16.refs_2_
  50.7 0.6 visit.9
  51.3 3.0 %collective-permute-start.17 = (bf16[136,1024]{1,0:T(8,128)(2,1)S(1)}, bf16[136,1024]{1,0:T(8,128)(2,1)S(1)}, u32[]{:S(2)}, u32[]{:S(2)}) collective-permute-start(bf16[136,1024]{1,0:T(8,128)(2,1)S(1)} %get-tuple-element.39), channel_id=1, source_target_pairs={{0,2},{1,63},{2,4},{3,1},{4,6},{5,3},{6,8},{7,5},{8,10},{9,7},{10,... | collective-permute-start | bytes 835592 | tf_op jit(solution)/shard_map/ppermute | solution.py:315
  54.3 1.9 %collective-permute-start.7 = (bf16[128,1024]{1,0:T(8,128)(2,1)S(1)}, bf16[128,1024]{1,0:T(8,128)(2,1)S(1)}, u32[]{:S(2)}, u32[]{:S(2)}) collective-permute-start(bf16[128,1024]{1,0:T(8,128)(2,1)S(1)} %collective-permute-done.6.refs_0_), channel_id=1, source_target_pairs={{0,2},{1,63},{2,4},{3,1},{4,6},{5,3},{6,8},{7,5},{8,10},{9,7},{10,... | collective-permute-start | bytes 786440 | tf_op jit(solution)/shard_map/ppermute | solution.py:315
  56.3 2.7 %collective-permute-start.13 = (bf16[128,1024]{1,0:T(8,128)(2,1)S(1)}, bf16[128,1024]{1,0:T(8,128)(2,1)S(1)}, u32[]{:S(2)}, u32[]{:S(2)}) collective-permute-start(bf16[128,1024]{1,0:T(8,128)(2,1)S(1)} %collective-permute-done.12.refs_1_), channel_id=1, source_target_pairs={{0,2},{1,63},{2,4},{3,1},{4,6},{5,3},{6,8},{7,5},{8,10},{9,7},{10,... | collective-permute-start | bytes 786440 | tf_op jit(solution)/shard_map/ppermute | solution.py:315
  59.0 0.3 collective-permute-done.17.refs_2_
  59.3 0.6 visit.10
  59.9 2.8 %collective-permute-start.18 = (bf16[136,1024]{1,0:T(8,128)(2,1)S(1)}, bf16[136,1024]{1,0:T(8,128)(2,1)S(1)}, u32[]{:S(2)}, u32[]{:S(2)}) collective-permute-start(bf16[136,1024]{1,0:T(8,128)(2,1)S(1)} %get-tuple-element.40), channel_id=1, source_target_pairs={{0,2},{1,63},{2,4},{3,1},{4,6},{5,3},{6,8},{7,5},{8,10},{9,7},{10,... | collective-permute-start | bytes 835592 | tf_op jit(solution)/shard_map/ppermute | solution.py:315
  62.7 2.1 %collective-permute-start.8 = (bf16[128,1024]{1,0:T(8,128)(2,1)S(1)}, bf16[128,1024]{1,0:T(8,128)(2,1)S(1)}, u32[]{:S(2)}, u32[]{:S(2)}) collective-permute-start(bf16[128,1024]{1,0:T(8,128)(2,1)S(1)} %collective-permute-done.7.refs_0_), channel_id=1, source_target_pairs={{0,2},{1,63},{2,4},{3,1},{4,6},{5,3},{6,8},{7,5},{8,10},{9,7},{10,... | collective-permute-start | bytes 786440 | tf_op jit(solution)/shard_map/ppermute | solution.py:315
  64.9 2.7 %collective-permute-start.14 = (bf16[128,1024]{1,0:T(8,128)(2,1)S(1)}, bf16[128,1024]{1,0:T(8,128)(2,1)S(1)}, u32[]{:S(2)}, u32[]{:S(2)}) collective-permute-start(bf16[128,1024]{1,0:T(8,128)(2,1)S(1)} %collective-permute-done.13.refs_1_), channel_id=1, source_target_pairs={{0,2},{1,63},{2,4},{3,1},{4,6},{5,3},{6,8},{7,5},{8,10},{9,7},{10,... | collective-permute-start | bytes 786440 | tf_op jit(solution)/shard_map/ppermute | solution.py:315
  67.6 0.3 collective-permute-done.18.refs_2_
  67.9 0.6 visit.11
  68.5 2.8 %collective-permute-start.19 = (bf16[136,1024]{1,0:T(8,128)(2,1)S(1)}, bf16[136,1024]{1,0:T(8,128)(2,1)S(1)}, u32[]{:S(2)}, u32[]{:S(2)}) collective-permute-start(bf16[136,1024]{1,0:T(8,128)(2,1)S(1)} %get-tuple-element.41), channel_id=1, source_target_pairs={{0,2},{1,63},{2,4},{3,1},{4,6},{5,3},{6,8},{7,5},{8,10},{9,7},{10,... | collective-permute-start | bytes 835592 | tf_op jit(solution)/shard_map/ppermute | solution.py:315
  71.3 2.1 %collective-permute-start.24 = (bf16[128,1024]{1,0:T(8,128)(2,1)S(1)}, bf16[128,1024]{1,0:T(8,128)(2,1)S(1)}, u32[]{:S(2)}, u32[]{:S(2)}) collective-permute-start(bf16[128,1024]{1,0:T(8,128)(2,1)S(1)} %collective-permute-done.8.refs_0_), channel_id=1, source_target_pairs={{0,2},{1,63},{2,4},{3,1},{4,6},{5,3},{6,8},{7,5},{8,10},{9,7},{10,... | collective-permute-start | bytes 786440 | tf_op jit(solution)/shard_map/ppermute | solution.py:315
  73.5 2.7 %collective-permute-start.25 = (bf16[128,1024]{1,0:T(8,128)(2,1)S(1)}, bf16[128,1024]{1,0:T(8,128)(2,1)S(1)}, u32[]{:S(2)}, u32[]{:S(2)}) collective-permute-start(bf16[128,1024]{1,0:T(8,128)(2,1)S(1)} %collective-permute-done.14.refs_1_), channel_id=1, source_target_pairs={{0,2},{1,63},{2,4},{3,1},{4,6},{5,3},{6,8},{7,5},{8,10},{9,7},{10,... | collective-permute-start | bytes 786440 | tf_op jit(solution)/shard_map/ppermute | solution.py:315
  76.2 0.3 collective-permute-done.19.refs_2_
  76.5 0.6 visit.12
  77.1 2.8 %collective-permute-start.20 = (bf16[136,1024]{1,0:T(8,128)(2,1)S(1)}, bf16[136,1024]{1,0:T(8,128)(2,1)S(1)}, u32[]{:S(2)}, u32[]{:S(2)}) collective-permute-start(bf16[136,1024]{1,0:T(8,128)(2,1)S(1)} %get-tuple-element.42), channel_id=1, source_target_pairs={{0,2},{1,63},{2,4},{3,1},{4,6},{5,3},{6,8},{7,5},{8,10},{9,7},{10,... | collective-permute-start | bytes 835592 | tf_op jit(solution)/shard_map/ppermute | solution.py:315
  79.9 2.4 %collective-permute-start.27 = (bf16[128,1024]{1,0:T(8,128)(2,1)S(1)}, bf16[128,1024]{1,0:T(8,128)(2,1)S(1)}, u32[]{:S(2)}, u32[]{:S(2)}) collective-permute-start(bf16[128,1024]{1,0:T(8,128)(2,1)S(1)} %collective-permute-done.24.refs_0_), channel_id=1, source_target_pairs={{0,3},{1,62},{2,5},{3,0},{4,7},{5,2},{6,9},{7,4},{8,11},{9,6},{10,... | collective-permute-start | bytes 786440 | tf_op jit(solution)/shard_map/ppermute | solution.py:315
  82.3 2.4 %collective-permute-start.28 = (bf16[128,1024]{1,0:T(8,128)(2,1)S(1)}, bf16[128,1024]{1,0:T(8,128)(2,1)S(1)}, u32[]{:S(2)}, u32[]{:S(2)}) collective-permute-start(bf16[128,1024]{1,0:T(8,128)(2,1)S(1)} %collective-permute-done.25.refs_1_), channel_id=1, source_target_pairs={{0,3},{1,62},{2,5},{3,0},{4,7},{5,2},{6,9},{7,4},{8,11},{9,6},{10,... | collective-permute-start | bytes 786440 | tf_op jit(solution)/shard_map/ppermute | solution.py:315
  84.7 0.4 collective-permute-done.20.refs_2_
  85.1 0.6 visit.13
  85.7 2.8 %collective-permute-start.21 = (bf16[136,1024]{1,0:T(8,128)(2,1)S(1)}, bf16[136,1024]{1,0:T(8,128)(2,1)S(1)}, u32[]{:S(2)}, u32[]{:S(2)}) collective-permute-start(bf16[136,1024]{1,0:T(8,128)(2,1)S(1)} %get-tuple-element.43), channel_id=1, source_target_pairs={{0,2},{1,63},{2,4},{3,1},{4,6},{5,3},{6,8},{7,5},{8,10},{9,7},{10,... | collective-permute-start | bytes 835592 | tf_op jit(solution)/shard_map/ppermute | solution.py:315
  88.5 1.0 collective-permute-done.27.refs_0_.refs_1_
  89.5 2.8 %collective-permute-done.28.refs_1_.refs_2_ = bf16[128,1024]{1,0:T(8,128)(2,1)S(1)} collective-permute-done((bf16[128,1024]{1,0:T(8,128)(2,1)S(1)}, bf16[128,1024]{1,0:T(8,128)(2,1)S(1)}, u32[]{:S(2)}, u32[]{:S(2)}) %collective-permute-start.28) | collective-permute-done | bytes 262176 | tf_op jit(solution)/shard_map/ppermute | solution.py:315
  92.3 0.1 collective-permute-start.29
  92.5 1.2 collective-permute-done.21.piece_ref.refs_2_
  93.7 2.6 %collective-permute-start.23 = (bf16[136,1024]{1,0:T(8,128)(2,1)S(1)}, bf16[136,1024]{1,0:T(8,128)(2,1)S(1)}, u32[]{:S(2)}, u32[]{:S(2)}) collective-permute-start(bf16[136,1024]{1,0:T(8,128)(2,1)S(1)} %collective-permute-done.21.piece_ref.refs_2_), channel_id=1, source_target_pairs={{0,3},{1,62},{2,5},{3,0},{4,7},{5,2},{6,9},{7,4},{8,11},{9,6},{10,... | collective-permute-start | bytes 835592 | tf_op jit(solution)/shard_map/ppermute | solution.py:315
  96.3 0.7 collective-permute-start.22
  97.1 0.1 lay.13
  97.3 0.1 lay.14
  97.4 0.1 lay.15
  97.5 0.1 lay.16
  97.7 0.1 lay.17
  97.8 1.6 %collective-permute-start.26 = (s32[1,384]{1,0:T(1,128)S(1)}, s32[1,384]{1,0:T(1,128)S(1)}, u32[]{:S(2)}, u32[]{:S(2)}) collective-permute-start(s32[1,384]{1,0:T(1,128)S(1)} %decode.1.refs_3_), channel_id=1, source_target_pairs={{0,2},{1,63},{2,4},{3,1},{4,6},{5,3},{6,8},{7,5},{8,10},{9,7},{10,... | collective-permute-start | bytes 4616 | tf_op jit(solution)/shard_map/ppermute | solution.py:315
  99.4 0.6 late_visit.1
  100.0 2.5 %collective-permute-start.30 = (f32[1,384]{1,0:T(1,128)S(1)}, f32[1,384]{1,0:T(1,128)S(1)}, u32[]{:S(2)}, u32[]{:S(2)}) collective-permute-start(f32[1,384]{1,0:T(1,128)S(1)} %late_visit.1), channel_id=1, source_target_pairs={{0,3},{1,62},{2,5},{3,0},{4,7},{5,2},{6,9},{7,4},{8,11},{9,6},{10,... | collective-permute-start | bytes 4616 | tf_op jit(solution)/shard_map/ppermute | solution.py:315
  102.6 0.1 lay.18
  102.7 2.0 %meet.3.refs_20_ = f32[1,256]{1,0:T(1,128)S(1)} custom-call(s32[1,384]{1,0:T(1,128)S(1)} %collective-permute-done.22.refs_0_, bf16[128,1024]{1,0:T(8,128)(2,1)S(1)} %collective-permute-done.27.refs_0_.refs_1_, bf16[128,1024]{1,0:T(8,128)(2,1)S(1)} %collective-permute-done.28.refs_1_.refs_2_, bf16[384,1024]{1,0:T(8,128)(2,1)S(1)} %get-tuple-element.36.own_ref.refs_3_.refs_2_, ...), custom_call_target="tpu_custom_call" | custom-call | flops 1610612736 | bytes 6815744 | tf_op jit(solution)/shard_map/meet/pallas_call | solution.py:240
  104.8 0.3 meet.4.refs_21_
  105.1 2.6 %meet.5 = f32[32,1,384]{2,1,0:T(1,128)} custom-call(s32[1,384]{1,0:T(1,128)S(1)} %collective-permute-done.22.refs_0_, bf16[136,1024]{1,0:T(8,128)(2,1)S(1)} %collective-permute-done.23.refs_1_, bf16[384,1024]{1,0:T(8,128)(2,1)S(1)} %get-tuple-element.36.own_ref.refs_3_.refs_2_, s32[384,128]{1,0:T(8,128)S(1)} %columns.1.own_columns_ref.refs_4_.refs_3_, ...), custom_call_target="tpu_custom_call" | custom-call | flops 909115392 | bytes 6963200 | tf_op jit(solution)/shard_map/meet/pallas_call | solution.py:240
  107.7 12.6 %all-to-all-start = ((f32[32,1,384]{2,1,0:T(1,128)}), f32[32,1,384]{2,1,0:T(1,128)S(1)}, u32[]{:S(2)}, u32[]{:S(2)}) async-start(f32[32,1,384]{2,1,0:T(1,128)} %meet.5), calls=%async_computation | async-start | bytes 98304 | tf_op jit(solution)/shard_map/all_to_all | solution.py:352
  120.3 24.2 %all-to-all-done = f32[32,1,384]{2,1,0:T(1,128)S(1)} async-done(((f32[32,1,384]{2,1,0:T(1,128)}), f32[32,1,384]{2,1,0:T(1,128)S(1)}, u32[]{:S(2)}, u32[]{:S(2)}) %all-to-all-start) | async-done | bytes 49184 | tf_op jit(solution)/shard_map/all_to_all | solution.py:352
  144.4 0.4 collective-permute-start.31
  145.6 0.2 collective-permute-done.31.theirs_ref
  145.7 1.2 finish.1
  (34 shorter events, 1.1 us)
Async XLA Ops:
  0.6 1.0 copy-start
  1.8 24.3 %collective-permute-start = (bf16[128,1024]{1,0:T(8,128)(2,1)S(1)}, bf16[128,1024]{1,0:T(8,128)(2,1)S(1)}, u32[]{:S(2)}, u32[]{:S(2)}) collective-permute-start(bf16[128,1024]{1,0:T(8,128)(2,1)S(1)} %get-tuple-element.34.refs_0_), channel_id=1, source_target_pairs={{0,1},{1,0},{2,3},{3,2},{4,5},{5,4},{6,7},{7,6},{8,9},{9,8},{10,11... | collective-permute-start | bytes 786440 | tf_op jit(solution)/shard_map/ppermute | solution.py:318
  22.3 7.1 %collective-permute-start.3 = (bf16[128,1024]{1,0:T(8,128)(2,1)S(1)}, bf16[128,1024]{1,0:T(8,128)(2,1)S(1)}, u32[]{:S(2)}, u32[]{:S(2)}) collective-permute-start(bf16[128,1024]{1,0:T(8,128)(2,1)S(1)} %get-tuple-element.34.refs_0_), channel_id=1, source_target_pairs={{0,2},{1,63},{2,4},{3,1},{4,6},{5,3},{6,8},{7,5},{8,10},{9,7},{10,... | collective-permute-start | bytes 786440 | tf_op jit(solution)/shard_map/ppermute | solution.py:315
  26.1 1.3 copy-start.1
  26.2 6.4 %collective-permute-start.9 = (bf16[128,1024]{1,0:T(8,128)(2,1)S(1)}, bf16[128,1024]{1,0:T(8,128)(2,1)S(1)}, u32[]{:S(2)}, u32[]{:S(2)}) collective-permute-start(bf16[128,1024]{1,0:T(8,128)(2,1)S(1)} %lay.11.refs_1_), channel_id=1, source_target_pairs={{0,2},{1,63},{2,4},{3,1},{4,6},{5,3},{6,8},{7,5},{8,10},{9,7},{10,... | collective-permute-start | bytes 786440 | tf_op jit(solution)/shard_map/ppermute | solution.py:315
  27.4 8.1 %collective-permute-start.1 = (bf16[64,1024]{1,0:T(8,128)(2,1)S(1)}, bf16[64,1024]{1,0:T(8,128)(2,1)S(1)}, u32[]{:S(2)}, u32[]{:S(2)}) collective-permute-start(bf16[64,1024]{1,0:T(8,128)(2,1)S(1)} %get-tuple-element.35.refs_1_.refs_0_), channel_id=1, source_target_pairs={{0,1},{1,0},{2,3},{3,2},{4,5},{5,4},{6,7},{7,6},{8,9},{9,8},{10,11... | collective-permute-start | bytes 393224 | tf_op jit(solution)/shard_map/ppermute | solution.py:318
  27.4 7.9 %collective-permute-start.2 = (s32[1,192]{1,0:T(1,128)S(1)}, s32[1,192]{1,0:T(1,128)S(1)}, u32[]{:S(2)}, u32[]{:S(2)}) collective-permute-start(s32[1,192]{1,0:T(1,128)S(1)} %bitcast.10), channel_id=1, source_target_pairs={{0,1},{1,0},{2,3},{3,2},{4,5},{5,4},{6,7},{7,6},{8,9},{9,8},{10,11... | collective-permute-start | bytes 2312 | tf_op jit(solution)/shard_map/ppermute | solution.py:318
  29.4 7.0 %collective-permute-start.4 = (bf16[128,1024]{1,0:T(8,128)(2,1)S(1)}, bf16[128,1024]{1,0:T(8,128)(2,1)S(1)}, u32[]{:S(2)}, u32[]{:S(2)}) collective-permute-start(bf16[128,1024]{1,0:T(8,128)(2,1)S(1)} %collective-permute-done.3.refs_0_), channel_id=1, source_target_pairs={{0,2},{1,63},{2,4},{3,1},{4,6},{5,3},{6,8},{7,5},{8,10},{9,7},{10,... | collective-permute-start | bytes 786440 | tf_op jit(solution)/shard_map/ppermute | solution.py:315
  32.6 6.4 %collective-permute-start.10 = (bf16[128,1024]{1,0:T(8,128)(2,1)S(1)}, bf16[128,1024]{1,0:T(8,128)(2,1)S(1)}, u32[]{:S(2)}, u32[]{:S(2)}) collective-permute-start(bf16[128,1024]{1,0:T(8,128)(2,1)S(1)} %collective-permute-done.9.refs_1_), channel_id=1, source_target_pairs={{0,2},{1,63},{2,4},{3,1},{4,6},{5,3},{6,8},{7,5},{8,10},{9,7},{10,... | collective-permute-start | bytes 786440 | tf_op jit(solution)/shard_map/ppermute | solution.py:315
  36.3 5.8 %collective-permute-start.15 = (bf16[136,1024]{1,0:T(8,128)(2,1)S(1)}, bf16[136,1024]{1,0:T(8,128)(2,1)S(1)}, u32[]{:S(2)}, u32[]{:S(2)}) collective-permute-start(bf16[136,1024]{1,0:T(8,128)(2,1)S(1)} %visit.7), channel_id=1, source_target_pairs={{0,2},{1,63},{2,4},{3,1},{4,6},{5,3},{6,8},{7,5},{8,10},{9,7},{10,... | collective-permute-start | bytes 835592 | tf_op jit(solution)/shard_map/ppermute | solution.py:315
  36.4 9.1 %collective-permute-start.5 = (bf16[128,1024]{1,0:T(8,128)(2,1)S(1)}, bf16[128,1024]{1,0:T(8,128)(2,1)S(1)}, u32[]{:S(2)}, u32[]{:S(2)}) collective-permute-start(bf16[128,1024]{1,0:T(8,128)(2,1)S(1)} %collective-permute-done.4.refs_0_), channel_id=1, source_target_pairs={{0,2},{1,63},{2,4},{3,1},{4,6},{5,3},{6,8},{7,5},{8,10},{9,7},{10,... | collective-permute-start | bytes 786440 | tf_op jit(solution)/shard_map/ppermute | solution.py:315
  39.0 8.7 %collective-permute-start.11 = (bf16[128,1024]{1,0:T(8,128)(2,1)S(1)}, bf16[128,1024]{1,0:T(8,128)(2,1)S(1)}, u32[]{:S(2)}, u32[]{:S(2)}) collective-permute-start(bf16[128,1024]{1,0:T(8,128)(2,1)S(1)} %collective-permute-done.10.refs_1_), channel_id=1, source_target_pairs={{0,2},{1,63},{2,4},{3,1},{4,6},{5,3},{6,8},{7,5},{8,10},{9,7},{10,... | collective-permute-start | bytes 786440 | tf_op jit(solution)/shard_map/ppermute | solution.py:315
  42.7 8.0 %collective-permute-start.16 = (bf16[136,1024]{1,0:T(8,128)(2,1)S(1)}, bf16[136,1024]{1,0:T(8,128)(2,1)S(1)}, u32[]{:S(2)}, u32[]{:S(2)}) collective-permute-start(bf16[136,1024]{1,0:T(8,128)(2,1)S(1)} %get-tuple-element.38), channel_id=1, source_target_pairs={{0,2},{1,63},{2,4},{3,1},{4,6},{5,3},{6,8},{7,5},{8,10},{9,7},{10,... | collective-permute-start | bytes 835592 | tf_op jit(solution)/shard_map/ppermute | solution.py:315
  45.5 8.8 %collective-permute-start.6 = (bf16[128,1024]{1,0:T(8,128)(2,1)S(1)}, bf16[128,1024]{1,0:T(8,128)(2,1)S(1)}, u32[]{:S(2)}, u32[]{:S(2)}) collective-permute-start(bf16[128,1024]{1,0:T(8,128)(2,1)S(1)} %collective-permute-done.5.refs_0_), channel_id=1, source_target_pairs={{0,2},{1,63},{2,4},{3,1},{4,6},{5,3},{6,8},{7,5},{8,10},{9,7},{10,... | collective-permute-start | bytes 786440 | tf_op jit(solution)/shard_map/ppermute | solution.py:315
  47.7 8.6 %collective-permute-start.12 = (bf16[128,1024]{1,0:T(8,128)(2,1)S(1)}, bf16[128,1024]{1,0:T(8,128)(2,1)S(1)}, u32[]{:S(2)}, u32[]{:S(2)}) collective-permute-start(bf16[128,1024]{1,0:T(8,128)(2,1)S(1)} %collective-permute-done.11.refs_1_), channel_id=1, source_target_pairs={{0,2},{1,63},{2,4},{3,1},{4,6},{5,3},{6,8},{7,5},{8,10},{9,7},{10,... | collective-permute-start | bytes 786440 | tf_op jit(solution)/shard_map/ppermute | solution.py:315
  51.3 8.0 %collective-permute-start.17 = (bf16[136,1024]{1,0:T(8,128)(2,1)S(1)}, bf16[136,1024]{1,0:T(8,128)(2,1)S(1)}, u32[]{:S(2)}, u32[]{:S(2)}) collective-permute-start(bf16[136,1024]{1,0:T(8,128)(2,1)S(1)} %get-tuple-element.39), channel_id=1, source_target_pairs={{0,2},{1,63},{2,4},{3,1},{4,6},{5,3},{6,8},{7,5},{8,10},{9,7},{10,... | collective-permute-start | bytes 835592 | tf_op jit(solution)/shard_map/ppermute | solution.py:315
  54.3 8.4 %collective-permute-start.7 = (bf16[128,1024]{1,0:T(8,128)(2,1)S(1)}, bf16[128,1024]{1,0:T(8,128)(2,1)S(1)}, u32[]{:S(2)}, u32[]{:S(2)}) collective-permute-start(bf16[128,1024]{1,0:T(8,128)(2,1)S(1)} %collective-permute-done.6.refs_0_), channel_id=1, source_target_pairs={{0,2},{1,63},{2,4},{3,1},{4,6},{5,3},{6,8},{7,5},{8,10},{9,7},{10,... | collective-permute-start | bytes 786440 | tf_op jit(solution)/shard_map/ppermute | solution.py:315
  56.3 8.6 %collective-permute-start.13 = (bf16[128,1024]{1,0:T(8,128)(2,1)S(1)}, bf16[128,1024]{1,0:T(8,128)(2,1)S(1)}, u32[]{:S(2)}, u32[]{:S(2)}) collective-permute-start(bf16[128,1024]{1,0:T(8,128)(2,1)S(1)} %collective-permute-done.12.refs_1_), channel_id=1, source_target_pairs={{0,2},{1,63},{2,4},{3,1},{4,6},{5,3},{6,8},{7,5},{8,10},{9,7},{10,... | collective-permute-start | bytes 786440 | tf_op jit(solution)/shard_map/ppermute | solution.py:315
  59.9 8.0 %collective-permute-start.18 = (bf16[136,1024]{1,0:T(8,128)(2,1)S(1)}, bf16[136,1024]{1,0:T(8,128)(2,1)S(1)}, u32[]{:S(2)}, u32[]{:S(2)}) collective-permute-start(bf16[136,1024]{1,0:T(8,128)(2,1)S(1)} %get-tuple-element.40), channel_id=1, source_target_pairs={{0,2},{1,63},{2,4},{3,1},{4,6},{5,3},{6,8},{7,5},{8,10},{9,7},{10,... | collective-permute-start | bytes 835592 | tf_op jit(solution)/shard_map/ppermute | solution.py:315
  62.7 8.6 %collective-permute-start.8 = (bf16[128,1024]{1,0:T(8,128)(2,1)S(1)}, bf16[128,1024]{1,0:T(8,128)(2,1)S(1)}, u32[]{:S(2)}, u32[]{:S(2)}) collective-permute-start(bf16[128,1024]{1,0:T(8,128)(2,1)S(1)} %collective-permute-done.7.refs_0_), channel_id=1, source_target_pairs={{0,2},{1,63},{2,4},{3,1},{4,6},{5,3},{6,8},{7,5},{8,10},{9,7},{10,... | collective-permute-start | bytes 786440 | tf_op jit(solution)/shard_map/ppermute | solution.py:315
  64.9 8.6 %collective-permute-start.14 = (bf16[128,1024]{1,0:T(8,128)(2,1)S(1)}, bf16[128,1024]{1,0:T(8,128)(2,1)S(1)}, u32[]{:S(2)}, u32[]{:S(2)}) collective-permute-start(bf16[128,1024]{1,0:T(8,128)(2,1)S(1)} %collective-permute-done.13.refs_1_), channel_id=1, source_target_pairs={{0,2},{1,63},{2,4},{3,1},{4,6},{5,3},{6,8},{7,5},{8,10},{9,7},{10,... | collective-permute-start | bytes 786440 | tf_op jit(solution)/shard_map/ppermute | solution.py:315
  68.5 8.0 %collective-permute-start.19 = (bf16[136,1024]{1,0:T(8,128)(2,1)S(1)}, bf16[136,1024]{1,0:T(8,128)(2,1)S(1)}, u32[]{:S(2)}, u32[]{:S(2)}) collective-permute-start(bf16[136,1024]{1,0:T(8,128)(2,1)S(1)} %get-tuple-element.41), channel_id=1, source_target_pairs={{0,2},{1,63},{2,4},{3,1},{4,6},{5,3},{6,8},{7,5},{8,10},{9,7},{10,... | collective-permute-start | bytes 835592 | tf_op jit(solution)/shard_map/ppermute | solution.py:315
  71.3 8.6 %collective-permute-start.24 = (bf16[128,1024]{1,0:T(8,128)(2,1)S(1)}, bf16[128,1024]{1,0:T(8,128)(2,1)S(1)}, u32[]{:S(2)}, u32[]{:S(2)}) collective-permute-start(bf16[128,1024]{1,0:T(8,128)(2,1)S(1)} %collective-permute-done.8.refs_0_), channel_id=1, source_target_pairs={{0,2},{1,63},{2,4},{3,1},{4,6},{5,3},{6,8},{7,5},{8,10},{9,7},{10,... | collective-permute-start | bytes 786440 | tf_op jit(solution)/shard_map/ppermute | solution.py:315
  73.5 8.8 %collective-permute-start.25 = (bf16[128,1024]{1,0:T(8,128)(2,1)S(1)}, bf16[128,1024]{1,0:T(8,128)(2,1)S(1)}, u32[]{:S(2)}, u32[]{:S(2)}) collective-permute-start(bf16[128,1024]{1,0:T(8,128)(2,1)S(1)} %collective-permute-done.14.refs_1_), channel_id=1, source_target_pairs={{0,2},{1,63},{2,4},{3,1},{4,6},{5,3},{6,8},{7,5},{8,10},{9,7},{10,... | collective-permute-start | bytes 786440 | tf_op jit(solution)/shard_map/ppermute | solution.py:315
  77.1 8.0 %collective-permute-start.20 = (bf16[136,1024]{1,0:T(8,128)(2,1)S(1)}, bf16[136,1024]{1,0:T(8,128)(2,1)S(1)}, u32[]{:S(2)}, u32[]{:S(2)}) collective-permute-start(bf16[136,1024]{1,0:T(8,128)(2,1)S(1)} %get-tuple-element.42), channel_id=1, source_target_pairs={{0,2},{1,63},{2,4},{3,1},{4,6},{5,3},{6,8},{7,5},{8,10},{9,7},{10,... | collective-permute-start | bytes 835592 | tf_op jit(solution)/shard_map/ppermute | solution.py:315
  79.9 9.6 %collective-permute-start.27 = (bf16[128,1024]{1,0:T(8,128)(2,1)S(1)}, bf16[128,1024]{1,0:T(8,128)(2,1)S(1)}, u32[]{:S(2)}, u32[]{:S(2)}) collective-permute-start(bf16[128,1024]{1,0:T(8,128)(2,1)S(1)} %collective-permute-done.24.refs_0_), channel_id=1, source_target_pairs={{0,3},{1,62},{2,5},{3,0},{4,7},{5,2},{6,9},{7,4},{8,11},{9,6},{10,... | collective-permute-start | bytes 786440 | tf_op jit(solution)/shard_map/ppermute | solution.py:315
  82.3 9.9 %collective-permute-start.28 = (bf16[128,1024]{1,0:T(8,128)(2,1)S(1)}, bf16[128,1024]{1,0:T(8,128)(2,1)S(1)}, u32[]{:S(2)}, u32[]{:S(2)}) collective-permute-start(bf16[128,1024]{1,0:T(8,128)(2,1)S(1)} %collective-permute-done.25.refs_1_), channel_id=1, source_target_pairs={{0,3},{1,62},{2,5},{3,0},{4,7},{5,2},{6,9},{7,4},{8,11},{9,6},{10,... | collective-permute-start | bytes 786440 | tf_op jit(solution)/shard_map/ppermute | solution.py:315
  85.7 8.0 %collective-permute-start.21 = (bf16[136,1024]{1,0:T(8,128)(2,1)S(1)}, bf16[136,1024]{1,0:T(8,128)(2,1)S(1)}, u32[]{:S(2)}, u32[]{:S(2)}) collective-permute-start(bf16[136,1024]{1,0:T(8,128)(2,1)S(1)} %get-tuple-element.43), channel_id=1, source_target_pairs={{0,2},{1,63},{2,4},{3,1},{4,6},{5,3},{6,8},{7,5},{8,10},{9,7},{10,... | collective-permute-start | bytes 835592 | tf_op jit(solution)/shard_map/ppermute | solution.py:315
  92.3 12.4 %collective-permute-start.29 = (bf16[192,1024]{1,0:T(8,128)(2,1)S(1)}, bf16[192,1024]{1,0:T(8,128)(2,1)S(1)}, u32[]{:S(2)}, u32[]{:S(2)}) collective-permute-start(bf16[192,1024]{1,0:T(8,128)(2,1)S(1)} %lay.19), channel_id=1, source_target_pairs={{0,1},{1,0},{2,3},{3,2},{4,5},{5,4},{6,7},{7,6},{8,9},{9,8},{10,11... | collective-permute-start | bytes 1179656 | tf_op jit(solution)/shard_map/ppermute | solution.py:318
  93.7 11.4 %collective-permute-start.23 = (bf16[136,1024]{1,0:T(8,128)(2,1)S(1)}, bf16[136,1024]{1,0:T(8,128)(2,1)S(1)}, u32[]{:S(2)}, u32[]{:S(2)}) collective-permute-start(bf16[136,1024]{1,0:T(8,128)(2,1)S(1)} %collective-permute-done.21.piece_ref.refs_2_), channel_id=1, source_target_pairs={{0,3},{1,62},{2,5},{3,0},{4,7},{5,2},{6,9},{7,4},{8,11},{9,6},{10,... | collective-permute-start | bytes 835592 | tf_op jit(solution)/shard_map/ppermute | solution.py:315
  96.3 6.4 %collective-permute-start.22 = (s32[1,384]{1,0:T(1,128)S(1)}, s32[1,384]{1,0:T(1,128)S(1)}, u32[]{:S(2)}, u32[]{:S(2)}) collective-permute-start(s32[1,384]{1,0:T(1,128)S(1)} %decode.1.refs_3_), channel_id=1, source_target_pairs={{0,3},{1,62},{2,5},{3,0},{4,7},{5,2},{6,9},{7,4},{8,11},{9,6},{10,... | collective-permute-start | bytes 4616 | tf_op jit(solution)/shard_map/ppermute | solution.py:315
  97.8 6.9 %collective-permute-start.26 = (s32[1,384]{1,0:T(1,128)S(1)}, s32[1,384]{1,0:T(1,128)S(1)}, u32[]{:S(2)}, u32[]{:S(2)}) collective-permute-start(s32[1,384]{1,0:T(1,128)S(1)} %decode.1.refs_3_), channel_id=1, source_target_pairs={{0,2},{1,63},{2,4},{3,1},{4,6},{5,3},{6,8},{7,5},{8,10},{9,7},{10,... | collective-permute-start | bytes 4616 | tf_op jit(solution)/shard_map/ppermute | solution.py:315
  100.0 5.1 %collective-permute-start.30 = (f32[1,384]{1,0:T(1,128)S(1)}, f32[1,384]{1,0:T(1,128)S(1)}, u32[]{:S(2)}, u32[]{:S(2)}) collective-permute-start(f32[1,384]{1,0:T(1,128)S(1)} %late_visit.1), channel_id=1, source_target_pairs={{0,3},{1,62},{2,5},{3,0},{4,7},{5,2},{6,9},{7,4},{8,11},{9,6},{10,... | collective-permute-start | bytes 4616 | tf_op jit(solution)/shard_map/ppermute | solution.py:315
  107.7 36.7 %all-to-all-start = ((f32[32,1,384]{2,1,0:T(1,128)}), f32[32,1,384]{2,1,0:T(1,128)S(1)}, u32[]{:S(2)}, u32[]{:S(2)}) async-start(f32[32,1,384]{2,1,0:T(1,128)} %meet.5), calls=%async_computation | async-start | bytes 98304 | tf_op jit(solution)/shard_map/all_to_all | solution.py:352
  144.4 1.3 collective-permute-start.31

commit v4 on v3

--- a/solution.py
+++ b/solution.py
@@ -202,46 +202,27 @@
     )(keys)
 
 
-def meet_kernel(first_row, pieces, blocks, extra, spread, *refs):
-    note_ref = refs[0]
-    count = min(sum(r.shape[0] for r in refs[1 : 1 + pieces]), note_ref.shape[1] - first_row)
-    rows = jnp.concatenate([r[...] for r in refs[1 : 1 + pieces]], axis=0)[:count]
-    at = 1 + pieces
-    row_key = note_ref[:, first_row : first_row + count]
+def meet_kernel(first_row, pieces, keys_ref, *refs):
+    out_ref = refs[-1]
+    count = out_ref.shape[1]
+    rows = jnp.concatenate([r[...] for r in refs[:pieces]], axis=0)[:count]
+    row_key = keys_ref[:, first_row : first_row + count]
     low = row_key & jnp.int32(-label_stride)
     best = jnp.full((1, count), -1.0, jnp.float32)
-    for _ in range(blocks):
+    for at in range(pieces, len(refs) - 1, 2):
         best = best_of(best, row_key, low, rows, refs[at][...], refs[at + 1][...])
-        at += 2
-    if extra:
-        others = jnp.concatenate([r[...] for r in refs[at + 1 : at + 1 + extra]], axis=0)
-        columns = key_columns(refs[at][...])[: others.shape[0]]
-        best = best_of(best, row_key, low, rows, others, columns)
-        at += 1 + extra
-    out_ref = refs[-1]
-    if spread:
-        earlier = jnp.maximum(refs[at][...], refs[at + 1][...])
-        best = jnp.concatenate([earlier, best], axis=1)
-        best = jnp.maximum(best, read_tail(refs[1], best.shape[1])[1])
-        best = jnp.maximum(best, refs[at + 2][...])
-        out_ref[...] = jnp.broadcast_to(best[:, None, :], out_ref.shape)
-    else:
-        out_ref[...] = best
-
-
-def meet(note, first_row, pieces, blocks, extra=(), spread=(), chips=0):
-    count, width = sum(p.shape[0] for p in pieces), pieces[0].shape[1]
-    operands = [note, *pieces]
+    out_ref[...] = best
+
+
+def meet(keys, first_row, count, pieces, blocks):
+    width = pieces[0].shape[1]
+    operands = [keys, *pieces]
     for whole, columns in blocks:
         operands += [whole, columns]
-    operands += [*extra, *spread]
-    others = sum(whole.shape[0] for whole, _ in blocks) + sum(p.shape[0] for p in extra[1:])
-    out = (chips, 1, note.shape[1]) if spread else (1, count)
-    return pl.pallas_call(
-        functools.partial(
-            meet_kernel, first_row, len(pieces), len(blocks), max(len(extra) - 1, 0), bool(spread)
-        ),
-        out_shape=jax.ShapeDtypeStruct(out, jnp.float32),
+    others = sum(whole.shape[0] for whole, _ in blocks)
+    return pl.pallas_call(
+        functools.partial(meet_kernel, first_row, len(pieces)),
+        out_shape=jax.ShapeDtypeStruct((1, count), jnp.float32),
         in_specs=[VMEM] * len(operands),
         out_specs=VMEM,
         compiler_params=PARAMS,
@@ -254,14 +235,55 @@
     )(*operands)
 
 
-def finish_kernel(width, place_ref, limit_ref, mine_ref, theirs_ref, best_ref, share_ref):
+def join_kernel(pieces, keys_ref, facing_keys_ref, facing_ref, late_ref, front_ref, back_ref, *refs):
+    out_ref = refs[-1]
+    keys = keys_ref[...]
+    rows = jnp.concatenate([r[...] for r in refs[:pieces]], axis=0)[: keys.shape[1]]
+    low = keys & jnp.int32(-label_stride)
+    columns = key_columns(facing_keys_ref[...])[: facing_ref.shape[0]]
+    best = jnp.concatenate([front_ref[...], back_ref[...]], axis=1)
+    best = jnp.maximum(best, late_ref[...])
+    best = best_of(best, keys, low, rows, facing_ref[...], columns)
+    out_ref[...] = jnp.broadcast_to(best[:, None, :], out_ref.shape)
+
+
+def join(keys, facing_keys, facing, late, front, back, pieces, chips):
+    total = keys.shape[1]
+    operands = [keys, facing_keys, facing, late, front, back, *pieces]
+    return pl.pallas_call(
+        functools.partial(join_kernel, len(pieces)),
+        out_shape=jax.ShapeDtypeStruct((chips, 1, total), jnp.float32),
+        in_specs=[VMEM] * len(operands),
+        out_specs=VMEM,
+        compiler_params=PARAMS,
+        name="join",
+    )(*operands)
+
+
+def limit_kernel(root, index_ref, limit_ref):
+    limit = jnp.zeros(limit_ref.shape, jnp.float32)
+    for entry in range(LIMITS):
+        value = jnp.float32((2.0 + 0.5 * entry) / root)
+        limit = jnp.where(index_ref[0] == entry, value, limit)
+    limit_ref[...] = limit
+
+
+def limit_of(limit_index, root):
+    return pl.pallas_call(
+        functools.partial(limit_kernel, root),
+        out_shape=jax.ShapeDtypeStruct((1, 128), jnp.float32),
+        in_specs=[pl.BlockSpec(memory_space=pltpu.SMEM)],
+        out_specs=VMEM,
+        compiler_params=PARAMS,
+        name="limit",
+    )(limit_index)
+
+
+def finish_kernel(width, limit_ref, mine_ref, theirs_ref, best_ref, share_ref):
     blocks, rows = mine_ref.shape
     half = rows // 2
-    core, blk = place_ref[0], place_ref[1]
-    k = limit_ref[0]
-    limit = jnp.float32(0.0)
-    for entry in range(LIMITS):
-        limit = jnp.where(k == entry, jnp.float32((2.0 + 0.5 * entry) / width), limit)
+    core, blk = lax.axis_index("sub"), lax.axis_index("blk")
+    limit = limit_ref[:, :1]
     quarter = blocks // 4
 
     def turned(x, by):
@@ -283,20 +305,19 @@
     best_ref[...] = own[:, :half]
 
 
-def finish(place, limit_index, mine, theirs, width):
-    _, rows = mine.shape
-    smem = pl.BlockSpec(memory_space=pltpu.SMEM)
+def finish(limit, mine, theirs, width):
+    rows = mine.shape[1]
     return pl.pallas_call(
         functools.partial(finish_kernel, width),
         out_shape=[
             jax.ShapeDtypeStruct((1, rows // 2), jnp.float32),
             jax.ShapeDtypeStruct((1, 1), jnp.float32),
         ],
-        in_specs=[smem, smem, VMEM, VMEM],
+        in_specs=[VMEM] * 3,
         out_specs=[VMEM, VMEM],
         compiler_params=PARAMS,
         name="finish",
-    )(place, limit_index, mine, theirs)
+    )(limit, mine, theirs)
 
 
 def program(embeddings, member_key, limit_index):
@@ -344,15 +365,18 @@
     late = send(late, 1, True)
     block = [send(b, 1, True) for b in block]
     (first,) = lay(block[:-1], [(0, rows)])
-    facing = [next_keys, across(first)]
     split = size * (PIECES - 1)
-    early = [meet(last_keys, 0, block[:-1], held), meet(last_keys, 0, block[:-1], [], facing)]
-    everyone = meet(last_keys, split, block[-1:], held, facing, (*early, late), chips)
-
+    front = meet(last_keys, 0, split, block[:-1], held)
+    first, front = lax.optimization_barrier((first, front))
+    facing = across(first)
+    back = meet(last_keys, split, size, block[-1:], held)
+    everyone = join(last_keys, next_keys, facing, late, front, back, block, chips)
+
+    limit = limit_of(limit_index, math.sqrt(width))
     gathered = lax.all_to_all(everyone, "blk", 0, 0, tiled=True).reshape(chips, -1)
     other_side = across(gathered)
-    place = jnp.stack([lax.axis_index("sub"), lax.axis_index("blk")]).astype(jnp.int32)
-    best, share = finish(place, limit_index, gathered, other_side, math.sqrt(width))
+    root = math.sqrt(width)
+    best, share = finish(limit, gathered, other_side, root)
     return (best.reshape(-1), share.reshape(1))
 
 

time: 147 us -> 144 us (0.980)
  blocking collectives: 0 us -> 35.4 us
  waiting for transfers between devices: 33.2 us -> 8.58 us
  starting transfers between devices: 98.7 us -> 85.9 us
    all_to_all x0 -> x1, blocking collectives: none -> 35.4 us  [program(): lax.all_to_all(everyone, 'blk', 0, 0, tiled=True).reshape(chips, -1)]
    all_to_all x1 -> x0, waiting for transfers between devices: 24.2 us -> none  [program(): lax.all_to_all(everyone, 'blk', 0, 0, tiled=True).reshape(chips, -1)]
    all_to_all x1 -> x0, starting transfers between devices: 12.6 us -> none  [program(): lax.all_to_all(everyone, 'blk', 0, 0, tiled=True).reshape(chips, -1)]
    pallas_call x3 -> x4, Pallas kernels: 4.93 us -> 4.31 us  [the longest x2 3.84 us: meet(): pl.pallas_call(functools.partial(meet_kernel, first_row, len(pieces)), ou...]
  transfers between devices with their start and end apart: 33 -> 32, of which waited for: 16 -> 12; matrix products, arithmetic and copies ran while one was open for 0% -> 0% of each run, Pallas kernels for 6% -> 6%
where the time goes in v4:
time: 144 us
  starting transfers between devices  85.9 us (60%)
  blocking collectives  35.4 us (25%)
  Pallas kernels  11.3 us (8%)
  waiting for transfers between devices  8.58 us (6%)
  between operations  1.49 us (1%)
    ppermute x27, starting transfers between devices, send(): return lax.ppermute(x, ('blk', 'sub'), moves(by, change))  64.3 us
    all_to_all x1, blocking collectives, program(): lax.all_to_all(everyone, 'blk', 0, 0, tiled=True).reshape(chips, -1)  35.4 us
    ppermute x5, starting transfers between devices, across(): return lax.ppermute(x, 'sub', [(0, 1), (1, 0)])  21.6 us
    ppermute x27, waiting for transfers between devices, send(): return lax.ppermute(x, ('blk', 'sub'), moves(by, change))  7.52 us
    pallas_call x7, Pallas kernels, visit(): pl.pallas_call(functools.partial(visit_kernel, begins, len(pieces)), out_...  4.28 us
    pallas_call x2, Pallas kernels, meet(): pl.pallas_call(functools.partial(meet_kernel, first_row, len(pieces)), ou...  3.84 us
  transfers between devices with their start and end apart: 32, of which 12 were waited for; matrix products, arithmetic and copies ran while one was open for 0% of the time, Pallas kernels for 6%

profile of v4, /device:TPU:37, one launch (start us, length us, event | category | flops | bytes accessed | tf_op | source)
XLA Modules:
  0.0 143.7 jit_solution(15048663787151654036)
XLA Ops:
  0.6 1.0 copy-done
  1.6 0.2 normalize.1
  1.8 20.5 %collective-permute-start = (bf16[128,1024]{1,0:T(8,128)(2,1)S(1)}, bf16[128,1024]{1,0:T(8,128)(2,1)S(1)}, u32[]{:S(2)}, u32[]{:S(2)}) collective-permute-start(bf16[128,1024]{1,0:T(8,128)(2,1)S(1)} %get-tuple-element.36.refs_0_), channel_id=1, source_target_pairs={{0,1},{1,0},{2,3},{3,2},{4,5},{5,4},{6,7},{7,6},{8,9},{9,8},{10,11... | collective-permute-start | bytes 786440 | tf_op jit(solution)/shard_map/ppermute | solution.py:339
  22.3 3.8 %collective-permute-start.3 = (bf16[128,1024]{1,0:T(8,128)(2,1)S(1)}, bf16[128,1024]{1,0:T(8,128)(2,1)S(1)}, u32[]{:S(2)}, u32[]{:S(2)}) collective-permute-start(bf16[128,1024]{1,0:T(8,128)(2,1)S(1)} %get-tuple-element.36.refs_0_), channel_id=1, source_target_pairs={{0,2},{1,63},{2,4},{3,1},{4,6},{5,3},{6,8},{7,5},{8,10},{9,7},{10,... | collective-permute-start | bytes 786440 | tf_op jit(solution)/shard_map/ppermute | solution.py:336
  26.2 1.3 collective-permute-start.9
  27.4 0.5 collective-permute-start.2
  27.9 0.8 collective-permute-done.2
  29.1 0.6 visit.7
  29.7 0.6 collective-permute-start.15
  30.3 2.2 %collective-permute-start.4 = (bf16[128,1024]{1,0:T(8,128)(2,1)S(1)}, bf16[128,1024]{1,0:T(8,128)(2,1)S(1)}, u32[]{:S(2)}, u32[]{:S(2)}) collective-permute-start(bf16[128,1024]{1,0:T(8,128)(2,1)S(1)} %collective-permute-done.3.refs_0_), channel_id=1, source_target_pairs={{0,2},{1,63},{2,4},{3,1},{4,6},{5,3},{6,8},{7,5},{8,10},{9,7},{10,... | collective-permute-start | bytes 786440 | tf_op jit(solution)/shard_map/ppermute | solution.py:336
  32.6 2.8 %collective-permute-start.10 = (bf16[128,1024]{1,0:T(8,128)(2,1)S(1)}, bf16[128,1024]{1,0:T(8,128)(2,1)S(1)}, u32[]{:S(2)}, u32[]{:S(2)}) collective-permute-start(bf16[128,1024]{1,0:T(8,128)(2,1)S(1)} %collective-permute-done.9.refs_1_), channel_id=1, source_target_pairs={{0,2},{1,63},{2,4},{3,1},{4,6},{5,3},{6,8},{7,5},{8,10},{9,7},{10,... | collective-permute-start | bytes 786440 | tf_op jit(solution)/shard_map/ppermute | solution.py:336
  35.4 0.1 collective-permute-done.15.refs_2_
  35.5 0.6 visit.8
  36.1 3.0 %collective-permute-start.16 = (bf16[136,1024]{1,0:T(8,128)(2,1)S(1)}, bf16[136,1024]{1,0:T(8,128)(2,1)S(1)}, u32[]{:S(2)}, u32[]{:S(2)}) collective-permute-start(bf16[136,1024]{1,0:T(8,128)(2,1)S(1)} %get-tuple-element.40), channel_id=1, source_target_pairs={{0,2},{1,63},{2,4},{3,1},{4,6},{5,3},{6,8},{7,5},{8,10},{9,7},{10,... | collective-permute-start | bytes 835592 | tf_op jit(solution)/shard_map/ppermute | solution.py:336
  39.1 2.1 %collective-permute-start.5 = (bf16[128,1024]{1,0:T(8,128)(2,1)S(1)}, bf16[128,1024]{1,0:T(8,128)(2,1)S(1)}, u32[]{:S(2)}, u32[]{:S(2)}) collective-permute-start(bf16[128,1024]{1,0:T(8,128)(2,1)S(1)} %collective-permute-done.4.refs_0_), channel_id=1, source_target_pairs={{0,2},{1,63},{2,4},{3,1},{4,6},{5,3},{6,8},{7,5},{8,10},{9,7},{10,... | collective-permute-start | bytes 786440 | tf_op jit(solution)/shard_map/ppermute | solution.py:336
  41.2 2.8 %collective-permute-start.11 = (bf16[128,1024]{1,0:T(8,128)(2,1)S(1)}, bf16[128,1024]{1,0:T(8,128)(2,1)S(1)}, u32[]{:S(2)}, u32[]{:S(2)}) collective-permute-start(bf16[128,1024]{1,0:T(8,128)(2,1)S(1)} %collective-permute-done.10.refs_1_), channel_id=1, source_target_pairs={{0,2},{1,63},{2,4},{3,1},{4,6},{5,3},{6,8},{7,5},{8,10},{9,7},{10,... | collective-permute-start | bytes 786440 | tf_op jit(solution)/shard_map/ppermute | solution.py:336
  44.0 0.1 collective-permute-done.16.refs_2_
  44.1 0.6 visit.9
  44.7 3.0 %collective-permute-start.17 = (bf16[136,1024]{1,0:T(8,128)(2,1)S(1)}, bf16[136,1024]{1,0:T(8,128)(2,1)S(1)}, u32[]{:S(2)}, u32[]{:S(2)}) collective-permute-start(bf16[136,1024]{1,0:T(8,128)(2,1)S(1)} %get-tuple-element.41), channel_id=1, source_target_pairs={{0,2},{1,63},{2,4},{3,1},{4,6},{5,3},{6,8},{7,5},{8,10},{9,7},{10,... | collective-permute-start | bytes 835592 | tf_op jit(solution)/shard_map/ppermute | solution.py:336
  47.7 2.1 %collective-permute-start.6 = (bf16[128,1024]{1,0:T(8,128)(2,1)S(1)}, bf16[128,1024]{1,0:T(8,128)(2,1)S(1)}, u32[]{:S(2)}, u32[]{:S(2)}) collective-permute-start(bf16[128,1024]{1,0:T(8,128)(2,1)S(1)} %collective-permute-done.5.refs_0_), channel_id=1, source_target_pairs={{0,2},{1,63},{2,4},{3,1},{4,6},{5,3},{6,8},{7,5},{8,10},{9,7},{10,... | collective-permute-start | bytes 786440 | tf_op jit(solution)/shard_map/ppermute | solution.py:336
  49.8 2.8 %collective-permute-start.12 = (bf16[128,1024]{1,0:T(8,128)(2,1)S(1)}, bf16[128,1024]{1,0:T(8,128)(2,1)S(1)}, u32[]{:S(2)}, u32[]{:S(2)}) collective-permute-start(bf16[128,1024]{1,0:T(8,128)(2,1)S(1)} %collective-permute-done.11.refs_1_), channel_id=1, source_target_pairs={{0,2},{1,63},{2,4},{3,1},{4,6},{5,3},{6,8},{7,5},{8,10},{9,7},{10,... | collective-permute-start | bytes 786440 | tf_op jit(solution)/shard_map/ppermute | solution.py:336
  52.6 0.1 collective-permute-done.17.refs_2_
  52.7 0.6 visit.10
  53.3 3.0 %collective-permute-start.18 = (bf16[136,1024]{1,0:T(8,128)(2,1)S(1)}, bf16[136,1024]{1,0:T(8,128)(2,1)S(1)}, u32[]{:S(2)}, u32[]{:S(2)}) collective-permute-start(bf16[136,1024]{1,0:T(8,128)(2,1)S(1)} %get-tuple-element.42), channel_id=1, source_target_pairs={{0,2},{1,63},{2,4},{3,1},{4,6},{5,3},{6,8},{7,5},{8,10},{9,7},{10,... | collective-permute-start | bytes 835592 | tf_op jit(solution)/shard_map/ppermute | solution.py:336
  56.3 2.1 %collective-permute-start.7 = (bf16[128,1024]{1,0:T(8,128)(2,1)S(1)}, bf16[128,1024]{1,0:T(8,128)(2,1)S(1)}, u32[]{:S(2)}, u32[]{:S(2)}) collective-permute-start(bf16[128,1024]{1,0:T(8,128)(2,1)S(1)} %collective-permute-done.6.refs_0_), channel_id=1, source_target_pairs={{0,2},{1,63},{2,4},{3,1},{4,6},{5,3},{6,8},{7,5},{8,10},{9,7},{10,... | collective-permute-start | bytes 786440 | tf_op jit(solution)/shard_map/ppermute | solution.py:336
  58.4 2.8 %collective-permute-start.13 = (bf16[128,1024]{1,0:T(8,128)(2,1)S(1)}, bf16[128,1024]{1,0:T(8,128)(2,1)S(1)}, u32[]{:S(2)}, u32[]{:S(2)}) collective-permute-start(bf16[128,1024]{1,0:T(8,128)(2,1)S(1)} %collective-permute-done.12.refs_1_), channel_id=1, source_target_pairs={{0,2},{1,63},{2,4},{3,1},{4,6},{5,3},{6,8},{7,5},{8,10},{9,7},{10,... | collective-permute-start | bytes 786440 | tf_op jit(solution)/shard_map/ppermute | solution.py:336
  61.2 0.1 collective-permute-done.18.refs_2_
  61.3 0.6 visit.11
  61.9 3.0 %collective-permute-start.19 = (bf16[136,1024]{1,0:T(8,128)(2,1)S(1)}, bf16[136,1024]{1,0:T(8,128)(2,1)S(1)}, u32[]{:S(2)}, u32[]{:S(2)}) collective-permute-start(bf16[136,1024]{1,0:T(8,128)(2,1)S(1)} %get-tuple-element.43), channel_id=1, source_target_pairs={{0,2},{1,63},{2,4},{3,1},{4,6},{5,3},{6,8},{7,5},{8,10},{9,7},{10,... | collective-permute-start | bytes 835592 | tf_op jit(solution)/shard_map/ppermute | solution.py:336
  64.9 2.1 %collective-permute-start.8 = (bf16[128,1024]{1,0:T(8,128)(2,1)S(1)}, bf16[128,1024]{1,0:T(8,128)(2,1)S(1)}, u32[]{:S(2)}, u32[]{:S(2)}) collective-permute-start(bf16[128,1024]{1,0:T(8,128)(2,1)S(1)} %collective-permute-done.7.refs_0_), channel_id=1, source_target_pairs={{0,2},{1,63},{2,4},{3,1},{4,6},{5,3},{6,8},{7,5},{8,10},{9,7},{10,... | collective-permute-start | bytes 786440 | tf_op jit(solution)/shard_map/ppermute | solution.py:336
  67.0 2.8 %collective-permute-start.14 = (bf16[128,1024]{1,0:T(8,128)(2,1)S(1)}, bf16[128,1024]{1,0:T(8,128)(2,1)S(1)}, u32[]{:S(2)}, u32[]{:S(2)}) collective-permute-start(bf16[128,1024]{1,0:T(8,128)(2,1)S(1)} %collective-permute-done.13.refs_1_), channel_id=1, source_target_pairs={{0,2},{1,63},{2,4},{3,1},{4,6},{5,3},{6,8},{7,5},{8,10},{9,7},{10,... | collective-permute-start | bytes 786440 | tf_op jit(solution)/shard_map/ppermute | solution.py:336
  69.8 0.1 collective-permute-done.19.refs_2_
  69.9 0.6 visit.12
  70.5 3.0 %collective-permute-start.20 = (bf16[136,1024]{1,0:T(8,128)(2,1)S(1)}, bf16[136,1024]{1,0:T(8,128)(2,1)S(1)}, u32[]{:S(2)}, u32[]{:S(2)}) collective-permute-start(bf16[136,1024]{1,0:T(8,128)(2,1)S(1)} %get-tuple-element.44), channel_id=1, source_target_pairs={{0,2},{1,63},{2,4},{3,1},{4,6},{5,3},{6,8},{7,5},{8,10},{9,7},{10,... | collective-permute-start | bytes 835592 | tf_op jit(solution)/shard_map/ppermute | solution.py:336
  73.5 2.1 %collective-permute-start.24 = (bf16[128,1024]{1,0:T(8,128)(2,1)S(1)}, bf16[128,1024]{1,0:T(8,128)(2,1)S(1)}, u32[]{:S(2)}, u32[]{:S(2)}) collective-permute-start(bf16[128,1024]{1,0:T(8,128)(2,1)S(1)} %collective-permute-done.8.refs_0_), channel_id=1, source_target_pairs={{0,2},{1,63},{2,4},{3,1},{4,6},{5,3},{6,8},{7,5},{8,10},{9,7},{10,... | collective-permute-start | bytes 786440 | tf_op jit(solution)/shard_map/ppermute | solution.py:336
  75.6 2.8 %collective-permute-start.26 = (bf16[128,1024]{1,0:T(8,128)(2,1)S(1)}, bf16[128,1024]{1,0:T(8,128)(2,1)S(1)}, u32[]{:S(2)}, u32[]{:S(2)}) collective-permute-start(bf16[128,1024]{1,0:T(8,128)(2,1)S(1)} %collective-permute-done.14.refs_1_), channel_id=1, source_target_pairs={{0,2},{1,63},{2,4},{3,1},{4,6},{5,3},{6,8},{7,5},{8,10},{9,7},{10,... | collective-permute-start | bytes 786440 | tf_op jit(solution)/shard_map/ppermute | solution.py:336
  78.4 0.1 collective-permute-done.20.refs_2_
  78.5 0.6 visit.13
  79.1 3.0 %collective-permute-start.21 = (bf16[136,1024]{1,0:T(8,128)(2,1)S(1)}, bf16[136,1024]{1,0:T(8,128)(2,1)S(1)}, u32[]{:S(2)}, u32[]{:S(2)}) collective-permute-start(bf16[136,1024]{1,0:T(8,128)(2,1)S(1)} %get-tuple-element.45), channel_id=1, source_target_pairs={{0,2},{1,63},{2,4},{3,1},{4,6},{5,3},{6,8},{7,5},{8,10},{9,7},{10,... | collective-permute-start | bytes 835592 | tf_op jit(solution)/shard_map/ppermute | solution.py:336
  82.1 2.4 %collective-permute-start.25 = (bf16[128,1024]{1,0:T(8,128)(2,1)S(1)}, bf16[128,1024]{1,0:T(8,128)(2,1)S(1)}, u32[]{:S(2)}, u32[]{:S(2)}) collective-permute-start(bf16[128,1024]{1,0:T(8,128)(2,1)S(1)} %collective-permute-done.24.refs_0_), channel_id=1, source_target_pairs={{0,3},{1,62},{2,5},{3,0},{4,7},{5,2},{6,9},{7,4},{8,11},{9,6},{10,... | collective-permute-start | bytes 786440 | tf_op jit(solution)/shard_map/ppermute | solution.py:336
  84.5 2.5 %collective-permute-start.27 = (bf16[128,1024]{1,0:T(8,128)(2,1)S(1)}, bf16[128,1024]{1,0:T(8,128)(2,1)S(1)}, u32[]{:S(2)}, u32[]{:S(2)}) collective-permute-start(bf16[128,1024]{1,0:T(8,128)(2,1)S(1)} %collective-permute-done.26.refs_1_), channel_id=1, source_target_pairs={{0,3},{1,62},{2,5},{3,0},{4,7},{5,2},{6,9},{7,4},{8,11},{9,6},{10,... | collective-permute-start | bytes 786440 | tf_op jit(solution)/shard_map/ppermute | solution.py:336
  86.9 0.2 collective-permute-done.21.piece_ref.refs_2_
  87.1 3.1 %collective-permute-start.22 = (s32[1,384]{1,0:T(1,128)S(1)}, s32[1,384]{1,0:T(1,128)S(1)}, u32[]{:S(2)}, u32[]{:S(2)}) collective-permute-start(s32[1,384]{1,0:T(1,128)S(1)} %decode.1.refs_3_), channel_id=1, source_target_pairs={{0,3},{1,62},{2,5},{3,0},{4,7},{5,2},{6,9},{7,4},{8,11},{9,6},{10,... | collective-permute-start | bytes 4616 | tf_op jit(solution)/shard_map/ppermute | solution.py:336
  90.3 0.1 lay.13
  90.4 0.1 lay.14
  90.5 0.1 lay.15
  90.7 0.1 lay.16
  90.8 0.1 lay.17
  90.9 0.1 lay.18
  91.1 0.1 lay.19
  91.2 0.4 collective-permute-done.25.refs_0_
  91.6 2.8 %collective-permute-done.27.refs_1_ = bf16[128,1024]{1,0:T(8,128)(2,1)S(1)} collective-permute-done((bf16[128,1024]{1,0:T(8,128)(2,1)S(1)}, bf16[128,1024]{1,0:T(8,128)(2,1)S(1)}, u32[]{:S(2)}, u32[]{:S(2)}) %collective-permute-start.27) | collective-permute-done | bytes 262176 | tf_op jit(solution)/shard_map/ppermute | solution.py:336
  94.5 2.0 %meet.2.front_ref = f32[1,256]{1,0:T(1,128)S(1)} custom-call(s32[1,384]{1,0:T(1,128)S(1)} %collective-permute-done.22.keys_ref, bf16[128,1024]{1,0:T(8,128)(2,1)S(1)} %collective-permute-done.25.refs_0_, bf16[128,1024]{1,0:T(8,128)(2,1)S(1)} %collective-permute-done.27.refs_1_, bf16[384,1024]{1,0:T(8,128)(2,1)S(1)} %get-tuple-element.38.own_ref.refs_2_.refs_1_, ...), custom_call_target="tpu_custom_call" | custom-call | flops 1610612736 | bytes 6815744 | tf_op jit(solution)/shard_map/meet/pallas_call | solution.py:223
  96.5 0.1 collective-permute-start.28
  96.6 1.8 %collective-permute-start.30 = (bf16[136,1024]{1,0:T(8,128)(2,1)S(1)}, bf16[136,1024]{1,0:T(8,128)(2,1)S(1)}, u32[]{:S(2)}, u32[]{:S(2)}) collective-permute-start(bf16[136,1024]{1,0:T(8,128)(2,1)S(1)} %collective-permute-done.21.piece_ref.refs_2_), channel_id=1, source_target_pairs={{0,3},{1,62},{2,5},{3,0},{4,7},{5,2},{6,9},{7,4},{8,11},{9,6},{10,... | collective-permute-start | bytes 835592 | tf_op jit(solution)/shard_map/ppermute | solution.py:336
  98.5 0.6 late_visit.1
  99.1 1.6 %collective-permute-start.29 = (f32[1,384]{1,0:T(1,128)S(1)}, f32[1,384]{1,0:T(1,128)S(1)}, u32[]{:S(2)}, u32[]{:S(2)}) collective-permute-start(f32[1,384]{1,0:T(1,128)S(1)} %late_visit.1), channel_id=1, source_target_pairs={{0,3},{1,62},{2,5},{3,0},{4,7},{5,2},{6,9},{7,4},{8,11},{9,6},{10,... | collective-permute-start | bytes 4616 | tf_op jit(solution)/shard_map/ppermute | solution.py:336
  100.7 3.2 %collective-permute-done.30.refs_0_.refs_2_ = bf16[136,1024]{1,0:T(8,128)(2,1)S(1)} collective-permute-done((bf16[136,1024]{1,0:T(8,128)(2,1)S(1)}, bf16[136,1024]{1,0:T(8,128)(2,1)S(1)}, u32[]{:S(2)}, u32[]{:S(2)}) %collective-permute-start.30) | collective-permute-done | bytes 278560 | tf_op jit(solution)/shard_map/ppermute | solution.py:336
  103.9 1.8 %meet.3.back_ref = f32[1,128]{1,0:T(1,128)S(1)} custom-call(s32[1,384]{1,0:T(1,128)S(1)} %collective-permute-done.22.keys_ref, bf16[136,1024]{1,0:T(8,128)(2,1)S(1)} %collective-permute-done.30.refs_0_.refs_2_, bf16[384,1024]{1,0:T(8,128)(2,1)S(1)} %get-tuple-element.38.own_ref.refs_2_.refs_1_, s32[384,128]{1,0:T(8,128)S(1)} %columns.1.own_columns_ref.refs_3_.refs_2_, ...), custom_call_target="tpu_custom_call" | custom-call | flops 805306368 | bytes 6553600 | tf_op jit(solution)/shard_map/meet/pallas_call | solution.py:223
  105.8 0.5 join.1
  106.3 35.4 %all_to_all.5 = f32[32,1,384]{2,1,0:T(1,128)S(1)} all-to-all(f32[32,1,384]{2,1,0:T(1,128)S(1)} %join.1), channel_id=1, replica_groups=mesh['groups'=4,'blk'=32,'sub'=2] {'blk'}, dimensions={0} | all-to-all | bytes 98304 | tf_op jit(solution)/shard_map/all_to_all | solution.py:376
  141.7 0.4 collective-permute-start.31
  142.8 0.2 collective-permute-done.31.theirs_ref
  143.0 0.7 finish.1
  (33 shorter events, 0.4 us)
Async XLA Ops:
  0.6 1.0 copy-start
  1.8 24.3 %collective-permute-start = (bf16[128,1024]{1,0:T(8,128)(2,1)S(1)}, bf16[128,1024]{1,0:T(8,128)(2,1)S(1)}, u32[]{:S(2)}, u32[]{:S(2)}) collective-permute-start(bf16[128,1024]{1,0:T(8,128)(2,1)S(1)} %get-tuple-element.36.refs_0_), channel_id=1, source_target_pairs={{0,1},{1,0},{2,3},{3,2},{4,5},{5,4},{6,7},{7,6},{8,9},{9,8},{10,11... | collective-permute-start | bytes 786440 | tf_op jit(solution)/shard_map/ppermute | solution.py:339
  22.3 8.0 %collective-permute-start.3 = (bf16[128,1024]{1,0:T(8,128)(2,1)S(1)}, bf16[128,1024]{1,0:T(8,128)(2,1)S(1)}, u32[]{:S(2)}, u32[]{:S(2)}) collective-permute-start(bf16[128,1024]{1,0:T(8,128)(2,1)S(1)} %get-tuple-element.36.refs_0_), channel_id=1, source_target_pairs={{0,2},{1,63},{2,4},{3,1},{4,6},{5,3},{6,8},{7,5},{8,10},{9,7},{10,... | collective-permute-start | bytes 786440 | tf_op jit(solution)/shard_map/ppermute | solution.py:336
  26.1 1.3 copy-start.1
  26.2 6.4 %collective-permute-start.9 = (bf16[128,1024]{1,0:T(8,128)(2,1)S(1)}, bf16[128,1024]{1,0:T(8,128)(2,1)S(1)}, u32[]{:S(2)}, u32[]{:S(2)}) collective-permute-start(bf16[128,1024]{1,0:T(8,128)(2,1)S(1)} %lay.11.refs_1_), channel_id=1, source_target_pairs={{0,2},{1,63},{2,4},{3,1},{4,6},{5,3},{6,8},{7,5},{8,10},{9,7},{10,... | collective-permute-start | bytes 786440 | tf_op jit(solution)/shard_map/ppermute | solution.py:336
  27.4 1.6 %collective-permute-start.1 = (bf16[64,1024]{1,0:T(8,128)(2,1)S(1)}, bf16[64,1024]{1,0:T(8,128)(2,1)S(1)}, u32[]{:S(2)}, u32[]{:S(2)}) collective-permute-start(bf16[64,1024]{1,0:T(8,128)(2,1)S(1)} %get-tuple-element.37.refs_1_.refs_0_), channel_id=1, source_target_pairs={{0,1},{1,0},{2,3},{3,2},{4,5},{5,4},{6,7},{7,6},{8,9},{9,8},{10,11... | collective-permute-start | bytes 393224 | tf_op jit(solution)/shard_map/ppermute | solution.py:339
  27.4 1.3 collective-permute-start.2
  29.7 5.8 %collective-permute-start.15 = (bf16[136,1024]{1,0:T(8,128)(2,1)S(1)}, bf16[136,1024]{1,0:T(8,128)(2,1)S(1)}, u32[]{:S(2)}, u32[]{:S(2)}) collective-permute-start(bf16[136,1024]{1,0:T(8,128)(2,1)S(1)} %visit.7), channel_id=1, source_target_pairs={{0,2},{1,63},{2,4},{3,1},{4,6},{5,3},{6,8},{7,5},{8,10},{9,7},{10,... | collective-permute-start | bytes 835592 | tf_op jit(solution)/shard_map/ppermute | solution.py:336
  30.3 8.7 %collective-permute-start.4 = (bf16[128,1024]{1,0:T(8,128)(2,1)S(1)}, bf16[128,1024]{1,0:T(8,128)(2,1)S(1)}, u32[]{:S(2)}, u32[]{:S(2)}) collective-permute-start(bf16[128,1024]{1,0:T(8,128)(2,1)S(1)} %collective-permute-done.3.refs_0_), channel_id=1, source_target_pairs={{0,2},{1,63},{2,4},{3,1},{4,6},{5,3},{6,8},{7,5},{8,10},{9,7},{10,... | collective-permute-start | bytes 786440 | tf_op jit(solution)/shard_map/ppermute | solution.py:336
  32.6 8.6 %collective-permute-start.10 = (bf16[128,1024]{1,0:T(8,128)(2,1)S(1)}, bf16[128,1024]{1,0:T(8,128)(2,1)S(1)}, u32[]{:S(2)}, u32[]{:S(2)}) collective-permute-start(bf16[128,1024]{1,0:T(8,128)(2,1)S(1)} %collective-permute-done.9.refs_1_), channel_id=1, source_target_pairs={{0,2},{1,63},{2,4},{3,1},{4,6},{5,3},{6,8},{7,5},{8,10},{9,7},{10,... | collective-permute-start | bytes 786440 | tf_op jit(solution)/shard_map/ppermute | solution.py:336
  36.1 8.0 %collective-permute-start.16 = (bf16[136,1024]{1,0:T(8,128)(2,1)S(1)}, bf16[136,1024]{1,0:T(8,128)(2,1)S(1)}, u32[]{:S(2)}, u32[]{:S(2)}) collective-permute-start(bf16[136,1024]{1,0:T(8,128)(2,1)S(1)} %get-tuple-element.40), channel_id=1, source_target_pairs={{0,2},{1,63},{2,4},{3,1},{4,6},{5,3},{6,8},{7,5},{8,10},{9,7},{10,... | collective-permute-start | bytes 835592 | tf_op jit(solution)/shard_map/ppermute | solution.py:336
  39.1 8.6 %collective-permute-start.5 = (bf16[128,1024]{1,0:T(8,128)(2,1)S(1)}, bf16[128,1024]{1,0:T(8,128)(2,1)S(1)}, u32[]{:S(2)}, u32[]{:S(2)}) collective-permute-start(bf16[128,1024]{1,0:T(8,128)(2,1)S(1)} %collective-permute-done.4.refs_0_), channel_id=1, source_target_pairs={{0,2},{1,63},{2,4},{3,1},{4,6},{5,3},{6,8},{7,5},{8,10},{9,7},{10,... | collective-permute-start | bytes 786440 | tf_op jit(solution)/shard_map/ppermute | solution.py:336
  41.2 8.6 %collective-permute-start.11 = (bf16[128,1024]{1,0:T(8,128)(2,1)S(1)}, bf16[128,1024]{1,0:T(8,128)(2,1)S(1)}, u32[]{:S(2)}, u32[]{:S(2)}) collective-permute-start(bf16[128,1024]{1,0:T(8,128)(2,1)S(1)} %collective-permute-done.10.refs_1_), channel_id=1, source_target_pairs={{0,2},{1,63},{2,4},{3,1},{4,6},{5,3},{6,8},{7,5},{8,10},{9,7},{10,... | collective-permute-start | bytes 786440 | tf_op jit(solution)/shard_map/ppermute | solution.py:336
  44.7 8.0 %collective-permute-start.17 = (bf16[136,1024]{1,0:T(8,128)(2,1)S(1)}, bf16[136,1024]{1,0:T(8,128)(2,1)S(1)}, u32[]{:S(2)}, u32[]{:S(2)}) collective-permute-start(bf16[136,1024]{1,0:T(8,128)(2,1)S(1)} %get-tuple-element.41), channel_id=1, source_target_pairs={{0,2},{1,63},{2,4},{3,1},{4,6},{5,3},{6,8},{7,5},{8,10},{9,7},{10,... | collective-permute-start | bytes 835592 | tf_op jit(solution)/shard_map/ppermute | solution.py:336
  47.7 8.6 %collective-permute-start.6 = (bf16[128,1024]{1,0:T(8,128)(2,1)S(1)}, bf16[128,1024]{1,0:T(8,128)(2,1)S(1)}, u32[]{:S(2)}, u32[]{:S(2)}) collective-permute-start(bf16[128,1024]{1,0:T(8,128)(2,1)S(1)} %collective-permute-done.5.refs_0_), channel_id=1, source_target_pairs={{0,2},{1,63},{2,4},{3,1},{4,6},{5,3},{6,8},{7,5},{8,10},{9,7},{10,... | collective-permute-start | bytes 786440 | tf_op jit(solution)/shard_map/ppermute | solution.py:336
  49.8 8.6 %collective-permute-start.12 = (bf16[128,1024]{1,0:T(8,128)(2,1)S(1)}, bf16[128,1024]{1,0:T(8,128)(2,1)S(1)}, u32[]{:S(2)}, u32[]{:S(2)}) collective-permute-start(bf16[128,1024]{1,0:T(8,128)(2,1)S(1)} %collective-permute-done.11.refs_1_), channel_id=1, source_target_pairs={{0,2},{1,63},{2,4},{3,1},{4,6},{5,3},{6,8},{7,5},{8,10},{9,7},{10,... | collective-permute-start | bytes 786440 | tf_op jit(solution)/shard_map/ppermute | solution.py:336
  53.3 8.0 %collective-permute-start.18 = (bf16[136,1024]{1,0:T(8,128)(2,1)S(1)}, bf16[136,1024]{1,0:T(8,128)(2,1)S(1)}, u32[]{:S(2)}, u32[]{:S(2)}) collective-permute-start(bf16[136,1024]{1,0:T(8,128)(2,1)S(1)} %get-tuple-element.42), channel_id=1, source_target_pairs={{0,2},{1,63},{2,4},{3,1},{4,6},{5,3},{6,8},{7,5},{8,10},{9,7},{10,... | collective-permute-start | bytes 835592 | tf_op jit(solution)/shard_map/ppermute | solution.py:336
  56.3 8.6 %collective-permute-start.7 = (bf16[128,1024]{1,0:T(8,128)(2,1)S(1)}, bf16[128,1024]{1,0:T(8,128)(2,1)S(1)}, u32[]{:S(2)}, u32[]{:S(2)}) collective-permute-start(bf16[128,1024]{1,0:T(8,128)(2,1)S(1)} %collective-permute-done.6.refs_0_), channel_id=1, source_target_pairs={{0,2},{1,63},{2,4},{3,1},{4,6},{5,3},{6,8},{7,5},{8,10},{9,7},{10,... | collective-permute-start | bytes 786440 | tf_op jit(solution)/shard_map/ppermute | solution.py:336
  58.4 8.6 %collective-permute-start.13 = (bf16[128,1024]{1,0:T(8,128)(2,1)S(1)}, bf16[128,1024]{1,0:T(8,128)(2,1)S(1)}, u32[]{:S(2)}, u32[]{:S(2)}) collective-permute-start(bf16[128,1024]{1,0:T(8,128)(2,1)S(1)} %collective-permute-done.12.refs_1_), channel_id=1, source_target_pairs={{0,2},{1,63},{2,4},{3,1},{4,6},{5,3},{6,8},{7,5},{8,10},{9,7},{10,... | collective-permute-start | bytes 786440 | tf_op jit(solution)/shard_map/ppermute | solution.py:336
  61.9 8.0 %collective-permute-start.19 = (bf16[136,1024]{1,0:T(8,128)(2,1)S(1)}, bf16[136,1024]{1,0:T(8,128)(2,1)S(1)}, u32[]{:S(2)}, u32[]{:S(2)}) collective-permute-start(bf16[136,1024]{1,0:T(8,128)(2,1)S(1)} %get-tuple-element.43), channel_id=1, source_target_pairs={{0,2},{1,63},{2,4},{3,1},{4,6},{5,3},{6,8},{7,5},{8,10},{9,7},{10,... | collective-permute-start | bytes 835592 | tf_op jit(solution)/shard_map/ppermute | solution.py:336
  64.9 8.6 %collective-permute-start.8 = (bf16[128,1024]{1,0:T(8,128)(2,1)S(1)}, bf16[128,1024]{1,0:T(8,128)(2,1)S(1)}, u32[]{:S(2)}, u32[]{:S(2)}) collective-permute-start(bf16[128,1024]{1,0:T(8,128)(2,1)S(1)} %collective-permute-done.7.refs_0_), channel_id=1, source_target_pairs={{0,2},{1,63},{2,4},{3,1},{4,6},{5,3},{6,8},{7,5},{8,10},{9,7},{10,... | collective-permute-start | bytes 786440 | tf_op jit(solution)/shard_map/ppermute | solution.py:336
  67.0 8.6 %collective-permute-start.14 = (bf16[128,1024]{1,0:T(8,128)(2,1)S(1)}, bf16[128,1024]{1,0:T(8,128)(2,1)S(1)}, u32[]{:S(2)}, u32[]{:S(2)}) collective-permute-start(bf16[128,1024]{1,0:T(8,128)(2,1)S(1)} %collective-permute-done.13.refs_1_), channel_id=1, source_target_pairs={{0,2},{1,63},{2,4},{3,1},{4,6},{5,3},{6,8},{7,5},{8,10},{9,7},{10,... | collective-permute-start | bytes 786440 | tf_op jit(solution)/shard_map/ppermute | solution.py:336
  70.5 8.0 %collective-permute-start.20 = (bf16[136,1024]{1,0:T(8,128)(2,1)S(1)}, bf16[136,1024]{1,0:T(8,128)(2,1)S(1)}, u32[]{:S(2)}, u32[]{:S(2)}) collective-permute-start(bf16[136,1024]{1,0:T(8,128)(2,1)S(1)} %get-tuple-element.44), channel_id=1, source_target_pairs={{0,2},{1,63},{2,4},{3,1},{4,6},{5,3},{6,8},{7,5},{8,10},{9,7},{10,... | collective-permute-start | bytes 835592 | tf_op jit(solution)/shard_map/ppermute | solution.py:336
  73.5 8.6 %collective-permute-start.24 = (bf16[128,1024]{1,0:T(8,128)(2,1)S(1)}, bf16[128,1024]{1,0:T(8,128)(2,1)S(1)}, u32[]{:S(2)}, u32[]{:S(2)}) collective-permute-start(bf16[128,1024]{1,0:T(8,128)(2,1)S(1)} %collective-permute-done.8.refs_0_), channel_id=1, source_target_pairs={{0,2},{1,63},{2,4},{3,1},{4,6},{5,3},{6,8},{7,5},{8,10},{9,7},{10,... | collective-permute-start | bytes 786440 | tf_op jit(solution)/shard_map/ppermute | solution.py:336
  75.6 8.9 %collective-permute-start.26 = (bf16[128,1024]{1,0:T(8,128)(2,1)S(1)}, bf16[128,1024]{1,0:T(8,128)(2,1)S(1)}, u32[]{:S(2)}, u32[]{:S(2)}) collective-permute-start(bf16[128,1024]{1,0:T(8,128)(2,1)S(1)} %collective-permute-done.14.refs_1_), channel_id=1, source_target_pairs={{0,2},{1,63},{2,4},{3,1},{4,6},{5,3},{6,8},{7,5},{8,10},{9,7},{10,... | collective-permute-start | bytes 786440 | tf_op jit(solution)/shard_map/ppermute | solution.py:336
  79.1 8.0 %collective-permute-start.21 = (bf16[136,1024]{1,0:T(8,128)(2,1)S(1)}, bf16[136,1024]{1,0:T(8,128)(2,1)S(1)}, u32[]{:S(2)}, u32[]{:S(2)}) collective-permute-start(bf16[136,1024]{1,0:T(8,128)(2,1)S(1)} %get-tuple-element.45), channel_id=1, source_target_pairs={{0,2},{1,63},{2,4},{3,1},{4,6},{5,3},{6,8},{7,5},{8,10},{9,7},{10,... | collective-permute-start | bytes 835592 | tf_op jit(solution)/shard_map/ppermute | solution.py:336
  82.1 9.5 %collective-permute-start.25 = (bf16[128,1024]{1,0:T(8,128)(2,1)S(1)}, bf16[128,1024]{1,0:T(8,128)(2,1)S(1)}, u32[]{:S(2)}, u32[]{:S(2)}) collective-permute-start(bf16[128,1024]{1,0:T(8,128)(2,1)S(1)} %collective-permute-done.24.refs_0_), channel_id=1, source_target_pairs={{0,3},{1,62},{2,5},{3,0},{4,7},{5,2},{6,9},{7,4},{8,11},{9,6},{10,... | collective-permute-start | bytes 786440 | tf_op jit(solution)/shard_map/ppermute | solution.py:336
  84.5 9.9 %collective-permute-start.27 = (bf16[128,1024]{1,0:T(8,128)(2,1)S(1)}, bf16[128,1024]{1,0:T(8,128)(2,1)S(1)}, u32[]{:S(2)}, u32[]{:S(2)}) collective-permute-start(bf16[128,1024]{1,0:T(8,128)(2,1)S(1)} %collective-permute-done.26.refs_1_), channel_id=1, source_target_pairs={{0,3},{1,62},{2,5},{3,0},{4,7},{5,2},{6,9},{7,4},{8,11},{9,6},{10,... | collective-permute-start | bytes 786440 | tf_op jit(solution)/shard_map/ppermute | solution.py:336
  87.1 7.3 %collective-permute-start.22 = (s32[1,384]{1,0:T(1,128)S(1)}, s32[1,384]{1,0:T(1,128)S(1)}, u32[]{:S(2)}, u32[]{:S(2)}) collective-permute-start(s32[1,384]{1,0:T(1,128)S(1)} %decode.1.refs_3_), channel_id=1, source_target_pairs={{0,3},{1,62},{2,5},{3,0},{4,7},{5,2},{6,9},{7,4},{8,11},{9,6},{10,... | collective-permute-start | bytes 4616 | tf_op jit(solution)/shard_map/ppermute | solution.py:336
  96.5 9.3 %collective-permute-start.28 = (bf16[192,1024]{1,0:T(8,128)(2,1)S(1)}, bf16[192,1024]{1,0:T(8,128)(2,1)S(1)}, u32[]{:S(2)}, u32[]{:S(2)}) collective-permute-start(bf16[192,1024]{1,0:T(8,128)(2,1)S(1)} %lay.12), channel_id=1, source_target_pairs={{0,1},{1,0},{2,3},{3,2},{4,5},{5,4},{6,7},{7,6},{8,9},{9,8},{10,11... | collective-permute-start | bytes 1179656 | tf_op jit(solution)/shard_map/ppermute | solution.py:339
  96.6 7.3 %collective-permute-start.30 = (bf16[136,1024]{1,0:T(8,128)(2,1)S(1)}, bf16[136,1024]{1,0:T(8,128)(2,1)S(1)}, u32[]{:S(2)}, u32[]{:S(2)}) collective-permute-start(bf16[136,1024]{1,0:T(8,128)(2,1)S(1)} %collective-permute-done.21.piece_ref.refs_2_), channel_id=1, source_target_pairs={{0,3},{1,62},{2,5},{3,0},{4,7},{5,2},{6,9},{7,4},{8,11},{9,6},{10,... | collective-permute-start | bytes 835592 | tf_op jit(solution)/shard_map/ppermute | solution.py:336
  98.5 7.3 %collective-permute-start.23 = (s32[1,384]{1,0:T(1,128)S(1)}, s32[1,384]{1,0:T(1,128)S(1)}, u32[]{:S(2)}, u32[]{:S(2)}) collective-permute-start(s32[1,384]{1,0:T(1,128)S(1)} %decode.1.refs_3_), channel_id=1, source_target_pairs={{0,2},{1,63},{2,4},{3,1},{4,6},{5,3},{6,8},{7,5},{8,10},{9,7},{10,... | collective-permute-start | bytes 4616 | tf_op jit(solution)/shard_map/ppermute | solution.py:336
  99.1 6.7 %collective-permute-start.29 = (f32[1,384]{1,0:T(1,128)S(1)}, f32[1,384]{1,0:T(1,128)S(1)}, u32[]{:S(2)}, u32[]{:S(2)}) collective-permute-start(f32[1,384]{1,0:T(1,128)S(1)} %late_visit.1), channel_id=1, source_target_pairs={{0,3},{1,62},{2,5},{3,0},{4,7},{5,2},{6,9},{7,4},{8,11},{9,6},{10,... | collective-permute-start | bytes 4616 | tf_op jit(solution)/shard_map/ppermute | solution.py:336
  141.7 1.3 collective-permute-start.31

commit v5 on v4

--- a/solution.py
+++ b/solution.py
@@ -147,46 +147,6 @@
     )(*operands)
 
 
-def late_visit_kernel(pieces, own_ref, own_columns_ref, *refs):
-    piece_refs, out_ref = refs[:pieces], refs[-1]
-    total = out_ref.shape[1]
-    rows = jnp.concatenate([r[...] for r in piece_refs], axis=0)[:total]
-    keys, acc = read_tail(piece_refs[-1], total)
-    low = keys & jnp.int32(-label_stride)
-    out_ref[...] = best_of(acc, keys, low, rows, own_ref[...], own_columns_ref[...])
-
-
-def late_visit(own, pieces):
-    total, width = own[0].shape
-    operands = [*own, *pieces]
-    return pl.pallas_call(
-        functools.partial(late_visit_kernel, len(pieces)),
-        out_shape=jax.ShapeDtypeStruct((1, total), jnp.float32),
-        in_specs=[VMEM] * len(operands),
-        out_specs=VMEM,
-        compiler_params=PARAMS,
-        cost_estimate=pl.CostEstimate(
-            flops=total, bytes_accessed=4 * total * width, transcendentals=0
-        ),
-        name="late_visit",
-    )(*operands)
-
-
-def decode_kernel(piece_ref, keys_ref):
-    keys_ref[...] = read_tail(piece_ref, keys_ref.shape[1])[0]
-
-
-def decode(piece, count):
-    return pl.pallas_call(
-        decode_kernel,
-        out_shape=jax.ShapeDtypeStruct((1, count), jnp.int32),
-        in_specs=[VMEM],
-        out_specs=VMEM,
-        compiler_params=PARAMS,
-        name="decode",
-    )(piece)
-
-
 def columns_kernel(keys_ref, columns_ref):
     columns_ref[...] = key_columns(keys_ref[...])
 
@@ -235,21 +195,21 @@
     )(*operands)
 
 
-def join_kernel(pieces, keys_ref, facing_keys_ref, facing_ref, late_ref, front_ref, back_ref, *refs):
+def join_kernel(pieces, keys_ref, facing_keys_ref, facing_ref, front_ref, back_ref, *refs):
     out_ref = refs[-1]
     keys = keys_ref[...]
     rows = jnp.concatenate([r[...] for r in refs[:pieces]], axis=0)[: keys.shape[1]]
     low = keys & jnp.int32(-label_stride)
     columns = key_columns(facing_keys_ref[...])[: facing_ref.shape[0]]
     best = jnp.concatenate([front_ref[...], back_ref[...]], axis=1)
-    best = jnp.maximum(best, late_ref[...])
+    best = jnp.maximum(best, read_tail(refs[pieces - 1], best.shape[1])[1])
     best = best_of(best, keys, low, rows, facing_ref[...], columns)
     out_ref[...] = jnp.broadcast_to(best[:, None, :], out_ref.shape)
 
 
-def join(keys, facing_keys, facing, late, front, back, pieces, chips):
+def join(keys, facing_keys, facing, front, back, pieces, chips):
     total = keys.shape[1]
-    operands = [keys, facing_keys, facing, late, front, back, *pieces]
+    operands = [keys, facing_keys, facing, front, back, *pieces]
     return pl.pallas_call(
         functools.partial(join_kernel, len(pieces)),
         out_shape=jax.ShapeDtypeStruct((chips, 1, total), jnp.float32),
@@ -351,18 +311,13 @@
     own = (whole, columns_of(keys))
     held = [own]
     (block[-1],) = visit(own, block, keys)
-    for h in range(1, hops):
+    for _ in range(1, hops):
         block = [send(b, 1) for b in block]
-        if h < hops - 1:
-            keys, last = visit(own, block)
-        else:
-            keys, last = decode(block[-1], total), block[-1]
-            late = late_visit(own, block)
+        keys, last = visit(own, block)
         held.append(lay(block, [(0, total)], [keys]))
         block[-1] = last
     last_keys = send(keys, 1, True)
     next_keys = send(keys, 1)
-    late = send(late, 1, True)
     block = [send(b, 1, True) for b in block]
     (first,) = lay(block[:-1], [(0, rows)])
     split = size * (PIECES - 1)
@@ -370,7 +325,7 @@
     first, front = lax.optimization_barrier((first, front))
     facing = across(first)
     back = meet(last_keys, split, size, block[-1:], held)
-    everyone = join(last_keys, next_keys, facing, late, front, back, block, chips)
+    everyone = join(last_keys, next_keys, facing, front, back, block, chips)
 
     limit = limit_of(limit_index, math.sqrt(width))
     gathered = lax.all_to_all(everyone, "blk", 0, 0, tiled=True).reshape(chips, -1)

time: 144 us -> 144 us (level)
  waiting for transfers between devices: 8.58 us -> 10.2 us
  starting transfers between devices: 85.9 us -> 84.3 us
    ppermute x27 -> x26, waiting for transfers between devices: 7.52 us -> 9.13 us  [send(): return lax.ppermute(x, ('blk', 'sub'), moves(by, change))]
    ppermute x27 -> x26, starting transfers between devices: 64.3 us -> 62.7 us  [send(): return lax.ppermute(x, ('blk', 'sub'), moves(by, change))]
    pallas_call x7 -> x8, Pallas kernels: 4.28 us -> 4.9 us  [visit(): pl.pallas_call(functools.partial(visit_kernel, begins, len(pieces)), out_...]
  transfers between devices with their start and end apart: 32 -> 31, of which waited for: 12 -> 11; matrix products, arithmetic and copies ran while one was open for 0% -> 0% of each run, Pallas kernels for 6% -> 5%
where the time goes in v5:
time: 144 us
  starting transfers between devices  84.3 us (59%)
  blocking collectives  35.4 us (25%)
  Pallas kernels  11.3 us (8%)
  waiting for transfers between devices  10.2 us (7%)
  between operations  1.48 us (1%)
    ppermute x26, starting transfers between devices, send(): return lax.ppermute(x, ('blk', 'sub'), moves(by, change))  62.7 us
    all_to_all x1, blocking collectives, program(): lax.all_to_all(everyone, 'blk', 0, 0, tiled=True).reshape(chips, -1)  35.4 us
    ppermute x5, starting transfers between devices, across(): return lax.ppermute(x, 'sub', [(0, 1), (1, 0)])  21.6 us
    ppermute x26, waiting for transfers between devices, send(): return lax.ppermute(x, ('blk', 'sub'), moves(by, change))  9.13 us
    pallas_call x8, Pallas kernels, visit(): pl.pallas_call(functools.partial(visit_kernel, begins, len(pieces)), out_...  4.9 us
    pallas_call x2, Pallas kernels, meet(): pl.pallas_call(functools.partial(meet_kernel, first_row, len(pieces)), ou...  3.83 us
  transfers between devices with their start and end apart: 31, of which 11 were waited for; matrix products, arithmetic and copies ran while one was open for 0% of the time, Pallas kernels for 5%

profile of v5, /device:TPU:37, one launch (start us, length us, event | category | flops | bytes accessed | tf_op | source)
XLA Modules:
  0.0 143.7 jit_solution(12692902877642107336)
XLA Ops:
  0.6 1.0 copy-done
  1.6 0.2 normalize.1
  1.8 20.5 %collective-permute-start = (bf16[128,1024]{1,0:T(8,128)(2,1)S(1)}, bf16[128,1024]{1,0:T(8,128)(2,1)S(1)}, u32[]{:S(2)}, u32[]{:S(2)}) collective-permute-start(bf16[128,1024]{1,0:T(8,128)(2,1)S(1)} %get-tuple-element.38.refs_0_), channel_id=1, source_target_pairs={{0,1},{1,0},{2,3},{3,2},{4,5},{5,4},{6,7},{7,6},{8,9},{9,8},{10,11... | collective-permute-start | bytes 786440 | tf_op jit(solution)/shard_map/ppermute | solution.py:299
  22.3 3.8 %collective-permute-start.3 = (bf16[128,1024]{1,0:T(8,128)(2,1)S(1)}, bf16[128,1024]{1,0:T(8,128)(2,1)S(1)}, u32[]{:S(2)}, u32[]{:S(2)}) collective-permute-start(bf16[128,1024]{1,0:T(8,128)(2,1)S(1)} %get-tuple-element.38.refs_0_), channel_id=1, source_target_pairs={{0,2},{1,63},{2,4},{3,1},{4,6},{5,3},{6,8},{7,5},{8,10},{9,7},{10,... | collective-permute-start | bytes 786440 | tf_op jit(solution)/shard_map/ppermute | solution.py:296
  26.2 1.3 collective-permute-start.10
  27.4 0.5 collective-permute-start.2
  27.9 0.8 collective-permute-done.2
  28.8 0.1 pad_add_fusion.keys_ref.refs_3_
  28.8 0.1 columns.1.own_columns_ref.refs_3_.refs_2_
  29.1 0.6 visit.8
  29.7 0.6 collective-permute-start.17
  30.3 2.2 %collective-permute-start.4 = (bf16[128,1024]{1,0:T(8,128)(2,1)S(1)}, bf16[128,1024]{1,0:T(8,128)(2,1)S(1)}, u32[]{:S(2)}, u32[]{:S(2)}) collective-permute-start(bf16[128,1024]{1,0:T(8,128)(2,1)S(1)} %collective-permute-done.3.refs_0_), channel_id=1, source_target_pairs={{0,2},{1,63},{2,4},{3,1},{4,6},{5,3},{6,8},{7,5},{8,10},{9,7},{10,... | collective-permute-start | bytes 786440 | tf_op jit(solution)/shard_map/ppermute | solution.py:296
  32.6 2.8 %collective-permute-start.11 = (bf16[128,1024]{1,0:T(8,128)(2,1)S(1)}, bf16[128,1024]{1,0:T(8,128)(2,1)S(1)}, u32[]{:S(2)}, u32[]{:S(2)}) collective-permute-start(bf16[128,1024]{1,0:T(8,128)(2,1)S(1)} %collective-permute-done.10.refs_1_), channel_id=1, source_target_pairs={{0,2},{1,63},{2,4},{3,1},{4,6},{5,3},{6,8},{7,5},{8,10},{9,7},{10,... | collective-permute-start | bytes 786440 | tf_op jit(solution)/shard_map/ppermute | solution.py:296
  35.4 0.1 collective-permute-done.17.refs_2_
  35.5 0.6 visit.9
  36.1 3.0 %collective-permute-start.18 = (bf16[136,1024]{1,0:T(8,128)(2,1)S(1)}, bf16[136,1024]{1,0:T(8,128)(2,1)S(1)}, u32[]{:S(2)}, u32[]{:S(2)}) collective-permute-start(bf16[136,1024]{1,0:T(8,128)(2,1)S(1)} %get-tuple-element.42), channel_id=1, source_target_pairs={{0,2},{1,63},{2,4},{3,1},{4,6},{5,3},{6,8},{7,5},{8,10},{9,7},{10,... | collective-permute-start | bytes 835592 | tf_op jit(solution)/shard_map/ppermute | solution.py:296
  39.1 2.1 %collective-permute-start.5 = (bf16[128,1024]{1,0:T(8,128)(2,1)S(1)}, bf16[128,1024]{1,0:T(8,128)(2,1)S(1)}, u32[]{:S(2)}, u32[]{:S(2)}) collective-permute-start(bf16[128,1024]{1,0:T(8,128)(2,1)S(1)} %collective-permute-done.4.refs_0_), channel_id=1, source_target_pairs={{0,2},{1,63},{2,4},{3,1},{4,6},{5,3},{6,8},{7,5},{8,10},{9,7},{10,... | collective-permute-start | bytes 786440 | tf_op jit(solution)/shard_map/ppermute | solution.py:296
  41.2 2.8 %collective-permute-start.12 = (bf16[128,1024]{1,0:T(8,128)(2,1)S(1)}, bf16[128,1024]{1,0:T(8,128)(2,1)S(1)}, u32[]{:S(2)}, u32[]{:S(2)}) collective-permute-start(bf16[128,1024]{1,0:T(8,128)(2,1)S(1)} %collective-permute-done.11.refs_1_), channel_id=1, source_target_pairs={{0,2},{1,63},{2,4},{3,1},{4,6},{5,3},{6,8},{7,5},{8,10},{9,7},{10,... | collective-permute-start | bytes 786440 | tf_op jit(solution)/shard_map/ppermute | solution.py:296
  44.0 0.1 collective-permute-done.18.refs_2_
  44.1 0.6 visit.10
  44.7 3.0 %collective-permute-start.19 = (bf16[136,1024]{1,0:T(8,128)(2,1)S(1)}, bf16[136,1024]{1,0:T(8,128)(2,1)S(1)}, u32[]{:S(2)}, u32[]{:S(2)}) collective-permute-start(bf16[136,1024]{1,0:T(8,128)(2,1)S(1)} %get-tuple-element.43), channel_id=1, source_target_pairs={{0,2},{1,63},{2,4},{3,1},{4,6},{5,3},{6,8},{7,5},{8,10},{9,7},{10,... | collective-permute-start | bytes 835592 | tf_op jit(solution)/shard_map/ppermute | solution.py:296
  47.7 2.1 %collective-permute-start.6 = (bf16[128,1024]{1,0:T(8,128)(2,1)S(1)}, bf16[128,1024]{1,0:T(8,128)(2,1)S(1)}, u32[]{:S(2)}, u32[]{:S(2)}) collective-permute-start(bf16[128,1024]{1,0:T(8,128)(2,1)S(1)} %collective-permute-done.5.refs_0_), channel_id=1, source_target_pairs={{0,2},{1,63},{2,4},{3,1},{4,6},{5,3},{6,8},{7,5},{8,10},{9,7},{10,... | collective-permute-start | bytes 786440 | tf_op jit(solution)/shard_map/ppermute | solution.py:296
  49.8 2.8 %collective-permute-start.13 = (bf16[128,1024]{1,0:T(8,128)(2,1)S(1)}, bf16[128,1024]{1,0:T(8,128)(2,1)S(1)}, u32[]{:S(2)}, u32[]{:S(2)}) collective-permute-start(bf16[128,1024]{1,0:T(8,128)(2,1)S(1)} %collective-permute-done.12.refs_1_), channel_id=1, source_target_pairs={{0,2},{1,63},{2,4},{3,1},{4,6},{5,3},{6,8},{7,5},{8,10},{9,7},{10,... | collective-permute-start | bytes 786440 | tf_op jit(solution)/shard_map/ppermute | solution.py:296
  52.6 0.1 collective-permute-done.19.refs_2_
  52.7 0.6 visit.11
  53.3 3.0 %collective-permute-start.20 = (bf16[136,1024]{1,0:T(8,128)(2,1)S(1)}, bf16[136,1024]{1,0:T(8,128)(2,1)S(1)}, u32[]{:S(2)}, u32[]{:S(2)}) collective-permute-start(bf16[136,1024]{1,0:T(8,128)(2,1)S(1)} %get-tuple-element.44), channel_id=1, source_target_pairs={{0,2},{1,63},{2,4},{3,1},{4,6},{5,3},{6,8},{7,5},{8,10},{9,7},{10,... | collective-permute-start | bytes 835592 | tf_op jit(solution)/shard_map/ppermute | solution.py:296
  56.3 2.1 %collective-permute-start.7 = (bf16[128,1024]{1,0:T(8,128)(2,1)S(1)}, bf16[128,1024]{1,0:T(8,128)(2,1)S(1)}, u32[]{:S(2)}, u32[]{:S(2)}) collective-permute-start(bf16[128,1024]{1,0:T(8,128)(2,1)S(1)} %collective-permute-done.6.refs_0_), channel_id=1, source_target_pairs={{0,2},{1,63},{2,4},{3,1},{4,6},{5,3},{6,8},{7,5},{8,10},{9,7},{10,... | collective-permute-start | bytes 786440 | tf_op jit(solution)/shard_map/ppermute | solution.py:296
  58.4 2.8 %collective-permute-start.14 = (bf16[128,1024]{1,0:T(8,128)(2,1)S(1)}, bf16[128,1024]{1,0:T(8,128)(2,1)S(1)}, u32[]{:S(2)}, u32[]{:S(2)}) collective-permute-start(bf16[128,1024]{1,0:T(8,128)(2,1)S(1)} %collective-permute-done.13.refs_1_), channel_id=1, source_target_pairs={{0,2},{1,63},{2,4},{3,1},{4,6},{5,3},{6,8},{7,5},{8,10},{9,7},{10,... | collective-permute-start | bytes 786440 | tf_op jit(solution)/shard_map/ppermute | solution.py:296
  61.2 0.1 collective-permute-done.20.refs_2_
  61.3 0.6 visit.12
  61.9 3.0 %collective-permute-start.21 = (bf16[136,1024]{1,0:T(8,128)(2,1)S(1)}, bf16[136,1024]{1,0:T(8,128)(2,1)S(1)}, u32[]{:S(2)}, u32[]{:S(2)}) collective-permute-start(bf16[136,1024]{1,0:T(8,128)(2,1)S(1)} %get-tuple-element.45), channel_id=1, source_target_pairs={{0,2},{1,63},{2,4},{3,1},{4,6},{5,3},{6,8},{7,5},{8,10},{9,7},{10,... | collective-permute-start | bytes 835592 | tf_op jit(solution)/shard_map/ppermute | solution.py:296
  64.9 2.1 %collective-permute-start.8 = (bf16[128,1024]{1,0:T(8,128)(2,1)S(1)}, bf16[128,1024]{1,0:T(8,128)(2,1)S(1)}, u32[]{:S(2)}, u32[]{:S(2)}) collective-permute-start(bf16[128,1024]{1,0:T(8,128)(2,1)S(1)} %collective-permute-done.7.refs_0_), channel_id=1, source_target_pairs={{0,2},{1,63},{2,4},{3,1},{4,6},{5,3},{6,8},{7,5},{8,10},{9,7},{10,... | collective-permute-start | bytes 786440 | tf_op jit(solution)/shard_map/ppermute | solution.py:296
  67.0 2.8 %collective-permute-start.15 = (bf16[128,1024]{1,0:T(8,128)(2,1)S(1)}, bf16[128,1024]{1,0:T(8,128)(2,1)S(1)}, u32[]{:S(2)}, u32[]{:S(2)}) collective-permute-start(bf16[128,1024]{1,0:T(8,128)(2,1)S(1)} %collective-permute-done.14.refs_1_), channel_id=1, source_target_pairs={{0,2},{1,63},{2,4},{3,1},{4,6},{5,3},{6,8},{7,5},{8,10},{9,7},{10,... | collective-permute-start | bytes 786440 | tf_op jit(solution)/shard_map/ppermute | solution.py:296
  69.8 0.1 collective-permute-done.21.refs_2_
  69.9 0.6 visit.13
  70.5 3.0 %collective-permute-start.22 = (bf16[136,1024]{1,0:T(8,128)(2,1)S(1)}, bf16[136,1024]{1,0:T(8,128)(2,1)S(1)}, u32[]{:S(2)}, u32[]{:S(2)}) collective-permute-start(bf16[136,1024]{1,0:T(8,128)(2,1)S(1)} %get-tuple-element.46), channel_id=1, source_target_pairs={{0,2},{1,63},{2,4},{3,1},{4,6},{5,3},{6,8},{7,5},{8,10},{9,7},{10,... | collective-permute-start | bytes 835592 | tf_op jit(solution)/shard_map/ppermute | solution.py:296
  73.5 2.1 %collective-permute-start.9 = (bf16[128,1024]{1,0:T(8,128)(2,1)S(1)}, bf16[128,1024]{1,0:T(8,128)(2,1)S(1)}, u32[]{:S(2)}, u32[]{:S(2)}) collective-permute-start(bf16[128,1024]{1,0:T(8,128)(2,1)S(1)} %collective-permute-done.8.refs_0_), channel_id=1, source_target_pairs={{0,2},{1,63},{2,4},{3,1},{4,6},{5,3},{6,8},{7,5},{8,10},{9,7},{10,... | collective-permute-start | bytes 786440 | tf_op jit(solution)/shard_map/ppermute | solution.py:296
  75.6 2.8 %collective-permute-start.16 = (bf16[128,1024]{1,0:T(8,128)(2,1)S(1)}, bf16[128,1024]{1,0:T(8,128)(2,1)S(1)}, u32[]{:S(2)}, u32[]{:S(2)}) collective-permute-start(bf16[128,1024]{1,0:T(8,128)(2,1)S(1)} %collective-permute-done.15.refs_1_), channel_id=1, source_target_pairs={{0,2},{1,63},{2,4},{3,1},{4,6},{5,3},{6,8},{7,5},{8,10},{9,7},{10,... | collective-permute-start | bytes 786440 | tf_op jit(solution)/shard_map/ppermute | solution.py:296
  78.4 0.1 collective-permute-done.22.refs_2_
  78.5 0.6 visit.14
  79.1 3.0 %collective-permute-start.23 = (bf16[136,1024]{1,0:T(8,128)(2,1)S(1)}, bf16[136,1024]{1,0:T(8,128)(2,1)S(1)}, u32[]{:S(2)}, u32[]{:S(2)}) collective-permute-start(bf16[136,1024]{1,0:T(8,128)(2,1)S(1)} %get-tuple-element.47), channel_id=1, source_target_pairs={{0,2},{1,63},{2,4},{3,1},{4,6},{5,3},{6,8},{7,5},{8,10},{9,7},{10,... | collective-permute-start | bytes 835592 | tf_op jit(solution)/shard_map/ppermute | solution.py:296
  82.1 2.4 %collective-permute-start.26 = (bf16[128,1024]{1,0:T(8,128)(2,1)S(1)}, bf16[128,1024]{1,0:T(8,128)(2,1)S(1)}, u32[]{:S(2)}, u32[]{:S(2)}) collective-permute-start(bf16[128,1024]{1,0:T(8,128)(2,1)S(1)} %collective-permute-done.9.refs_0_), channel_id=1, source_target_pairs={{0,3},{1,62},{2,5},{3,0},{4,7},{5,2},{6,9},{7,4},{8,11},{9,6},{10,... | collective-permute-start | bytes 786440 | tf_op jit(solution)/shard_map/ppermute | solution.py:296
  84.5 2.5 %collective-permute-start.27 = (bf16[128,1024]{1,0:T(8,128)(2,1)S(1)}, bf16[128,1024]{1,0:T(8,128)(2,1)S(1)}, u32[]{:S(2)}, u32[]{:S(2)}) collective-permute-start(bf16[128,1024]{1,0:T(8,128)(2,1)S(1)} %collective-permute-done.16.refs_1_), channel_id=1, source_target_pairs={{0,3},{1,62},{2,5},{3,0},{4,7},{5,2},{6,9},{7,4},{8,11},{9,6},{10,... | collective-permute-start | bytes 786440 | tf_op jit(solution)/shard_map/ppermute | solution.py:296
  86.9 0.2 collective-permute-done.23.refs_2_
  87.1 0.6 visit.15
  87.7 3.1 %collective-permute-start.24 = (s32[1,384]{1,0:T(1,128)S(1)}, s32[1,384]{1,0:T(1,128)S(1)}, u32[]{:S(2)}, u32[]{:S(2)}) collective-permute-start(s32[1,384]{1,0:T(1,128)S(1)} %get-tuple-element.48.refs_3_), channel_id=1, source_target_pairs={{0,3},{1,62},{2,5},{3,0},{4,7},{5,2},{6,9},{7,4},{8,11},{9,6},{10,... | collective-permute-start | bytes 4616 | tf_op jit(solution)/shard_map/ppermute | solution.py:296
  90.9 0.1 lay.13
  91.0 0.1 lay.14
  91.1 0.1 lay.15
  91.3 0.1 lay.16
  91.4 0.1 lay.17
  91.6 0.1 lay.18
  91.7 0.1 lay.19
  91.8 2.6 %collective-permute-done.27.refs_1_ = bf16[128,1024]{1,0:T(8,128)(2,1)S(1)} collective-permute-done((bf16[128,1024]{1,0:T(8,128)(2,1)S(1)}, bf16[128,1024]{1,0:T(8,128)(2,1)S(1)}, u32[]{:S(2)}, u32[]{:S(2)}) %collective-permute-start.27) | collective-permute-done | bytes 262176 | tf_op jit(solution)/shard_map/ppermute | solution.py:296
  94.5 2.0 %meet.2.front_ref = f32[1,256]{1,0:T(1,128)S(1)} custom-call(s32[1,384]{1,0:T(1,128)S(1)} %collective-permute-done.24.keys_ref, bf16[128,1024]{1,0:T(8,128)(2,1)S(1)} %collective-permute-done.26.refs_0_, bf16[128,1024]{1,0:T(8,128)(2,1)S(1)} %collective-permute-done.27.refs_1_, bf16[384,1024]{1,0:T(8,128)(2,1)S(1)} %get-tuple-element.40.own_ref.refs_2_.refs_1_, ...), custom_call_target="tpu_custom_call" | custom-call | flops 1610612736 | bytes 6815744 | tf_op jit(solution)/shard_map/meet/pallas_call | solution.py:183
  96.5 0.1 collective-permute-start.28
  96.6 1.8 %collective-permute-start.29 = (bf16[136,1024]{1,0:T(8,128)(2,1)S(1)}, bf16[136,1024]{1,0:T(8,128)(2,1)S(1)}, u32[]{:S(2)}, u32[]{:S(2)}) collective-permute-start(bf16[136,1024]{1,0:T(8,128)(2,1)S(1)} %get-tuple-element.71), channel_id=1, source_target_pairs={{0,3},{1,62},{2,5},{3,0},{4,7},{5,2},{6,9},{7,4},{8,11},{9,6},{10,... | collective-permute-start | bytes 835592 | tf_op jit(solution)/shard_map/ppermute | solution.py:296
  98.5 5.5 %collective-permute-done.29.refs_0_.refs_2_ = bf16[136,1024]{1,0:T(8,128)(2,1)S(1)} collective-permute-done((bf16[136,1024]{1,0:T(8,128)(2,1)S(1)}, bf16[136,1024]{1,0:T(8,128)(2,1)S(1)}, u32[]{:S(2)}, u32[]{:S(2)}) %collective-permute-start.29) | collective-permute-done | bytes 278560 | tf_op jit(solution)/shard_map/ppermute | solution.py:296
  103.9 1.8 %meet.3.back_ref = f32[1,128]{1,0:T(1,128)S(1)} custom-call(s32[1,384]{1,0:T(1,128)S(1)} %collective-permute-done.24.keys_ref, bf16[136,1024]{1,0:T(8,128)(2,1)S(1)} %collective-permute-done.29.refs_0_.refs_2_, bf16[384,1024]{1,0:T(8,128)(2,1)S(1)} %get-tuple-element.40.own_ref.refs_2_.refs_1_, s32[384,128]{1,0:T(8,128)S(1)} %columns.1.own_columns_ref.refs_3_.refs_2_, ...), custom_call_target="tpu_custom_call" | custom-call | flops 805306368 | bytes 6553600 | tf_op jit(solution)/shard_map/meet/pallas_call | solution.py:183
  105.8 0.5 join.1
  106.3 35.4 %all_to_all.5 = f32[32,1,384]{2,1,0:T(1,128)S(1)} all-to-all(f32[32,1,384]{2,1,0:T(1,128)S(1)} %join.1), channel_id=1, replica_groups=mesh['groups'=4,'blk'=32,'sub'=2] {'blk'}, dimensions={0} | all-to-all | bytes 98304 | tf_op jit(solution)/shard_map/all_to_all | solution.py:331
  141.7 0.4 collective-permute-start.30
  142.7 0.2 collective-permute-done.30.theirs_ref
  143.0 0.7 finish.1
  (30 shorter events, 0.2 us)
Async XLA Ops:
  0.6 1.0 copy-start
  1.8 24.3 %collective-permute-start = (bf16[128,1024]{1,0:T(8,128)(2,1)S(1)}, bf16[128,1024]{1,0:T(8,128)(2,1)S(1)}, u32[]{:S(2)}, u32[]{:S(2)}) collective-permute-start(bf16[128,1024]{1,0:T(8,128)(2,1)S(1)} %get-tuple-element.38.refs_0_), channel_id=1, source_target_pairs={{0,1},{1,0},{2,3},{3,2},{4,5},{5,4},{6,7},{7,6},{8,9},{9,8},{10,11... | collective-permute-start | bytes 786440 | tf_op jit(solution)/shard_map/ppermute | solution.py:299
  22.3 8.0 %collective-permute-start.3 = (bf16[128,1024]{1,0:T(8,128)(2,1)S(1)}, bf16[128,1024]{1,0:T(8,128)(2,1)S(1)}, u32[]{:S(2)}, u32[]{:S(2)}) collective-permute-start(bf16[128,1024]{1,0:T(8,128)(2,1)S(1)} %get-tuple-element.38.refs_0_), channel_id=1, source_target_pairs={{0,2},{1,63},{2,4},{3,1},{4,6},{5,3},{6,8},{7,5},{8,10},{9,7},{10,... | collective-permute-start | bytes 786440 | tf_op jit(solution)/shard_map/ppermute | solution.py:296
  26.1 1.3 copy-start.1
  26.2 6.4 %collective-permute-start.10 = (bf16[128,1024]{1,0:T(8,128)(2,1)S(1)}, bf16[128,1024]{1,0:T(8,128)(2,1)S(1)}, u32[]{:S(2)}, u32[]{:S(2)}) collective-permute-start(bf16[128,1024]{1,0:T(8,128)(2,1)S(1)} %lay.11.refs_1_), channel_id=1, source_target_pairs={{0,2},{1,63},{2,4},{3,1},{4,6},{5,3},{6,8},{7,5},{8,10},{9,7},{10,... | collective-permute-start | bytes 786440 | tf_op jit(solution)/shard_map/ppermute | solution.py:296
  27.4 1.6 %collective-permute-start.1 = (bf16[64,1024]{1,0:T(8,128)(2,1)S(1)}, bf16[64,1024]{1,0:T(8,128)(2,1)S(1)}, u32[]{:S(2)}, u32[]{:S(2)}) collective-permute-start(bf16[64,1024]{1,0:T(8,128)(2,1)S(1)} %get-tuple-element.39.refs_1_.refs_0_), channel_id=1, source_target_pairs={{0,1},{1,0},{2,3},{3,2},{4,5},{5,4},{6,7},{7,6},{8,9},{9,8},{10,11... | collective-permute-start | bytes 393224 | tf_op jit(solution)/shard_map/ppermute | solution.py:299
  27.4 1.3 collective-permute-start.2
  29.7 5.8 %collective-permute-start.17 = (bf16[136,1024]{1,0:T(8,128)(2,1)S(1)}, bf16[136,1024]{1,0:T(8,128)(2,1)S(1)}, u32[]{:S(2)}, u32[]{:S(2)}) collective-permute-start(bf16[136,1024]{1,0:T(8,128)(2,1)S(1)} %visit.8), channel_id=1, source_target_pairs={{0,2},{1,63},{2,4},{3,1},{4,6},{5,3},{6,8},{7,5},{8,10},{9,7},{10,... | collective-permute-start | bytes 835592 | tf_op jit(solution)/shard_map/ppermute | solution.py:296
  30.3 8.7 %collective-permute-start.4 = (bf16[128,1024]{1,0:T(8,128)(2,1)S(1)}, bf16[128,1024]{1,0:T(8,128)(2,1)S(1)}, u32[]{:S(2)}, u32[]{:S(2)}) collective-permute-start(bf16[128,1024]{1,0:T(8,128)(2,1)S(1)} %collective-permute-done.3.refs_0_), channel_id=1, source_target_pairs={{0,2},{1,63},{2,4},{3,1},{4,6},{5,3},{6,8},{7,5},{8,10},{9,7},{10,... | collective-permute-start | bytes 786440 | tf_op jit(solution)/shard_map/ppermute | solution.py:296
  32.6 8.6 %collective-permute-start.11 = (bf16[128,1024]{1,0:T(8,128)(2,1)S(1)}, bf16[128,1024]{1,0:T(8,128)(2,1)S(1)}, u32[]{:S(2)}, u32[]{:S(2)}) collective-permute-start(bf16[128,1024]{1,0:T(8,128)(2,1)S(1)} %collective-permute-done.10.refs_1_), channel_id=1, source_target_pairs={{0,2},{1,63},{2,4},{3,1},{4,6},{5,3},{6,8},{7,5},{8,10},{9,7},{10,... | collective-permute-start | bytes 786440 | tf_op jit(solution)/shard_map/ppermute | solution.py:296
  36.1 8.0 %collective-permute-start.18 = (bf16[136,1024]{1,0:T(8,128)(2,1)S(1)}, bf16[136,1024]{1,0:T(8,128)(2,1)S(1)}, u32[]{:S(2)}, u32[]{:S(2)}) collective-permute-start(bf16[136,1024]{1,0:T(8,128)(2,1)S(1)} %get-tuple-element.42), channel_id=1, source_target_pairs={{0,2},{1,63},{2,4},{3,1},{4,6},{5,3},{6,8},{7,5},{8,10},{9,7},{10,... | collective-permute-start | bytes 835592 | tf_op jit(solution)/shard_map/ppermute | solution.py:296
  39.1 8.6 %collective-permute-start.5 = (bf16[128,1024]{1,0:T(8,128)(2,1)S(1)}, bf16[128,1024]{1,0:T(8,128)(2,1)S(1)}, u32[]{:S(2)}, u32[]{:S(2)}) collective-permute-start(bf16[128,1024]{1,0:T(8,128)(2,1)S(1)} %collective-permute-done.4.refs_0_), channel_id=1, source_target_pairs={{0,2},{1,63},{2,4},{3,1},{4,6},{5,3},{6,8},{7,5},{8,10},{9,7},{10,... | collective-permute-start | bytes 786440 | tf_op jit(solution)/shard_map/ppermute | solution.py:296
  41.2 8.6 %collective-permute-start.12 = (bf16[128,1024]{1,0:T(8,128)(2,1)S(1)}, bf16[128,1024]{1,0:T(8,128)(2,1)S(1)}, u32[]{:S(2)}, u32[]{:S(2)}) collective-permute-start(bf16[128,1024]{1,0:T(8,128)(2,1)S(1)} %collective-permute-done.11.refs_1_), channel_id=1, source_target_pairs={{0,2},{1,63},{2,4},{3,1},{4,6},{5,3},{6,8},{7,5},{8,10},{9,7},{10,... | collective-permute-start | bytes 786440 | tf_op jit(solution)/shard_map/ppermute | solution.py:296
  44.7 8.0 %collective-permute-start.19 = (bf16[136,1024]{1,0:T(8,128)(2,1)S(1)}, bf16[136,1024]{1,0:T(8,128)(2,1)S(1)}, u32[]{:S(2)}, u32[]{:S(2)}) collective-permute-start(bf16[136,1024]{1,0:T(8,128)(2,1)S(1)} %get-tuple-element.43), channel_id=1, source_target_pairs={{0,2},{1,63},{2,4},{3,1},{4,6},{5,3},{6,8},{7,5},{8,10},{9,7},{10,... | collective-permute-start | bytes 835592 | tf_op jit(solution)/shard_map/ppermute | solution.py:296
  47.7 8.6 %collective-permute-start.6 = (bf16[128,1024]{1,0:T(8,128)(2,1)S(1)}, bf16[128,1024]{1,0:T(8,128)(2,1)S(1)}, u32[]{:S(2)}, u32[]{:S(2)}) collective-permute-start(bf16[128,1024]{1,0:T(8,128)(2,1)S(1)} %collective-permute-done.5.refs_0_), channel_id=1, source_target_pairs={{0,2},{1,63},{2,4},{3,1},{4,6},{5,3},{6,8},{7,5},{8,10},{9,7},{10,... | collective-permute-start | bytes 786440 | tf_op jit(solution)/shard_map/ppermute | solution.py:296
  49.8 8.6 %collective-permute-start.13 = (bf16[128,1024]{1,0:T(8,128)(2,1)S(1)}, bf16[128,1024]{1,0:T(8,128)(2,1)S(1)}, u32[]{:S(2)}, u32[]{:S(2)}) collective-permute-start(bf16[128,1024]{1,0:T(8,128)(2,1)S(1)} %collective-permute-done.12.refs_1_), channel_id=1, source_target_pairs={{0,2},{1,63},{2,4},{3,1},{4,6},{5,3},{6,8},{7,5},{8,10},{9,7},{10,... | collective-permute-start | bytes 786440 | tf_op jit(solution)/shard_map/ppermute | solution.py:296
  53.3 8.0 %collective-permute-start.20 = (bf16[136,1024]{1,0:T(8,128)(2,1)S(1)}, bf16[136,1024]{1,0:T(8,128)(2,1)S(1)}, u32[]{:S(2)}, u32[]{:S(2)}) collective-permute-start(bf16[136,1024]{1,0:T(8,128)(2,1)S(1)} %get-tuple-element.44), channel_id=1, source_target_pairs={{0,2},{1,63},{2,4},{3,1},{4,6},{5,3},{6,8},{7,5},{8,10},{9,7},{10,... | collective-permute-start | bytes 835592 | tf_op jit(solution)/shard_map/ppermute | solution.py:296
  56.3 8.6 %collective-permute-start.7 = (bf16[128,1024]{1,0:T(8,128)(2,1)S(1)}, bf16[128,1024]{1,0:T(8,128)(2,1)S(1)}, u32[]{:S(2)}, u32[]{:S(2)}) collective-permute-start(bf16[128,1024]{1,0:T(8,128)(2,1)S(1)} %collective-permute-done.6.refs_0_), channel_id=1, source_target_pairs={{0,2},{1,63},{2,4},{3,1},{4,6},{5,3},{6,8},{7,5},{8,10},{9,7},{10,... | collective-permute-start | bytes 786440 | tf_op jit(solution)/shard_map/ppermute | solution.py:296
  58.4 8.6 %collective-permute-start.14 = (bf16[128,1024]{1,0:T(8,128)(2,1)S(1)}, bf16[128,1024]{1,0:T(8,128)(2,1)S(1)}, u32[]{:S(2)}, u32[]{:S(2)}) collective-permute-start(bf16[128,1024]{1,0:T(8,128)(2,1)S(1)} %collective-permute-done.13.refs_1_), channel_id=1, source_target_pairs={{0,2},{1,63},{2,4},{3,1},{4,6},{5,3},{6,8},{7,5},{8,10},{9,7},{10,... | collective-permute-start | bytes 786440 | tf_op jit(solution)/shard_map/ppermute | solution.py:296
  61.9 8.0 %collective-permute-start.21 = (bf16[136,1024]{1,0:T(8,128)(2,1)S(1)}, bf16[136,1024]{1,0:T(8,128)(2,1)S(1)}, u32[]{:S(2)}, u32[]{:S(2)}) collective-permute-start(bf16[136,1024]{1,0:T(8,128)(2,1)S(1)} %get-tuple-element.45), channel_id=1, source_target_pairs={{0,2},{1,63},{2,4},{3,1},{4,6},{5,3},{6,8},{7,5},{8,10},{9,7},{10,... | collective-permute-start | bytes 835592 | tf_op jit(solution)/shard_map/ppermute | solution.py:296
  64.9 8.6 %collective-permute-start.8 = (bf16[128,1024]{1,0:T(8,128)(2,1)S(1)}, bf16[128,1024]{1,0:T(8,128)(2,1)S(1)}, u32[]{:S(2)}, u32[]{:S(2)}) collective-permute-start(bf16[128,1024]{1,0:T(8,128)(2,1)S(1)} %collective-permute-done.7.refs_0_), channel_id=1, source_target_pairs={{0,2},{1,63},{2,4},{3,1},{4,6},{5,3},{6,8},{7,5},{8,10},{9,7},{10,... | collective-permute-start | bytes 786440 | tf_op jit(solution)/shard_map/ppermute | solution.py:296
  67.0 8.6 %collective-permute-start.15 = (bf16[128,1024]{1,0:T(8,128)(2,1)S(1)}, bf16[128,1024]{1,0:T(8,128)(2,1)S(1)}, u32[]{:S(2)}, u32[]{:S(2)}) collective-permute-start(bf16[128,1024]{1,0:T(8,128)(2,1)S(1)} %collective-permute-done.14.refs_1_), channel_id=1, source_target_pairs={{0,2},{1,63},{2,4},{3,1},{4,6},{5,3},{6,8},{7,5},{8,10},{9,7},{10,... | collective-permute-start | bytes 786440 | tf_op jit(solution)/shard_map/ppermute | solution.py:296
  70.5 8.0 %collective-permute-start.22 = (bf16[136,1024]{1,0:T(8,128)(2,1)S(1)}, bf16[136,1024]{1,0:T(8,128)(2,1)S(1)}, u32[]{:S(2)}, u32[]{:S(2)}) collective-permute-start(bf16[136,1024]{1,0:T(8,128)(2,1)S(1)} %get-tuple-element.46), channel_id=1, source_target_pairs={{0,2},{1,63},{2,4},{3,1},{4,6},{5,3},{6,8},{7,5},{8,10},{9,7},{10,... | collective-permute-start | bytes 835592 | tf_op jit(solution)/shard_map/ppermute | solution.py:296
  73.5 8.6 %collective-permute-start.9 = (bf16[128,1024]{1,0:T(8,128)(2,1)S(1)}, bf16[128,1024]{1,0:T(8,128)(2,1)S(1)}, u32[]{:S(2)}, u32[]{:S(2)}) collective-permute-start(bf16[128,1024]{1,0:T(8,128)(2,1)S(1)} %collective-permute-done.8.refs_0_), channel_id=1, source_target_pairs={{0,2},{1,63},{2,4},{3,1},{4,6},{5,3},{6,8},{7,5},{8,10},{9,7},{10,... | collective-permute-start | bytes 786440 | tf_op jit(solution)/shard_map/ppermute | solution.py:296
  75.6 8.9 %collective-permute-start.16 = (bf16[128,1024]{1,0:T(8,128)(2,1)S(1)}, bf16[128,1024]{1,0:T(8,128)(2,1)S(1)}, u32[]{:S(2)}, u32[]{:S(2)}) collective-permute-start(bf16[128,1024]{1,0:T(8,128)(2,1)S(1)} %collective-permute-done.15.refs_1_), channel_id=1, source_target_pairs={{0,2},{1,63},{2,4},{3,1},{4,6},{5,3},{6,8},{7,5},{8,10},{9,7},{10,... | collective-permute-start | bytes 786440 | tf_op jit(solution)/shard_map/ppermute | solution.py:296
  79.1 8.0 %collective-permute-start.23 = (bf16[136,1024]{1,0:T(8,128)(2,1)S(1)}, bf16[136,1024]{1,0:T(8,128)(2,1)S(1)}, u32[]{:S(2)}, u32[]{:S(2)}) collective-permute-start(bf16[136,1024]{1,0:T(8,128)(2,1)S(1)} %get-tuple-element.47), channel_id=1, source_target_pairs={{0,2},{1,63},{2,4},{3,1},{4,6},{5,3},{6,8},{7,5},{8,10},{9,7},{10,... | collective-permute-start | bytes 835592 | tf_op jit(solution)/shard_map/ppermute | solution.py:296
  82.1 9.7 %collective-permute-start.26 = (bf16[128,1024]{1,0:T(8,128)(2,1)S(1)}, bf16[128,1024]{1,0:T(8,128)(2,1)S(1)}, u32[]{:S(2)}, u32[]{:S(2)}) collective-permute-start(bf16[128,1024]{1,0:T(8,128)(2,1)S(1)} %collective-permute-done.9.refs_0_), channel_id=1, source_target_pairs={{0,3},{1,62},{2,5},{3,0},{4,7},{5,2},{6,9},{7,4},{8,11},{9,6},{10,... | collective-permute-start | bytes 786440 | tf_op jit(solution)/shard_map/ppermute | solution.py:296
  84.5 9.9 %collective-permute-start.27 = (bf16[128,1024]{1,0:T(8,128)(2,1)S(1)}, bf16[128,1024]{1,0:T(8,128)(2,1)S(1)}, u32[]{:S(2)}, u32[]{:S(2)}) collective-permute-start(bf16[128,1024]{1,0:T(8,128)(2,1)S(1)} %collective-permute-done.16.refs_1_), channel_id=1, source_target_pairs={{0,3},{1,62},{2,5},{3,0},{4,7},{5,2},{6,9},{7,4},{8,11},{9,6},{10,... | collective-permute-start | bytes 786440 | tf_op jit(solution)/shard_map/ppermute | solution.py:296
  87.7 6.7 %collective-permute-start.24 = (s32[1,384]{1,0:T(1,128)S(1)}, s32[1,384]{1,0:T(1,128)S(1)}, u32[]{:S(2)}, u32[]{:S(2)}) collective-permute-start(s32[1,384]{1,0:T(1,128)S(1)} %get-tuple-element.48.refs_3_), channel_id=1, source_target_pairs={{0,3},{1,62},{2,5},{3,0},{4,7},{5,2},{6,9},{7,4},{8,11},{9,6},{10,... | collective-permute-start | bytes 4616 | tf_op jit(solution)/shard_map/ppermute | solution.py:296
  96.5 9.3 %collective-permute-start.28 = (bf16[192,1024]{1,0:T(8,128)(2,1)S(1)}, bf16[192,1024]{1,0:T(8,128)(2,1)S(1)}, u32[]{:S(2)}, u32[]{:S(2)}) collective-permute-start(bf16[192,1024]{1,0:T(8,128)(2,1)S(1)} %lay.12), channel_id=1, source_target_pairs={{0,1},{1,0},{2,3},{3,2},{4,5},{5,4},{6,7},{7,6},{8,9},{9,8},{10,11... | collective-permute-start | bytes 1179656 | tf_op jit(solution)/shard_map/ppermute | solution.py:299
  96.6 7.3 %collective-permute-start.29 = (bf16[136,1024]{1,0:T(8,128)(2,1)S(1)}, bf16[136,1024]{1,0:T(8,128)(2,1)S(1)}, u32[]{:S(2)}, u32[]{:S(2)}) collective-permute-start(bf16[136,1024]{1,0:T(8,128)(2,1)S(1)} %get-tuple-element.71), channel_id=1, source_target_pairs={{0,3},{1,62},{2,5},{3,0},{4,7},{5,2},{6,9},{7,4},{8,11},{9,6},{10,... | collective-permute-start | bytes 835592 | tf_op jit(solution)/shard_map/ppermute | solution.py:296
  98.5 7.3 %collective-permute-start.25 = (s32[1,384]{1,0:T(1,128)S(1)}, s32[1,384]{1,0:T(1,128)S(1)}, u32[]{:S(2)}, u32[]{:S(2)}) collective-permute-start(s32[1,384]{1,0:T(1,128)S(1)} %get-tuple-element.48.refs_3_), channel_id=1, source_target_pairs={{0,2},{1,63},{2,4},{3,1},{4,6},{5,3},{6,8},{7,5},{8,10},{9,7},{10,... | collective-permute-start | bytes 4616 | tf_op jit(solution)/shard_map/ppermute | solution.py:296
  141.7 1.3 collective-permute-start.30

commit v6 on v5

--- a/solution.py
+++ b/solution.py
@@ -19,24 +19,40 @@
 PARAMS = pltpu.CompilerParams(vmem_limit_bytes=16 * 1024 * 1024)
 
 
-def normalize_kernel(emb_ref, *out_refs):
-    at = 0
+def normalize_kernel(emb_ref, *refs):
+    held, arrived = refs[-2:]
+    out_refs = refs[:-2]
+    part = held.shape[1]
+    copies = [
+        pltpu.make_async_copy(emb_ref.at[pl.ds(n * part, part)], held.at[n], arrived.at[n])
+        for n in range(held.shape[0])
+    ]
+    for copy in copies:
+        copy.start()
+    n = 0
     for out in out_refs:
-        values = emb_ref[at : at + out.shape[0], :].astype(jnp.float32)
-        mean_square = jnp.mean(values * values, axis=1, keepdims=True)
-        scaled = values * lax.rsqrt(mean_square + 1e-06) * (1.0 / math.sqrt(values.shape[1]))
-        out[...] = scaled.astype(jnp.bfloat16)
-        at += out.shape[0]
+        for at in range(0, out.shape[0], part):
+            copies[n].wait()
+            values = held[n].astype(jnp.float32)
+            mean_square = jnp.mean(values * values, axis=1, keepdims=True)
+            scaled = values * lax.rsqrt(mean_square + 1e-06) * (1.0 / math.sqrt(values.shape[1]))
+            out[at : at + part, :] = scaled.astype(jnp.bfloat16)
+            n += 1
 
 
 def normalize(embeddings, sizes):
     rows, width = embeddings.shape
+    part = math.gcd(*sizes) // 2
     return pl.pallas_call(
         normalize_kernel,
         out_shape=[jax.ShapeDtypeStruct((size, width), jnp.bfloat16) for size in sizes],
-        in_specs=[VMEM],
+        in_specs=[pl.BlockSpec(memory_space=pltpu.HBM)],
         out_specs=[VMEM] * len(sizes),
-        compiler_params=PARAMS,
+        scratch_shapes=[
+            pltpu.VMEM((rows // part, part, width), embeddings.dtype),
+            pltpu.SemaphoreType.DMA((rows // part,)),
+        ],
+        compiler_params=pltpu.CompilerParams(vmem_limit_bytes=63 * 1024 * 1024 + 300 * 1024),
         cost_estimate=pl.CostEstimate(
             flops=rows * width * 4, bytes_accessed=rows * width * 4, transcendentals=rows
         ),

time: 144 us -> 146 us (1.014)
  waiting for transfers between devices: 10.2 us -> 23.7 us
  starting transfers between devices: 84.3 us -> 70.9 us
  Pallas kernels: 11.3 us -> 13.3 us
    ppermute x26, waiting for transfers between devices: 9.13 us -> 22.7 us  [send(): return lax.ppermute(x, ('blk', 'sub'), moves(by, change))]
    ppermute x26, starting transfers between devices: 62.7 us -> 49.3 us  [send(): return lax.ppermute(x, ('blk', 'sub'), moves(by, change))]
    pallas_call x1, Pallas kernels: 0.18 us -> 2.2 us  [normalize(): pl.pallas_call(normalize_kernel, out_shape=[jax.ShapeDtypeStruct((size, w...]
  transfers between devices with their start and end apart: 31 -> 31, of which waited for: 11 -> 23; matrix products, arithmetic and copies ran while one was open for 0% -> 0% of each run, Pallas kernels for 5% -> 5%
where the time goes in v6:
time: 146 us; the launch traced here: 145 us
  starting transfers between devices  70.9 us (49%)
  blocking collectives  34.9 us (24%)
  waiting for transfers between devices  23.7 us (16%)
  Pallas kernels  13.3 us (9%)
  between operations  1.49 us (1%)
    ppermute x26, starting transfers between devices, send(): return lax.ppermute(x, ('blk', 'sub'), moves(by, change))  49.3 us
    all_to_all x1, blocking collectives, program(): lax.all_to_all(everyone, 'blk', 0, 0, tiled=True).reshape(chips, -1)  34.9 us
    ppermute x26, waiting for transfers between devices, send(): return lax.ppermute(x, ('blk', 'sub'), moves(by, change))  22.7 us
    ppermute x5, starting transfers between devices, across(): return lax.ppermute(x, 'sub', [(0, 1), (1, 0)])  21.6 us
    pallas_call x8, Pallas kernels, visit(): pl.pallas_call(functools.partial(visit_kernel, begins, len(pieces)), out_...  4.89 us
    pallas_call x2, Pallas kernels, meet(): pl.pallas_call(functools.partial(meet_kernel, first_row, len(pieces)), ou...  3.83 us
  transfers between devices with their start and end apart: 31, of which 23 were waited for; matrix products, arithmetic and copies ran while one was open for 0% of the time, Pallas kernels for 5%

profile of v6, /device:TPU:37, one launch (start us, length us, event | category | flops | bytes accessed | tf_op | source)
XLA Modules:
  0.0 145.4 jit_solution(1203936240890795576)
XLA Ops:
  0.6 2.2 %normalize.1 = (bf16[128,1024]{1,0:T(8,128)(2,1)}, bf16[64,1024]{1,0:T(8,128)(2,1)}) custom-call(bf16[192,1024]{1,0:T(8,128)(2,1)} %emb_ref.1), custom_call_target="tpu_custom_call" | custom-call | flops 786432 | bytes 786432 | tf_op jit(solution)/shard_map/normalize/pallas_call | solution.py:46
  2.8 20.5 %collective-permute-start = (bf16[128,1024]{1,0:T(8,128)(2,1)}, bf16[128,1024]{1,0:T(8,128)(2,1)S(1)}, u32[]{:S(2)}, u32[]{:S(2)}) collective-permute-start(bf16[128,1024]{1,0:T(8,128)(2,1)} %get-tuple-element.38.refs_0_), channel_id=1, source_target_pairs={{0,1},{1,0},{2,3},{3,2},{4,5},{5,4},{6,7},{7,6},{8,9},{9,8},{10,11... | collective-permute-start | bytes 786440 | tf_op jit(solution)/shard_map/ppermute | solution.py:315
  23.4 3.8 %collective-permute-start.3 = (bf16[128,1024]{1,0:T(8,128)(2,1)}, bf16[128,1024]{1,0:T(8,128)(2,1)S(1)}, u32[]{:S(2)}, u32[]{:S(2)}) collective-permute-start(bf16[128,1024]{1,0:T(8,128)(2,1)} %get-tuple-element.38.refs_0_), channel_id=1, source_target_pairs={{0,2},{1,63},{2,4},{3,1},{4,6},{5,3},{6,8},{7,5},{8,10},{9,7},{10,... | collective-permute-start | bytes 786440 | tf_op jit(solution)/shard_map/ppermute | solution.py:312
  27.1 0.9 copy-done.1
  28.1 1.5 %collective-permute-start.10 = (bf16[128,1024]{1,0:T(8,128)(2,1)S(1)}, bf16[128,1024]{1,0:T(8,128)(2,1)S(1)}, u32[]{:S(2)}, u32[]{:S(2)}) collective-permute-start(bf16[128,1024]{1,0:T(8,128)(2,1)S(1)} %lay.11.refs_1_), channel_id=1, source_target_pairs={{0,2},{1,63},{2,4},{3,1},{4,6},{5,3},{6,8},{7,5},{8,10},{9,7},{10,... | collective-permute-start | bytes 786440 | tf_op jit(solution)/shard_map/ppermute | solution.py:312
  29.6 0.5 collective-permute-start.2
  30.1 0.8 collective-permute-done.2
  31.2 0.6 visit.8
  31.8 1.1 collective-permute-start.17
  32.9 1.0 collective-permute-start.4
  33.9 2.7 %collective-permute-start.11 = (bf16[128,1024]{1,0:T(8,128)(2,1)S(1)}, bf16[128,1024]{1,0:T(8,128)(2,1)S(1)}, u32[]{:S(2)}, u32[]{:S(2)}) collective-permute-start(bf16[128,1024]{1,0:T(8,128)(2,1)S(1)} %collective-permute-done.10.refs_1_), channel_id=1, source_target_pairs={{0,2},{1,63},{2,4},{3,1},{4,6},{5,3},{6,8},{7,5},{8,10},{9,7},{10,... | collective-permute-start | bytes 786440 | tf_op jit(solution)/shard_map/ppermute | solution.py:312
  36.6 1.1 collective-permute-done.17.refs_2_
  37.7 0.6 visit.9
  38.3 2.0 %collective-permute-start.18 = (bf16[136,1024]{1,0:T(8,128)(2,1)S(1)}, bf16[136,1024]{1,0:T(8,128)(2,1)S(1)}, u32[]{:S(2)}, u32[]{:S(2)}) collective-permute-start(bf16[136,1024]{1,0:T(8,128)(2,1)S(1)} %get-tuple-element.42), channel_id=1, source_target_pairs={{0,2},{1,63},{2,4},{3,1},{4,6},{5,3},{6,8},{7,5},{8,10},{9,7},{10,... | collective-permute-start | bytes 835592 | tf_op jit(solution)/shard_map/ppermute | solution.py:312
  40.5 1.9 %collective-permute-start.5 = (bf16[128,1024]{1,0:T(8,128)(2,1)S(1)}, bf16[128,1024]{1,0:T(8,128)(2,1)S(1)}, u32[]{:S(2)}, u32[]{:S(2)}) collective-permute-start(bf16[128,1024]{1,0:T(8,128)(2,1)S(1)} %collective-permute-done.4.refs_0_), channel_id=1, source_target_pairs={{0,2},{1,63},{2,4},{3,1},{4,6},{5,3},{6,8},{7,5},{8,10},{9,7},{10,... | collective-permute-start | bytes 786440 | tf_op jit(solution)/shard_map/ppermute | solution.py:312
  42.4 0.9 collective-permute-done.11.refs_1_
  43.3 1.9 %collective-permute-start.12 = (bf16[128,1024]{1,0:T(8,128)(2,1)S(1)}, bf16[128,1024]{1,0:T(8,128)(2,1)S(1)}, u32[]{:S(2)}, u32[]{:S(2)}) collective-permute-start(bf16[128,1024]{1,0:T(8,128)(2,1)S(1)} %collective-permute-done.11.refs_1_), channel_id=1, source_target_pairs={{0,2},{1,63},{2,4},{3,1},{4,6},{5,3},{6,8},{7,5},{8,10},{9,7},{10,... | collective-permute-start | bytes 786440 | tf_op jit(solution)/shard_map/ppermute | solution.py:312
  45.2 1.1 collective-permute-done.18.refs_2_
  46.3 0.6 visit.10
  46.9 2.0 %collective-permute-start.19 = (bf16[136,1024]{1,0:T(8,128)(2,1)S(1)}, bf16[136,1024]{1,0:T(8,128)(2,1)S(1)}, u32[]{:S(2)}, u32[]{:S(2)}) collective-permute-start(bf16[136,1024]{1,0:T(8,128)(2,1)S(1)} %get-tuple-element.43), channel_id=1, source_target_pairs={{0,2},{1,63},{2,4},{3,1},{4,6},{5,3},{6,8},{7,5},{8,10},{9,7},{10,... | collective-permute-start | bytes 835592 | tf_op jit(solution)/shard_map/ppermute | solution.py:312
  48.9 0.2 collective-permute-done.5.refs_0_
  49.1 1.9 %collective-permute-start.6 = (bf16[128,1024]{1,0:T(8,128)(2,1)S(1)}, bf16[128,1024]{1,0:T(8,128)(2,1)S(1)}, u32[]{:S(2)}, u32[]{:S(2)}) collective-permute-start(bf16[128,1024]{1,0:T(8,128)(2,1)S(1)} %collective-permute-done.5.refs_0_), channel_id=1, source_target_pairs={{0,2},{1,63},{2,4},{3,1},{4,6},{5,3},{6,8},{7,5},{8,10},{9,7},{10,... | collective-permute-start | bytes 786440 | tf_op jit(solution)/shard_map/ppermute | solution.py:312
  51.0 0.9 collective-permute-done.12.refs_1_
  51.9 1.9 %collective-permute-start.13 = (bf16[128,1024]{1,0:T(8,128)(2,1)S(1)}, bf16[128,1024]{1,0:T(8,128)(2,1)S(1)}, u32[]{:S(2)}, u32[]{:S(2)}) collective-permute-start(bf16[128,1024]{1,0:T(8,128)(2,1)S(1)} %collective-permute-done.12.refs_1_), channel_id=1, source_target_pairs={{0,2},{1,63},{2,4},{3,1},{4,6},{5,3},{6,8},{7,5},{8,10},{9,7},{10,... | collective-permute-start | bytes 786440 | tf_op jit(solution)/shard_map/ppermute | solution.py:312
  53.8 1.1 collective-permute-done.19.refs_2_
  54.9 0.6 visit.11
  55.5 2.0 %collective-permute-start.20 = (bf16[136,1024]{1,0:T(8,128)(2,1)S(1)}, bf16[136,1024]{1,0:T(8,128)(2,1)S(1)}, u32[]{:S(2)}, u32[]{:S(2)}) collective-permute-start(bf16[136,1024]{1,0:T(8,128)(2,1)S(1)} %get-tuple-element.44), channel_id=1, source_target_pairs={{0,2},{1,63},{2,4},{3,1},{4,6},{5,3},{6,8},{7,5},{8,10},{9,7},{10,... | collective-permute-start | bytes 835592 | tf_op jit(solution)/shard_map/ppermute | solution.py:312
  57.5 0.2 collective-permute-done.6.refs_0_
  57.7 1.9 %collective-permute-start.7 = (bf16[128,1024]{1,0:T(8,128)(2,1)S(1)}, bf16[128,1024]{1,0:T(8,128)(2,1)S(1)}, u32[]{:S(2)}, u32[]{:S(2)}) collective-permute-start(bf16[128,1024]{1,0:T(8,128)(2,1)S(1)} %collective-permute-done.6.refs_0_), channel_id=1, source_target_pairs={{0,2},{1,63},{2,4},{3,1},{4,6},{5,3},{6,8},{7,5},{8,10},{9,7},{10,... | collective-permute-start | bytes 786440 | tf_op jit(solution)/shard_map/ppermute | solution.py:312
  59.6 0.9 collective-permute-done.13.refs_1_
  60.5 1.9 %collective-permute-start.14 = (bf16[128,1024]{1,0:T(8,128)(2,1)S(1)}, bf16[128,1024]{1,0:T(8,128)(2,1)S(1)}, u32[]{:S(2)}, u32[]{:S(2)}) collective-permute-start(bf16[128,1024]{1,0:T(8,128)(2,1)S(1)} %collective-permute-done.13.refs_1_), channel_id=1, source_target_pairs={{0,2},{1,63},{2,4},{3,1},{4,6},{5,3},{6,8},{7,5},{8,10},{9,7},{10,... | collective-permute-start | bytes 786440 | tf_op jit(solution)/shard_map/ppermute | solution.py:312
  62.4 1.1 collective-permute-done.20.refs_2_
  63.5 0.6 visit.12
  64.1 2.0 %collective-permute-start.21 = (bf16[136,1024]{1,0:T(8,128)(2,1)S(1)}, bf16[136,1024]{1,0:T(8,128)(2,1)S(1)}, u32[]{:S(2)}, u32[]{:S(2)}) collective-permute-start(bf16[136,1024]{1,0:T(8,128)(2,1)S(1)} %get-tuple-element.45), channel_id=1, source_target_pairs={{0,2},{1,63},{2,4},{3,1},{4,6},{5,3},{6,8},{7,5},{8,10},{9,7},{10,... | collective-permute-start | bytes 835592 | tf_op jit(solution)/shard_map/ppermute | solution.py:312
  66.1 0.2 collective-permute-done.7.refs_0_
  66.3 1.9 %collective-permute-start.8 = (bf16[128,1024]{1,0:T(8,128)(2,1)S(1)}, bf16[128,1024]{1,0:T(8,128)(2,1)S(1)}, u32[]{:S(2)}, u32[]{:S(2)}) collective-permute-start(bf16[128,1024]{1,0:T(8,128)(2,1)S(1)} %collective-permute-done.7.refs_0_), channel_id=1, source_target_pairs={{0,2},{1,63},{2,4},{3,1},{4,6},{5,3},{6,8},{7,5},{8,10},{9,7},{10,... | collective-permute-start | bytes 786440 | tf_op jit(solution)/shard_map/ppermute | solution.py:312
  68.2 0.9 collective-permute-done.14.refs_1_
  69.1 1.9 %collective-permute-start.15 = (bf16[128,1024]{1,0:T(8,128)(2,1)S(1)}, bf16[128,1024]{1,0:T(8,128)(2,1)S(1)}, u32[]{:S(2)}, u32[]{:S(2)}) collective-permute-start(bf16[128,1024]{1,0:T(8,128)(2,1)S(1)} %collective-permute-done.14.refs_1_), channel_id=1, source_target_pairs={{0,2},{1,63},{2,4},{3,1},{4,6},{5,3},{6,8},{7,5},{8,10},{9,7},{10,... | collective-permute-start | bytes 786440 | tf_op jit(solution)/shard_map/ppermute | solution.py:312
  71.0 1.1 collective-permute-done.21.refs_2_
  72.1 0.6 visit.13
  72.7 2.0 %collective-permute-start.22 = (bf16[136,1024]{1,0:T(8,128)(2,1)S(1)}, bf16[136,1024]{1,0:T(8,128)(2,1)S(1)}, u32[]{:S(2)}, u32[]{:S(2)}) collective-permute-start(bf16[136,1024]{1,0:T(8,128)(2,1)S(1)} %get-tuple-element.46), channel_id=1, source_target_pairs={{0,2},{1,63},{2,4},{3,1},{4,6},{5,3},{6,8},{7,5},{8,10},{9,7},{10,... | collective-permute-start | bytes 835592 | tf_op jit(solution)/shard_map/ppermute | solution.py:312
  74.7 0.2 collective-permute-done.8.refs_0_
  74.9 1.9 %collective-permute-start.9 = (bf16[128,1024]{1,0:T(8,128)(2,1)S(1)}, bf16[128,1024]{1,0:T(8,128)(2,1)S(1)}, u32[]{:S(2)}, u32[]{:S(2)}) collective-permute-start(bf16[128,1024]{1,0:T(8,128)(2,1)S(1)} %collective-permute-done.8.refs_0_), channel_id=1, source_target_pairs={{0,2},{1,63},{2,4},{3,1},{4,6},{5,3},{6,8},{7,5},{8,10},{9,7},{10,... | collective-permute-start | bytes 786440 | tf_op jit(solution)/shard_map/ppermute | solution.py:312
  76.8 0.9 collective-permute-done.15.refs_1_
  77.7 1.9 %collective-permute-start.16 = (bf16[128,1024]{1,0:T(8,128)(2,1)S(1)}, bf16[128,1024]{1,0:T(8,128)(2,1)S(1)}, u32[]{:S(2)}, u32[]{:S(2)}) collective-permute-start(bf16[128,1024]{1,0:T(8,128)(2,1)S(1)} %collective-permute-done.15.refs_1_), channel_id=1, source_target_pairs={{0,2},{1,63},{2,4},{3,1},{4,6},{5,3},{6,8},{7,5},{8,10},{9,7},{10,... | collective-permute-start | bytes 786440 | tf_op jit(solution)/shard_map/ppermute | solution.py:312
  79.6 1.1 collective-permute-done.22.refs_2_
  80.7 0.6 visit.14
  81.3 2.0 %collective-permute-start.23 = (bf16[136,1024]{1,0:T(8,128)(2,1)S(1)}, bf16[136,1024]{1,0:T(8,128)(2,1)S(1)}, u32[]{:S(2)}, u32[]{:S(2)}) collective-permute-start(bf16[136,1024]{1,0:T(8,128)(2,1)S(1)} %get-tuple-element.47), channel_id=1, source_target_pairs={{0,2},{1,63},{2,4},{3,1},{4,6},{5,3},{6,8},{7,5},{8,10},{9,7},{10,... | collective-permute-start | bytes 835592 | tf_op jit(solution)/shard_map/ppermute | solution.py:312
  83.5 3.2 %collective-permute-start.26 = (bf16[128,1024]{1,0:T(8,128)(2,1)S(1)}, bf16[128,1024]{1,0:T(8,128)(2,1)S(1)}, u32[]{:S(2)}, u32[]{:S(2)}) collective-permute-start(bf16[128,1024]{1,0:T(8,128)(2,1)S(1)} %collective-permute-done.9.refs_0_), channel_id=1, source_target_pairs={{0,3},{1,62},{2,5},{3,0},{4,7},{5,2},{6,9},{7,4},{8,11},{9,6},{10,... | collective-permute-start | bytes 786440 | tf_op jit(solution)/shard_map/ppermute | solution.py:312
  86.6 1.5 %collective-permute-start.27 = (bf16[128,1024]{1,0:T(8,128)(2,1)S(1)}, bf16[128,1024]{1,0:T(8,128)(2,1)S(1)}, u32[]{:S(2)}, u32[]{:S(2)}) collective-permute-start(bf16[128,1024]{1,0:T(8,128)(2,1)S(1)} %collective-permute-done.16.refs_1_), channel_id=1, source_target_pairs={{0,3},{1,62},{2,5},{3,0},{4,7},{5,2},{6,9},{7,4},{8,11},{9,6},{10,... | collective-permute-start | bytes 786440 | tf_op jit(solution)/shard_map/ppermute | solution.py:312
  88.2 1.1 collective-permute-done.23.refs_2_
  89.3 0.6 visit.15
  89.9 2.2 %collective-permute-start.24 = (s32[1,384]{1,0:T(1,128)S(1)}, s32[1,384]{1,0:T(1,128)S(1)}, u32[]{:S(2)}, u32[]{:S(2)}) collective-permute-start(s32[1,384]{1,0:T(1,128)S(1)} %get-tuple-element.48.refs_3_), channel_id=1, source_target_pairs={{0,3},{1,62},{2,5},{3,0},{4,7},{5,2},{6,9},{7,4},{8,11},{9,6},{10,... | collective-permute-start | bytes 4616 | tf_op jit(solution)/shard_map/ppermute | solution.py:312
  93.1 0.7 collective-permute-done.26.refs_0_
  93.8 2.8 %collective-permute-done.27.refs_1_ = bf16[128,1024]{1,0:T(8,128)(2,1)S(1)} collective-permute-done((bf16[128,1024]{1,0:T(8,128)(2,1)S(1)}, bf16[128,1024]{1,0:T(8,128)(2,1)S(1)}, u32[]{:S(2)}, u32[]{:S(2)}) %collective-permute-start.27) | collective-permute-done | bytes 262176 | tf_op jit(solution)/shard_map/ppermute | solution.py:312
  96.6 2.0 %meet.2.front_ref = f32[1,256]{1,0:T(1,128)S(1)} custom-call(s32[1,384]{1,0:T(1,128)S(1)} %collective-permute-done.24.keys_ref, bf16[128,1024]{1,0:T(8,128)(2,1)S(1)} %collective-permute-done.26.refs_0_, bf16[128,1024]{1,0:T(8,128)(2,1)S(1)} %collective-permute-done.27.refs_1_, bf16[384,1024]{1,0:T(8,128)(2,1)S(1)} %get-tuple-element.40.own_ref.refs_2_.refs_1_, ...), custom_call_target="tpu_custom_call" | custom-call | flops 1610612736 | bytes 6815744 | tf_op jit(solution)/shard_map/meet/pallas_call | solution.py:199
  98.8 0.9 collective-permute-start.29
  99.8 6.4 %collective-permute-done.29.refs_0_.refs_2_ = bf16[136,1024]{1,0:T(8,128)(2,1)S(1)} collective-permute-done((bf16[136,1024]{1,0:T(8,128)(2,1)S(1)}, bf16[136,1024]{1,0:T(8,128)(2,1)S(1)}, u32[]{:S(2)}, u32[]{:S(2)}) %collective-permute-start.29) | collective-permute-done | bytes 278560 | tf_op jit(solution)/shard_map/ppermute | solution.py:312
  106.1 1.8 %meet.3.back_ref = f32[1,128]{1,0:T(1,128)S(1)} custom-call(s32[1,384]{1,0:T(1,128)S(1)} %collective-permute-done.24.keys_ref, bf16[136,1024]{1,0:T(8,128)(2,1)S(1)} %collective-permute-done.29.refs_0_.refs_2_, bf16[384,1024]{1,0:T(8,128)(2,1)S(1)} %get-tuple-element.40.own_ref.refs_2_.refs_1_, s32[384,128]{1,0:T(8,128)S(1)} %columns.1.own_columns_ref.refs_3_.refs_2_, ...), custom_call_target="tpu_custom_call" | custom-call | flops 805306368 | bytes 6553600 | tf_op jit(solution)/shard_map/meet/pallas_call | solution.py:199
  108.0 0.5 join.1
  108.4 34.9 %all_to_all.5 = f32[32,1,384]{2,1,0:T(1,128)S(1)} all-to-all(f32[32,1,384]{2,1,0:T(1,128)S(1)} %join.1), channel_id=1, replica_groups=mesh['groups'=4,'blk'=32,'sub'=2] {'blk'}, dimensions={0} | all-to-all | bytes 98304 | tf_op jit(solution)/shard_map/all_to_all | solution.py:347
  143.4 0.4 collective-permute-start.30
  144.5 0.2 collective-permute-done.30.theirs_ref
  144.7 0.7 finish.1
  (34 shorter events, 1.8 us)
Async XLA Ops:
  2.8 24.3 %collective-permute-start = (bf16[128,1024]{1,0:T(8,128)(2,1)}, bf16[128,1024]{1,0:T(8,128)(2,1)S(1)}, u32[]{:S(2)}, u32[]{:S(2)}) collective-permute-start(bf16[128,1024]{1,0:T(8,128)(2,1)} %get-tuple-element.38.refs_0_), channel_id=1, source_target_pairs={{0,1},{1,0},{2,3},{3,2},{4,5},{5,4},{6,7},{7,6},{8,9},{9,8},{10,11... | collective-permute-start | bytes 786440 | tf_op jit(solution)/shard_map/ppermute | solution.py:315
  23.4 9.5 %collective-permute-start.3 = (bf16[128,1024]{1,0:T(8,128)(2,1)}, bf16[128,1024]{1,0:T(8,128)(2,1)S(1)}, u32[]{:S(2)}, u32[]{:S(2)}) collective-permute-start(bf16[128,1024]{1,0:T(8,128)(2,1)} %get-tuple-element.38.refs_0_), channel_id=1, source_target_pairs={{0,2},{1,63},{2,4},{3,1},{4,6},{5,3},{6,8},{7,5},{8,10},{9,7},{10,... | collective-permute-start | bytes 786440 | tf_op jit(solution)/shard_map/ppermute | solution.py:312
  27.1 0.9 copy-start.1
  28.1 1.5 %copy-start.2 = (bf16[64,1024]{1,0:T(8,128)(2,1)S(1)}, bf16[64,1024]{1,0:T(8,128)(2,1)}, u32[]{:S(2)}) copy-start(bf16[64,1024]{1,0:T(8,128)(2,1)} %get-tuple-element.39.refs_1_.refs_0_) | copy-start | bytes 393220
  28.1 3.1 %copy-start = (bf16[128,1024]{1,0:T(8,128)(2,1)S(1)}, bf16[128,1024]{1,0:T(8,128)(2,1)}, u32[]{:S(2)}) copy-start(bf16[128,1024]{1,0:T(8,128)(2,1)} %get-tuple-element.38.refs_0_) | copy-start | bytes 786436
  28.1 1.5 %copy-start.3 = (s32[192]{0:T(256)S(1)}, s32[192]{0:T(256)}, u32[]{:S(2)}) copy-start(s32[192]{0:T(256)} %param.4) | copy-start | bytes 2308
  28.1 5.8 %collective-permute-start.10 = (bf16[128,1024]{1,0:T(8,128)(2,1)S(1)}, bf16[128,1024]{1,0:T(8,128)(2,1)S(1)}, u32[]{:S(2)}, u32[]{:S(2)}) collective-permute-start(bf16[128,1024]{1,0:T(8,128)(2,1)S(1)} %lay.11.refs_1_), channel_id=1, source_target_pairs={{0,2},{1,63},{2,4},{3,1},{4,6},{5,3},{6,8},{7,5},{8,10},{9,7},{10,... | collective-permute-start | bytes 786440 | tf_op jit(solution)/shard_map/ppermute | solution.py:312
  29.6 1.6 %collective-permute-start.1 = (bf16[64,1024]{1,0:T(8,128)(2,1)S(1)}, bf16[64,1024]{1,0:T(8,128)(2,1)S(1)}, u32[]{:S(2)}, u32[]{:S(2)}) collective-permute-start(bf16[64,1024]{1,0:T(8,128)(2,1)S(1)} %copy-done.2), channel_id=1, source_target_pairs={{0,1},{1,0},{2,3},{3,2},{4,5},{5,4},{6,7},{7,6},{8,9},{9,8},{10,11... | collective-permute-start | bytes 393224 | tf_op jit(solution)/shard_map/ppermute | solution.py:315
  29.6 1.3 collective-permute-start.2
  31.8 5.8 %collective-permute-start.17 = (bf16[136,1024]{1,0:T(8,128)(2,1)S(1)}, bf16[136,1024]{1,0:T(8,128)(2,1)S(1)}, u32[]{:S(2)}, u32[]{:S(2)}) collective-permute-start(bf16[136,1024]{1,0:T(8,128)(2,1)S(1)} %visit.8), channel_id=1, source_target_pairs={{0,2},{1,63},{2,4},{3,1},{4,6},{5,3},{6,8},{7,5},{8,10},{9,7},{10,... | collective-permute-start | bytes 835592 | tf_op jit(solution)/shard_map/ppermute | solution.py:312
  32.9 7.6 %collective-permute-start.4 = (bf16[128,1024]{1,0:T(8,128)(2,1)S(1)}, bf16[128,1024]{1,0:T(8,128)(2,1)S(1)}, u32[]{:S(2)}, u32[]{:S(2)}) collective-permute-start(bf16[128,1024]{1,0:T(8,128)(2,1)S(1)} %collective-permute-done.3.refs_0_), channel_id=1, source_target_pairs={{0,2},{1,63},{2,4},{3,1},{4,6},{5,3},{6,8},{7,5},{8,10},{9,7},{10,... | collective-permute-start | bytes 786440 | tf_op jit(solution)/shard_map/ppermute | solution.py:312
  33.9 9.4 %collective-permute-start.11 = (bf16[128,1024]{1,0:T(8,128)(2,1)S(1)}, bf16[128,1024]{1,0:T(8,128)(2,1)S(1)}, u32[]{:S(2)}, u32[]{:S(2)}) collective-permute-start(bf16[128,1024]{1,0:T(8,128)(2,1)S(1)} %collective-permute-done.10.refs_1_), channel_id=1, source_target_pairs={{0,2},{1,63},{2,4},{3,1},{4,6},{5,3},{6,8},{7,5},{8,10},{9,7},{10,... | collective-permute-start | bytes 786440 | tf_op jit(solution)/shard_map/ppermute | solution.py:312
  38.3 8.0 %collective-permute-start.18 = (bf16[136,1024]{1,0:T(8,128)(2,1)S(1)}, bf16[136,1024]{1,0:T(8,128)(2,1)S(1)}, u32[]{:S(2)}, u32[]{:S(2)}) collective-permute-start(bf16[136,1024]{1,0:T(8,128)(2,1)S(1)} %get-tuple-element.42), channel_id=1, source_target_pairs={{0,2},{1,63},{2,4},{3,1},{4,6},{5,3},{6,8},{7,5},{8,10},{9,7},{10,... | collective-permute-start | bytes 835592 | tf_op jit(solution)/shard_map/ppermute | solution.py:312
  40.5 8.6 %collective-permute-start.5 = (bf16[128,1024]{1,0:T(8,128)(2,1)S(1)}, bf16[128,1024]{1,0:T(8,128)(2,1)S(1)}, u32[]{:S(2)}, u32[]{:S(2)}) collective-permute-start(bf16[128,1024]{1,0:T(8,128)(2,1)S(1)} %collective-permute-done.4.refs_0_), channel_id=1, source_target_pairs={{0,2},{1,63},{2,4},{3,1},{4,6},{5,3},{6,8},{7,5},{8,10},{9,7},{10,... | collective-permute-start | bytes 786440 | tf_op jit(solution)/shard_map/ppermute | solution.py:312
  43.3 8.6 %collective-permute-start.12 = (bf16[128,1024]{1,0:T(8,128)(2,1)S(1)}, bf16[128,1024]{1,0:T(8,128)(2,1)S(1)}, u32[]{:S(2)}, u32[]{:S(2)}) collective-permute-start(bf16[128,1024]{1,0:T(8,128)(2,1)S(1)} %collective-permute-done.11.refs_1_), channel_id=1, source_target_pairs={{0,2},{1,63},{2,4},{3,1},{4,6},{5,3},{6,8},{7,5},{8,10},{9,7},{10,... | collective-permute-start | bytes 786440 | tf_op jit(solution)/shard_map/ppermute | solution.py:312
  46.9 8.0 %collective-permute-start.19 = (bf16[136,1024]{1,0:T(8,128)(2,1)S(1)}, bf16[136,1024]{1,0:T(8,128)(2,1)S(1)}, u32[]{:S(2)}, u32[]{:S(2)}) collective-permute-start(bf16[136,1024]{1,0:T(8,128)(2,1)S(1)} %get-tuple-element.43), channel_id=1, source_target_pairs={{0,2},{1,63},{2,4},{3,1},{4,6},{5,3},{6,8},{7,5},{8,10},{9,7},{10,... | collective-permute-start | bytes 835592 | tf_op jit(solution)/shard_map/ppermute | solution.py:312
  49.1 8.6 %collective-permute-start.6 = (bf16[128,1024]{1,0:T(8,128)(2,1)S(1)}, bf16[128,1024]{1,0:T(8,128)(2,1)S(1)}, u32[]{:S(2)}, u32[]{:S(2)}) collective-permute-start(bf16[128,1024]{1,0:T(8,128)(2,1)S(1)} %collective-permute-done.5.refs_0_), channel_id=1, source_target_pairs={{0,2},{1,63},{2,4},{3,1},{4,6},{5,3},{6,8},{7,5},{8,10},{9,7},{10,... | collective-permute-start | bytes 786440 | tf_op jit(solution)/shard_map/ppermute | solution.py:312
  51.9 8.6 %collective-permute-start.13 = (bf16[128,1024]{1,0:T(8,128)(2,1)S(1)}, bf16[128,1024]{1,0:T(8,128)(2,1)S(1)}, u32[]{:S(2)}, u32[]{:S(2)}) collective-permute-start(bf16[128,1024]{1,0:T(8,128)(2,1)S(1)} %collective-permute-done.12.refs_1_), channel_id=1, source_target_pairs={{0,2},{1,63},{2,4},{3,1},{4,6},{5,3},{6,8},{7,5},{8,10},{9,7},{10,... | collective-permute-start | bytes 786440 | tf_op jit(solution)/shard_map/ppermute | solution.py:312
  55.5 8.0 %collective-permute-start.20 = (bf16[136,1024]{1,0:T(8,128)(2,1)S(1)}, bf16[136,1024]{1,0:T(8,128)(2,1)S(1)}, u32[]{:S(2)}, u32[]{:S(2)}) collective-permute-start(bf16[136,1024]{1,0:T(8,128)(2,1)S(1)} %get-tuple-element.44), channel_id=1, source_target_pairs={{0,2},{1,63},{2,4},{3,1},{4,6},{5,3},{6,8},{7,5},{8,10},{9,7},{10,... | collective-permute-start | bytes 835592 | tf_op jit(solution)/shard_map/ppermute | solution.py:312
  57.7 8.6 %collective-permute-start.7 = (bf16[128,1024]{1,0:T(8,128)(2,1)S(1)}, bf16[128,1024]{1,0:T(8,128)(2,1)S(1)}, u32[]{:S(2)}, u32[]{:S(2)}) collective-permute-start(bf16[128,1024]{1,0:T(8,128)(2,1)S(1)} %collective-permute-done.6.refs_0_), channel_id=1, source_target_pairs={{0,2},{1,63},{2,4},{3,1},{4,6},{5,3},{6,8},{7,5},{8,10},{9,7},{10,... | collective-permute-start | bytes 786440 | tf_op jit(solution)/shard_map/ppermute | solution.py:312
  60.5 8.6 %collective-permute-start.14 = (bf16[128,1024]{1,0:T(8,128)(2,1)S(1)}, bf16[128,1024]{1,0:T(8,128)(2,1)S(1)}, u32[]{:S(2)}, u32[]{:S(2)}) collective-permute-start(bf16[128,1024]{1,0:T(8,128)(2,1)S(1)} %collective-permute-done.13.refs_1_), channel_id=1, source_target_pairs={{0,2},{1,63},{2,4},{3,1},{4,6},{5,3},{6,8},{7,5},{8,10},{9,7},{10,... | collective-permute-start | bytes 786440 | tf_op jit(solution)/shard_map/ppermute | solution.py:312
  64.1 8.0 %collective-permute-start.21 = (bf16[136,1024]{1,0:T(8,128)(2,1)S(1)}, bf16[136,1024]{1,0:T(8,128)(2,1)S(1)}, u32[]{:S(2)}, u32[]{:S(2)}) collective-permute-start(bf16[136,1024]{1,0:T(8,128)(2,1)S(1)} %get-tuple-element.45), channel_id=1, source_target_pairs={{0,2},{1,63},{2,4},{3,1},{4,6},{5,3},{6,8},{7,5},{8,10},{9,7},{10,... | collective-permute-start | bytes 835592 | tf_op jit(solution)/shard_map/ppermute | solution.py:312
  66.3 8.6 %collective-permute-start.8 = (bf16[128,1024]{1,0:T(8,128)(2,1)S(1)}, bf16[128,1024]{1,0:T(8,128)(2,1)S(1)}, u32[]{:S(2)}, u32[]{:S(2)}) collective-permute-start(bf16[128,1024]{1,0:T(8,128)(2,1)S(1)} %collective-permute-done.7.refs_0_), channel_id=1, source_target_pairs={{0,2},{1,63},{2,4},{3,1},{4,6},{5,3},{6,8},{7,5},{8,10},{9,7},{10,... | collective-permute-start | bytes 786440 | tf_op jit(solution)/shard_map/ppermute | solution.py:312
  69.1 8.6 %collective-permute-start.15 = (bf16[128,1024]{1,0:T(8,128)(2,1)S(1)}, bf16[128,1024]{1,0:T(8,128)(2,1)S(1)}, u32[]{:S(2)}, u32[]{:S(2)}) collective-permute-start(bf16[128,1024]{1,0:T(8,128)(2,1)S(1)} %collective-permute-done.14.refs_1_), channel_id=1, source_target_pairs={{0,2},{1,63},{2,4},{3,1},{4,6},{5,3},{6,8},{7,5},{8,10},{9,7},{10,... | collective-permute-start | bytes 786440 | tf_op jit(solution)/shard_map/ppermute | solution.py:312
  72.7 8.0 %collective-permute-start.22 = (bf16[136,1024]{1,0:T(8,128)(2,1)S(1)}, bf16[136,1024]{1,0:T(8,128)(2,1)S(1)}, u32[]{:S(2)}, u32[]{:S(2)}) collective-permute-start(bf16[136,1024]{1,0:T(8,128)(2,1)S(1)} %get-tuple-element.46), channel_id=1, source_target_pairs={{0,2},{1,63},{2,4},{3,1},{4,6},{5,3},{6,8},{7,5},{8,10},{9,7},{10,... | collective-permute-start | bytes 835592 | tf_op jit(solution)/shard_map/ppermute | solution.py:312
  74.9 8.6 %collective-permute-start.9 = (bf16[128,1024]{1,0:T(8,128)(2,1)S(1)}, bf16[128,1024]{1,0:T(8,128)(2,1)S(1)}, u32[]{:S(2)}, u32[]{:S(2)}) collective-permute-start(bf16[128,1024]{1,0:T(8,128)(2,1)S(1)} %collective-permute-done.8.refs_0_), channel_id=1, source_target_pairs={{0,2},{1,63},{2,4},{3,1},{4,6},{5,3},{6,8},{7,5},{8,10},{9,7},{10,... | collective-permute-start | bytes 786440 | tf_op jit(solution)/shard_map/ppermute | solution.py:312
  77.7 9.0 %collective-permute-start.16 = (bf16[128,1024]{1,0:T(8,128)(2,1)S(1)}, bf16[128,1024]{1,0:T(8,128)(2,1)S(1)}, u32[]{:S(2)}, u32[]{:S(2)}) collective-permute-start(bf16[128,1024]{1,0:T(8,128)(2,1)S(1)} %collective-permute-done.15.refs_1_), channel_id=1, source_target_pairs={{0,2},{1,63},{2,4},{3,1},{4,6},{5,3},{6,8},{7,5},{8,10},{9,7},{10,... | collective-permute-start | bytes 786440 | tf_op jit(solution)/shard_map/ppermute | solution.py:312
  81.3 8.0 %collective-permute-start.23 = (bf16[136,1024]{1,0:T(8,128)(2,1)S(1)}, bf16[136,1024]{1,0:T(8,128)(2,1)S(1)}, u32[]{:S(2)}, u32[]{:S(2)}) collective-permute-start(bf16[136,1024]{1,0:T(8,128)(2,1)S(1)} %get-tuple-element.47), channel_id=1, source_target_pairs={{0,2},{1,63},{2,4},{3,1},{4,6},{5,3},{6,8},{7,5},{8,10},{9,7},{10,... | collective-permute-start | bytes 835592 | tf_op jit(solution)/shard_map/ppermute | solution.py:312
  83.5 10.3 %collective-permute-start.26 = (bf16[128,1024]{1,0:T(8,128)(2,1)S(1)}, bf16[128,1024]{1,0:T(8,128)(2,1)S(1)}, u32[]{:S(2)}, u32[]{:S(2)}) collective-permute-start(bf16[128,1024]{1,0:T(8,128)(2,1)S(1)} %collective-permute-done.9.refs_0_), channel_id=1, source_target_pairs={{0,3},{1,62},{2,5},{3,0},{4,7},{5,2},{6,9},{7,4},{8,11},{9,6},{10,... | collective-permute-start | bytes 786440 | tf_op jit(solution)/shard_map/ppermute | solution.py:312
  86.6 9.9 %collective-permute-start.27 = (bf16[128,1024]{1,0:T(8,128)(2,1)S(1)}, bf16[128,1024]{1,0:T(8,128)(2,1)S(1)}, u32[]{:S(2)}, u32[]{:S(2)}) collective-permute-start(bf16[128,1024]{1,0:T(8,128)(2,1)S(1)} %collective-permute-done.16.refs_1_), channel_id=1, source_target_pairs={{0,3},{1,62},{2,5},{3,0},{4,7},{5,2},{6,9},{7,4},{8,11},{9,6},{10,... | collective-permute-start | bytes 786440 | tf_op jit(solution)/shard_map/ppermute | solution.py:312
  89.9 6.7 %collective-permute-start.24 = (s32[1,384]{1,0:T(1,128)S(1)}, s32[1,384]{1,0:T(1,128)S(1)}, u32[]{:S(2)}, u32[]{:S(2)}) collective-permute-start(s32[1,384]{1,0:T(1,128)S(1)} %get-tuple-element.48.refs_3_), channel_id=1, source_target_pairs={{0,3},{1,62},{2,5},{3,0},{4,7},{5,2},{6,9},{7,4},{8,11},{9,6},{10,... | collective-permute-start | bytes 4616 | tf_op jit(solution)/shard_map/ppermute | solution.py:312
  98.7 9.3 %collective-permute-start.28 = (bf16[192,1024]{1,0:T(8,128)(2,1)S(1)}, bf16[192,1024]{1,0:T(8,128)(2,1)S(1)}, u32[]{:S(2)}, u32[]{:S(2)}) collective-permute-start(bf16[192,1024]{1,0:T(8,128)(2,1)S(1)} %lay.12), channel_id=1, source_target_pairs={{0,1},{1,0},{2,3},{3,2},{4,5},{5,4},{6,7},{7,6},{8,9},{9,8},{10,11... | collective-permute-start | bytes 1179656 | tf_op jit(solution)/shard_map/ppermute | solution.py:315
  98.8 7.3 %collective-permute-start.29 = (bf16[136,1024]{1,0:T(8,128)(2,1)S(1)}, bf16[136,1024]{1,0:T(8,128)(2,1)S(1)}, u32[]{:S(2)}, u32[]{:S(2)}) collective-permute-start(bf16[136,1024]{1,0:T(8,128)(2,1)S(1)} %get-tuple-element.71), channel_id=1, source_target_pairs={{0,3},{1,62},{2,5},{3,0},{4,7},{5,2},{6,9},{7,4},{8,11},{9,6},{10,... | collective-permute-start | bytes 835592 | tf_op jit(solution)/shard_map/ppermute | solution.py:312
  99.7 8.2 %collective-permute-start.25 = (s32[1,384]{1,0:T(1,128)S(1)}, s32[1,384]{1,0:T(1,128)S(1)}, u32[]{:S(2)}, u32[]{:S(2)}) collective-permute-start(s32[1,384]{1,0:T(1,128)S(1)} %get-tuple-element.48.refs_3_), channel_id=1, source_target_pairs={{0,2},{1,63},{2,4},{3,1},{4,6},{5,3},{6,8},{7,5},{8,10},{9,7},{10,... | collective-permute-start | bytes 4616 | tf_op jit(solution)/shard_map/ppermute | solution.py:312
  143.4 1.3 collective-permute-start.30
